TPU v7x, 256 devices: a whole 4x4x8 slice. The times are simulated.
256 devices in a mesh: clip: 32 (over z_lo, y, core), row: 2 (over z_hi), src: 4 (over x).
Axes of the slice: x: 4, y: 4, z: 8 (z_hi: 2, z_lo: 4; z = z_hi * 4 + z_lo), core: 2. Of those that a mesh axis runs over, the one named last changes fastest.
Arguments:
- mask_clip: bfloat16 [131072, 4096], P(('clip', 'row'), 'src'), parts along dimension 0, may hold values from -6 to 6
- source_shifts: int32 [16, 2], P('src'), may hold values from -64 to 64
- source_weights: int32 [16], P('src'), may hold values from 1 to 8
Outputs:
- intensity: float32 [32768, 1024], P(('clip', 'row', 'src')), parts along dimension 0
There are 32 independent parts, one for each index of `clip`. A program takes and returns all parts, laid end to end along the dimension named above; an argument that names none is the same for every part. Nothing has to cross between parts.
All inputs are finite; a program needn't handle non-finite values.
Results may differ from a plain program's by a relative error of at most 0.0052.
Values may be sent and summed in bfloat16 or wider, within the bound.
No kernel may reach another device: no remote copies, remote signals or barrier semaphores. Data moves between devices by JAX's collectives and lax.ppermute only.
A program may use at most 64 MiB of HBM per device.

v0:
```python
import math

import jax
import jax.numpy as jnp
from jax import lax
from jax.sharding import PartitionSpec as P

NM = 4096
P_SIZE = 256
NI = 1024


def twiddles(positions, length, scaling):
    frequency = jnp.arange(P_SIZE, dtype=jnp.int32) - P_SIZE // 2
    product = jnp.mod(positions[:, None] * frequency[None, :], length)
    angles = product.astype(jnp.float32) * jnp.float32(2.0 * math.pi / length)
    return (jnp.cos(angles) * jnp.float32(scaling), jnp.sin(angles) * jnp.float32(scaling))


def tile_spectrum(mask_tile, row_first, col_first):
    row_index = row_first + jnp.arange(mask_tile.shape[0], dtype=jnp.int32)
    col_index = col_first + jnp.arange(mask_tile.shape[1], dtype=jnp.int32)
    col_cos, col_sin = twiddles(col_index, NM, 1.0 / math.sqrt(NM))
    col_table = jnp.concatenate([col_cos, -col_sin], 1).astype(jnp.bfloat16)
    half_way = jnp.dot(mask_tile, col_table, preferred_element_type=jnp.float32).astype(
        jnp.bfloat16
    )
    row_cos, row_sin = twiddles(row_index, NM, 1.0 / math.sqrt(NM))
    row_table = jnp.concatenate([row_cos, row_sin], 1).T.astype(jnp.bfloat16)
    blocks = jnp.dot(row_table, half_way, preferred_element_type=jnp.float32)
    real_part = blocks[:P_SIZE, :P_SIZE] + blocks[P_SIZE:, P_SIZE:]
    imag_part = blocks[:P_SIZE, P_SIZE:] - blocks[P_SIZE:, :P_SIZE]
    return jnp.stack([real_part, imag_part])


def build_left(image_rows):
    row_cos, row_sin = twiddles(image_rows, NI, 1.0 / math.sqrt(P_SIZE))
    return jnp.concatenate([row_cos, row_sin], 0).astype(jnp.bfloat16)


def build_right():
    col_cos, col_sin = twiddles(jnp.arange(NI, dtype=jnp.int32), NI, 1.0 / math.sqrt(P_SIZE))
    upper = jnp.concatenate([col_cos.T, col_sin.T], 1)
    lower = jnp.concatenate([-col_sin.T, col_cos.T], 1)
    return jnp.concatenate([upper, lower], 0).astype(jnp.bfloat16)


def source_image(spectrum, shift_pair, weight, left_table, right_table):
    frequency = jnp.arange(P_SIZE, dtype=jnp.int32) - P_SIZE // 2
    along_rows = frequency + shift_pair[0]
    along_cols = frequency + shift_pair[1]
    radius = P_SIZE // 4
    inside = (
        along_rows[:, None] * along_rows[:, None] + along_cols[None, :] * along_cols[None, :]
        <= radius * radius
    )
    pupil_mask = inside.astype(jnp.bfloat16)
    passed = jnp.concatenate([spectrum[0] * pupil_mask, spectrum[1] * pupil_mask], 1)
    blocks = jnp.dot(left_table, passed, preferred_element_type=jnp.float32)
    row_count = left_table.shape[0] // 2
    k_real = blocks[:row_count, :P_SIZE] - blocks[row_count:, P_SIZE:]
    k_imag = blocks[:row_count, P_SIZE:] + blocks[row_count:, :P_SIZE]
    partial_value = jnp.concatenate([k_real, k_imag], 1).astype(jnp.bfloat16)
    field_pair = jnp.dot(partial_value, right_table, preferred_element_type=jnp.float32)
    field_real = field_pair[:, :NI]
    field_imag = field_pair[:, NI:]
    return weight.astype(jnp.float32) * (field_real * field_real + field_imag * field_imag)


def image_rows_sum(spectrum, image_rows, all_shifts, all_weights, right_table):
    left_table = build_left(image_rows)

    def add_source(running, source_item):
        shift_pair, weight = source_item
        return (running + source_image(spectrum, shift_pair, weight, left_table, right_table), None)

    summed, _ = lax.scan(
        add_source, jnp.zeros((image_rows.shape[0], NI), jnp.float32), (all_shifts, all_weights)
    )
    return summed


def body(mask_clip, source_shifts, source_weights):
    row_id = lax.axis_index("row")
    src_id = lax.axis_index("src")
    strip_rows = mask_clip.shape[0]
    strip_cols = mask_clip.shape[1]
    partial_value = tile_spectrum(mask_clip, row_id * strip_rows, src_id * strip_cols)
    spectrum = lax.psum(partial_value, ("row", "src")).astype(jnp.bfloat16)
    right_table = build_right()
    image_strip = NI // lax.axis_size("row")
    rows_dev = image_strip // lax.axis_size("src")
    sources = source_shifts.shape[0] * lax.axis_size("src")
    image_rows = row_id * image_strip + jnp.arange(rows_dev * lax.axis_size("src"), dtype=jnp.int32)
    summed = lax.psum_scatter(
        image_rows_sum(spectrum, image_rows, source_shifts, source_weights, right_table),
        "src",
        scatter_dimension=0,
        tiled=True,
    )
    return summed / jnp.float32(sources)


def solution(mesh):
    placed = (P(("clip", "row"), "src"), P("src", None), P("src"))
    return jax.shard_map(
        body, mesh=mesh, in_specs=placed, out_specs=P(("clip", "row", "src"), None), check_vma=False
    )
```

profile of v0, /device:TPU:8, one launch (start us, length us, event | category | flops | bytes accessed | tf_op | source)
XLA Modules:
  0.0 176.2 jit_solution(12008709048086519349)
XLA Ops:
  6.5 0.0 reduce-scatter.2.cloned.1.call-start
  6.6 5.7 %fusion.35 = (bf16[256,1024]{1,0:T(8,128)(2,1)S(1)}, bf16[256,1024]{1,0:T(8,128)(2,1)}, bf16[256,1024]{1,0:T(8,128)(2,1)}) fusion(s32[256]{0:T(256)S(1)} %iota_add_fusion.4), kind=kLoop, calls=%fused_computation.70 | loop fusion | flops 5242880 | bytes 1573888 | tf_op jit(solution)/shard_map/convert.7
  12.3 3.2 %multiply_convert_fusion.5 = (bf16[512,256]{1,0:T(8,128)(2,1)}, bf16[512,256]{1,0:T(8,128)(2,1)}) fusion(s32[256]{0:T(256)S(1)} %iota_add_fusion.4, s32[512]{0:T(512)S(1)} %iota_add_fusion.3), kind=kLoop, calls=%fused_computation.79 | loop fusion | flops 2359296 | bytes 527360 | tf_op jit(solution)/shard_map/convert.8
  15.5 5.6 %multiply_convert_fusion.3 = (bf16[1024,256]{1,0:T(8,128)(2,1)S(1)}, bf16[1024,256]{1,0:T(8,128)(2,1)}) fusion(s32[256]{0:T(256)S(1)} %iota_add_fusion.4, s32[1024]{0:T(1024)S(1)} %iota_add_fusion.2), kind=kLoop, calls=%fused_computation.65 | loop fusion | flops 4980736 | bytes 1053696 | tf_op jit(solution)/shard_map/convert.10
  21.1 10.2 %multiply_convert_fusion.1 = (bf16[2048,256]{1,0:T(8,128)(2,1)}, bf16[2048,256]{1,0:T(8,128)(2,1)}) fusion(s32[256]{0:T(256)S(1)} %iota_add_fusion.4, s32[2048]{0:T(1024)S(1)} %iota_add_fusion.1), kind=kLoop, calls=%fused_computation.41 | loop fusion | flops 9437184 | bytes 2106368 | tf_op jit(solution)/shard_map/convert.12
  31.3 7.5 %fusion.19 = f32[512,512]{1,0:T(8,128)} fusion(bf16[2048,256]{1,0:T(8,128)(2,1)} %get-tuple-element.144, bf16[2048,256]{1,0:T(8,128)(2,1)} %get-tuple-element.143, bf16[2048,1024]{1,0:T(8,128)(2,1)} %param.5, bf16[1024,256]{1,0:T(8,128)(2,1)} %get-tuple-element.146, bf16[1024,256]{1,0:T(8,128)(2,1)S(1)} %get-tuple-element.145), kind=kOutput, calls=%fused_computation.35 | convolution fusion | flops 3228565504 | bytes 8388608 | tf_op jit(solution)/shard_map/dot_general | solution.py:30
  38.8 1.3 fusion.42
  40.1 66.0 %all-reduce.1 = bf16[2,256,256]{2,1,0:T(8,128)(2,1)S(1)} all-reduce(f32[2,256,256]{2,1,0:T(8,128)S(1)} %pad_maximum_fusion), channel_id=1, replica_groups=mesh['clip'=32,'row'=2,'src'=4] {'row','src'}, use_global_device_ids=true, to_apply=%region_0.1 | all-reduce | flops 131072 | bytes 786432 | tf_op jit(solution)/shard_map/psum | solution.py:89
  106.0 1.1 pad_maximum_fusion.1
  107.1 0.0 copy-start.2
  107.1 0.0 copy-start.3
  107.1 2.9 %maximum_maximum_fusion = bf16[512,2048]{1,0:T(8,128)(2,1)} fusion(bf16[256,1024]{1,0:T(8,128)(2,1)} %get-tuple-element.151, bf16[256,1024]{1,0:T(8,128)(2,1)} %get-tuple-element.150, bf16[256,1024]{1,0:T(8,128)(2,1)S(1)} %get-tuple-element.149), kind=kLoop, calls=%fused_computation.39 | loop fusion | flops 8388608 | bytes 3670016 | tf_op jit(solution)/shard_map/concatenate | solution.py:45
  110.0 0.0 copy-done.2
  110.0 0.0 copy-done.3
  110.0 29.0 %while.13 = (s32[]{:T(128)}, f32[512,1024]{1,0:T(8,128)S(1)}, s32[4]{0:T(128)S(1)}, s32[4,2]{0,1:T(2,128)S(1)}, bf16[2,256,256]{2,1,0:T(8,128)(2,1)S(1)}, /*inde...) while((s32[]{:T(128)}, f32[512,1024]{1,0:T(8,128)S(1)}, ...), condition=%wide.region_2.3_spmd.clone, body=%wide.region_1.2_spmd.clone.sunk | while | flops 1347683584 | bytes 29626572 | solution.py:77
  110.0 0.6 dynamic_slice.20
  111.3 0.1 constant_dynamic-slice_fusion.2
  111.3 0.5 fusion.62
  111.9 1.2 add_multiply_fusion.3
  113.1 0.1 fusion.63
  113.2 0.0 copy-start.1
  113.2 0.5 convolution_bitcast_fusion.2
  113.7 0.2 fusion.64
  113.9 0.9 copy-done.1
  114.8 1.3 fusion.65
  116.1 1.2 fusion.66
  117.3 0.6 dynamic_slice.20
  118.5 0.1 constant_dynamic-slice_fusion.2
  118.6 0.5 fusion.62
  119.1 1.2 add_multiply_fusion.3
  120.3 0.1 fusion.63
  120.5 0.0 copy-start.1
  120.5 0.5 convolution_bitcast_fusion.2
  121.0 0.2 fusion.64
  121.1 0.9 copy-done.1
  122.0 1.3 fusion.65
  123.3 1.2 fusion.66
  124.6 0.6 dynamic_slice.20
  125.8 0.1 constant_dynamic-slice_fusion.2
  125.9 0.5 fusion.62
  126.4 1.2 add_multiply_fusion.3
  127.6 0.1 fusion.63
  127.7 0.0 copy-start.1
  127.7 0.5 convolution_bitcast_fusion.2
  128.2 0.2 fusion.64
  128.4 0.9 copy-done.1
  129.3 1.3 fusion.65
  130.6 1.2 fusion.66
  131.8 0.6 dynamic_slice.20
  133.1 0.1 constant_dynamic-slice_fusion.2
  133.1 0.5 fusion.62
  133.7 1.2 add_multiply_fusion.3
  134.9 0.1 fusion.63
  135.0 0.0 copy-start.1
  135.0 0.5 convolution_bitcast_fusion.2
  135.5 0.2 fusion.64
  135.7 0.9 copy-done.1
  136.6 1.3 fusion.65
  137.9 1.2 fusion.66
  139.1 0.0 copy-start
  139.1 1.3 copy-done
  140.4 0.0 reduce-scatter.2.cloned.1.call-update
  140.4 27.0 %reduce-scatter.2.cloned.1.call-done = f32[128,1024]{1,0:T(8,128)} async-done(((f32[512,1024]{1,0:T(8,128)}), f32[128,1024]{1,0:T(8,128)}) %reduce-scatter.2.cloned.1.call-update) | async-done | bytes 524304 | tf_op jit(solution)/shard_map/reduce_scatter | solution.py:95
  167.5 1.9 %broadcast_multiply_fusion = f32[128,1024]{1,0:T(8,128)} fusion(f32[128,1024]{1,0:T(8,128)} %reduce-scatter.2.cloned.1.call-done), kind=kLoop, calls=%fused_computation.84 | loop fusion | flops 131072 | bytes 1048576 | tf_op jit(solution)/shard_map/div | solution.py:101
  (6 shorter events, 0.1 us)
Async XLA Ops:
  6.5 161.0 %reduce-scatter.2.cloned.1.call-start = ((), (), s32[]{:S(2)}) async-start(), calls=%async_computation.1 | async-start | bytes 2621440 | tf_op jit(solution)/shard_map/reduce_scatter | solution.py:95
  107.1 2.9 %copy-start.2 = (s32[4,2]{0,1:T(2,128)S(1)}, s32[4,2]{0,1:T(2,128)}, u32[]{:S(2)}) copy-start(s32[4,2]{0,1:T(2,128)} %param.6) | copy-start | bytes 100
  107.1 2.9 %copy-start.3 = (s32[4]{0:T(128)S(1)}, s32[4]{0:T(128)}, u32[]{:S(2)}) copy-start(s32[4]{0:T(128)} %param.7) | copy-start | bytes 52
  113.2 1.6 copy-start.1
  120.5 1.6 copy-start.1
  127.7 1.6 copy-start.1
  135.0 1.6 copy-start.1
  139.1 1.3 copy-start
Sparse Core Ops, SparseCore 0:
  140.6 26.8 reduce-scatter.1
where the time goes:
time: 178 us; the launch traced here: 176 us
  blocking collectives  66 us (37%)
  other arithmetic  42.6 us (24%)
  waiting for transfers between devices  27.1 us (15%)
  matrix products  14.5 us (8%)
  between operations  13.5 us (8%)
  local copies, waits for them, and re-layouts  9.76 us (5%)
  loops' own time  2.82 us (2%)
    psum x1, blocking collectives, body(): spectrum = lax.psum(partial_value, ('row', 'src')).astype(jnp.bfloat16)  66 us
    reduce_scatter x1, waiting for transfers between devices, body(): lax.psum_scatter(image_rows_sum(spectrum, image_rows, source_shifts, sour...  27 us
    another operation x8, other arithmetic  25.4 us
    dot_general x1, matrix products, tile_spectrum(): blocks = jnp.dot(row_table, half_way, preferred_element_type=jnp.float32)  7.46 us
    dot_general x4, matrix products, source_image(): jnp.dot(partial_value, right_table, preferred_element_type=jnp.float32)  5.14 us
    add x4, other arithmetic, add_source(): running + source_image(spectrum, shift_pair, weight, left_table, right_ta...  4.83 us
    mul x4, other arithmetic, source_image(): along_cols[None, :] * along_cols[None, :]  4.79 us
    while x8, local copies, waits for them, and re-layouts  3.7 us
  transfers between devices with their start and end apart: 1, of which 1 were waited for; matrix products, arithmetic and copies ran while one was open for 0% of the time, Pallas kernels for 0%

commit v1 on v0

v1 whole, which is shorter than its diff:
```python
import math

import jax
import jax.numpy as jnp
import numpy as np
from jax import lax
from jax.experimental import pallas as pl
from jax.experimental.pallas import tpu as pltpu
from jax.sharding import PartitionSpec as P

NM = 4096
NI = 1024
HALF = 128
BLOCK = 512
NT = (((1,), (1,)), ((), ()))
F32 = jnp.float32
BF16 = jnp.bfloat16


def forward_tables():
    freq = np.arange(HALF)
    pos = np.arange(NM // 4)
    angle = 2.0 * np.pi * ((freq[:, None] * pos[None, :]) % NM) / NM
    edge = 2.0 * np.pi * ((HALF * pos) % NM) / NM
    table = np.zeros((272, NM // 4), np.float64)
    table[:HALF] = np.cos(angle)
    table[HALF:256] = np.sin(angle)
    table[256] = np.cos(edge)
    table[257] = np.sin(edge)
    pattern = np.zeros((16, HALF), np.float64)
    pattern[2] = np.cos(edge[:HALF])
    pattern[3] = np.sin(edge[:HALF])
    return (table / 64).astype(np.float32), (pattern / 64).astype(np.float32)


def signed_frequencies():
    freq = np.concatenate([np.arange(HALF), -np.arange(HALF)])
    freq[HALF] = -HALF
    return freq


def inverse_tables():
    freq = signed_frequencies()
    rows = np.arange(NI)
    angle = 2.0 * np.pi * ((rows[:, None] * freq[None, :]) % NI) / NI
    left = np.stack([np.cos(angle), np.sin(angle)]).reshape(2, 8, HALF, 256)
    left = left.transpose(1, 0, 2, 3).reshape(8, 256, 256) / 16
    cos_y, sin_y = np.cos(angle).T / 16, np.sin(angle).T / 16
    right = np.stack([np.concatenate([cos_y, -sin_y], 0), np.concatenate([sin_y, cos_y], 0)])
    return left.astype(np.float32), right.astype(np.float32)


def quarter(turns):
    q = jnp.bitwise_and(turns, 3)
    cos_q = jnp.where(q == 0, 1.0, jnp.where(q == 2, -1.0, 0.0)).astype(F32)
    sin_q = jnp.where(q == 1, 1.0, jnp.where(q == 3, -1.0, 0.0)).astype(F32)
    return cos_q, sin_q


def forward_kernel(shifts, weights, mask, table, pattern, out, acc, acc_edge):
    step = pl.program_id(0)
    part = step // 2
    block = mask[...]
    half_way = lax.dot_general(block, table[:256, :], NT, preferred_element_type=F32).astype(BF16)
    folded = block[:, :HALF].astype(F32)
    for tile in range(1, 8):
        folded = folded + block[:, tile * HALF:(tile + 1) * HALF].astype(F32)
    folded = folded.astype(BF16)
    columns = pl.ds(pl.multiple_of((step % 2) * BLOCK, BLOCK), BLOCK)
    rows = table[:, columns]
    first = jnp.dot(rows, half_way, preferred_element_type=F32)
    second = jnp.dot(rows[:256], folded, preferred_element_type=F32)

    @pl.when(step % 2 == 0)
    def _():
        acc[part] = first
        acc_edge[part] = second

    @pl.when(step % 2 == 1)
    def _():
        acc[part] += first
        acc_edge[part] += second

    @pl.when(step == 3)
    def _():
        row_id = lax.axis_index("row")
        src_id = lax.axis_index("src")
        f_col = lax.broadcasted_iota(jnp.int32, (HALF, 256), 0)
        cos_q, sin_q = quarter(f_col)
        sign, _ = quarter(f_col * 2 * row_id)

        def join_rows(a, b, width):
            c, s, g = cos_q[:, :width], sin_q[:, :width], sign[:, :width]
            top = (a[:HALF] + c * b[:HALF] - s * b[HALF:256]) * g
            low = (a[HALF:256] + c * b[HALF:256] + s * b[:HALF]) * g
            return top, low

        def turn_columns(x):
            g_row = lax.broadcasted_iota(jnp.int32, (x.shape[0], HALF), 1)
            c, s = quarter(g_row * src_id)
            return c * x[:, :HALF] - s * x[:, HALF:], c * x[:, HALF:] + s * x[:, :HALF]

        a, b = acc[0], acc[1]
        top, low = join_rows(a, b, 256)
        for start, x in ((0, top), (HALF, low)):
            x_cos, x_sin = turn_columns(x)
            out[start:start + HALF, :HALF] = x_cos.astype(BF16)
            out[start:start + HALF, HALF:] = x_sin.astype(BF16)
        e_cos, e_sin = turn_columns(a[256:] + b[256:])
        edge_top, edge_low = join_rows(acc_edge[0], acc_edge[1], HALF)
        edges = jnp.concatenate([edge_top, edge_low], 0).astype(BF16)
        crossed = lax.dot_general(pattern[...], edges, NT, preferred_element_type=F32)
        row = lax.broadcasted_iota(jnp.int32, (16, HALF), 0)
        e_cos = e_cos + crossed[:, :HALF]
        e_sin = e_sin + crossed[:, HALF:]
        shift_f = jnp.zeros((16, HALF), F32)
        shift_g = jnp.zeros((16, HALF), F32)
        for i in range(4):
            w = weights[i].astype(F32)
            here = row == 4 + src_id * 2 + i // 2
            if i % 2 == 0:
                e_cos = jnp.where(here, w, e_cos)
            else:
                e_sin = jnp.where(here, w, e_sin)
            mine = row == src_id * 4 + i
            shift_f = jnp.where(mine, shifts[i, 0].astype(F32), shift_f)
            shift_g = jnp.where(mine, shifts[i, 1].astype(F32), shift_g)
        out[256:272, :HALF] = e_cos.astype(BF16)
        out[256:272, HALF:] = e_sin.astype(BF16)
        out[272:288, :HALF] = shift_f.astype(BF16)
        out[272:288, HALF:] = shift_g.astype(BF16)


def forward(mask_clip, shifts, weights, table, pattern):
    return pl.pallas_call(
        forward_kernel,
        grid=(4,),
        in_specs=[
            pl.BlockSpec(memory_space=pltpu.SMEM),
            pl.BlockSpec(memory_space=pltpu.SMEM),
            pl.BlockSpec((BLOCK, NM // 4), lambda i: (i, 0)),
            pl.BlockSpec((272, NM // 4), lambda i: (0, 0)),
            pl.BlockSpec((16, HALF), lambda i: (0, 0)),
        ],
        out_specs=pl.BlockSpec((288, 256), lambda i: (0, 0)),
        out_shape=jax.ShapeDtypeStruct((288, 256), BF16),
        scratch_shapes=[pltpu.VMEM((2, 272, 256), F32), pltpu.VMEM((2, 256, HALF), F32)],
        compiler_params=pltpu.CompilerParams(vmem_limit_bytes=60 * 1024 * 1024),
        cost_estimate=pl.CostEstimate(flops=1_700_000_000, bytes_accessed=5_000_000, transcendentals=0),
        name="forward",
    )(shifts, weights, mask_clip, table, pattern)


def inverse_kernel(mine, other, left, right, out, spec, fields):
    total = mine[:256].astype(F32) + other[:256].astype(F32)
    cc, cs = total[:HALF, :HALF], total[:HALF, HALF:]
    sc, ss = total[HALF:, :HALF], total[HALF:, HALF:]
    edge = mine[256:272].astype(F32) + other[256:272].astype(F32)
    rc, rs = edge[0:1], edge[1:2]
    xc, xs = edge[2:3], edge[3:4]
    row_re = (rc[:, :HALF] + rs[:, HALF:], rc[:, :HALF] - rs[:, HALF:])
    row_im = (rs[:, :HALF] - rc[:, HALF:], rs[:, :HALF] + rc[:, HALF:])
    col_re = jnp.concatenate([xc[:, :HALF] + xs[:, HALF:], xc[:, :HALF] - xs[:, HALF:]], 1)
    col_im = jnp.concatenate([xs[:, :HALF] - xc[:, HALF:], xs[:, :HALF] + xc[:, HALF:]], 1)
    first_row = lax.broadcasted_iota(jnp.int32, (HALF, HALF), 0) == 0
    first_lane = lax.broadcasted_iota(jnp.int32, (HALF, HALF), 1) == 0

    def stand(row):
        return jnp.broadcast_to(row, (HALF, HALF)).T

    quads = {
        (0, 0): (cc - ss, -(sc + cs)),
        (0, 1): (cc + ss, cs - sc),
        (1, 0): (cc + ss, sc - cs),
        (1, 1): (cc - ss, sc + cs),
    }
    for (i, j), (re, im) in quads.items():
        if i == 1:
            re = jnp.where(first_row, row_re[j], re)
            im = jnp.where(first_row, row_im[j], im)
        if j == 1:
            re = jnp.where(first_lane, stand(col_re[:, i * HALF:(i + 1) * HALF]), re)
            im = jnp.where(first_lane, stand(col_im[:, i * HALF:(i + 1) * HALF]), im)
        spec[i * HALF:(i + 1) * HALF, j * HALF:(j + 1) * HALF] = re.astype(BF16)
        spec[i * HALF:(i + 1) * HALF, 256 + j * HALF:256 + (j + 1) * HALF] = im.astype(BF16)

    shifts = mine[272:288].astype(F32)
    loads = jnp.sqrt(mine[256:272].astype(F32)) * 0.25
    f_low = lax.broadcasted_iota(jnp.int32, (HALF, HALF), 0)
    g_low = lax.broadcasted_iota(jnp.int32, (1, HALF), 1)
    f_halves = (f_low.astype(F32), jnp.where(f_low == 0, -HALF, -f_low).astype(F32))
    g_halves = (g_low.astype(F32), jnp.where(g_low == 0, -HALF, -g_low).astype(F32))
    zero = jnp.zeros((HALF, HALF), BF16)
    for s in range(16):
        a, b = shifts[s:s + 1, :HALF], shifts[s:s + 1, HALF:]
        w = loads[4 + s // 2:5 + s // 2, (s % 2) * HALF:(s % 2 + 1) * HALF]
        room = [4096.0 - (f + a) * (f + a) for f in f_halves]
        reach = [(g + b) * (g + b) for g in g_halves]
        inside = [[r >= q for q in reach] for r in room]
        passed = jnp.concatenate(
            [
                jnp.concatenate(
                    [
                        jnp.where(
                            inside[i][j % 2],
                            spec[i * HALF:(i + 1) * HALF, j * HALF:(j + 1) * HALF],
                            zero,
                        )
                        for j in range(4)
                    ],
                    1,
                )
                for i in range(2)
            ],
            0,
        )
        blocks = jnp.dot(left[...], passed, preferred_element_type=F32)
        w2 = jnp.concatenate([w, w], 1)
        k_re = (blocks[:HALF, :256] - blocks[HALF:, 256:]) * w2
        k_im = (blocks[:HALF, 256:] + blocks[HALF:, :256]) * w2
        fields[s * HALF:(s + 1) * HALF, :256] = k_re.astype(BF16)
        fields[s * HALF:(s + 1) * HALF, 256:] = k_im.astype(BF16)
    for chunk in range(4):
        span = slice(chunk * 256, (chunk + 1) * 256)
        summed = jnp.zeros((HALF, 256), F32)
        for group in range(4):
            k = fields[group * 512:(group + 1) * 512, :]
            e_re = jnp.dot(k, right[0, :, span], preferred_element_type=F32)
            e_im = jnp.dot(k, right[1, :, span], preferred_element_type=F32)
            power = e_re * e_re + e_im * e_im
            for i in range(4):
                summed = summed + power[i * HALF:(i + 1) * HALF]
        out[:, span] = summed


def inverse(mine, other, left, right):
    vmem = pl.BlockSpec(memory_space=pltpu.VMEM)
    return pl.pallas_call(
        inverse_kernel,
        in_specs=[vmem] * 4,
        out_specs=vmem,
        out_shape=jax.ShapeDtypeStruct((HALF, NI), F32),
        scratch_shapes=[pltpu.VMEM((256, 512), BF16), pltpu.VMEM((2048, 512), BF16)],
        compiler_params=pltpu.CompilerParams(vmem_limit_bytes=24 * 1024 * 1024),
        cost_estimate=pl.CostEstimate(flops=5_400_000_000, bytes_accessed=3_000_000, transcendentals=0),
        name="inverse",
    )(mine, other, left, right)


def body(mask_clip, source_shifts, source_weights):
    table, pattern = forward_tables()
    left, right = inverse_tables()
    place = lax.axis_index("row") * 4 + lax.axis_index("src")
    left_mine = lax.dynamic_index_in_dim(jnp.asarray(left, BF16), place, 0, keepdims=False)
    partial_sum = forward(
        mask_clip, source_shifts, source_weights, jnp.asarray(table, BF16), jnp.asarray(pattern, BF16)
    )
    summed = partial_sum.astype(F32)
    for k in (1, 2, 3):
        summed = summed + lax.ppermute(partial_sum, "src", [(i, (i + k) % 4) for i in range(4)]).astype(F32)
    summed = summed.astype(BF16)
    other = lax.ppermute(summed, "row", [(0, 1), (1, 0)])
    return inverse(summed, other, left_mine, jnp.asarray(right, BF16))


def solution(mesh):
    placed = (P(("clip", "row"), "src"), P("src", None), P("src"))
    return jax.shard_map(
        body, mesh=mesh, in_specs=placed, out_specs=P(("clip", "row", "src"), None), check_vma=False
    )
```

time: 178 us -> 43.5 us (0.24)
  the two profiles are of different devices: /device:TPU:8 before, /device:TPU:32 now
where the time goes in v1:
time: 43.5 us; the launch traced here: 43.3 us
  waiting for transfers between devices  14.8 us (34%)
  Pallas kernels  14.2 us (33%)
  starting transfers between devices  10.8 us (25%)
  local copies, waits for them, and re-layouts  2.4 us (6%)
  other arithmetic  0.99 us (2%)
    ppermute x3, waiting for transfers between devices, body(): lax.ppermute(partial_sum, 'src', [(i, (i + k) % 4) for i in range(4)])  8.5 us
    pallas_call x1, Pallas kernels, inverse(): pl.pallas_call(inverse_kernel, in_specs=[vmem] * 4, out_specs=vmem, out_s...  7.37 us
    pallas_call x1, Pallas kernels, forward(): pl.pallas_call(forward_kernel, grid=(4,), in_specs=[pl.BlockSpec(memory_s...  6.86 us
    ppermute x1, starting transfers between devices, body(): other = lax.ppermute(summed, 'row', [(0, 1), (1, 0)])  6.38 us
    ppermute x1, waiting for transfers between devices, body(): other = lax.ppermute(summed, 'row', [(0, 1), (1, 0)])  6.32 us
    ppermute x3, starting transfers between devices, body(): lax.ppermute(partial_sum, 'src', [(i, (i + k) % 4) for i in range(4)])  4.44 us
    unnamed x3, local copies, waits for them, and re-layouts  1.49 us
    convert_element_type x1, other arithmetic, body(): summed = summed.astype(BF16)  0.99 us
  transfers between devices with their start and end apart: 4, of which 4 were waited for; matrix products, arithmetic and copies ran while one was open for 2% of the time, Pallas kernels for 0%

profile of v1, /device:TPU:32, one launch (start us, length us, event | category | flops | bytes accessed | tf_op | source)
XLA Modules:
  0.0 43.3 jit_solution(3115220809979383395)
XLA Ops:
  0.0 0.0 copy-start
  0.0 1.5 %copy.8.shifts = s32[4,2]{1,0:T(4,128)} copy(s32[4,2]{0,1:T(2,128)} %param.8) | data formatting | bytes 64 | tf_op args[1]
  1.5 6.9 %forward.1 = bf16[288,256]{1,0:T(8,128)(2,1)} custom-call(s32[4,2]{1,0:T(4,128)} %copy.8.shifts, s32[4]{0:T(128)} %weights.1, bf16[2048,1024]{1,0:T(8,128)(2,1)} %mask.1, bf16[272,1024]{1,0:T(8,128)(2,1)} %constant.26.clone.table, bf16[16,128]{1,0:T(8,128)(2,1)} %constant.27.clone.pattern), custom_call_target="tpu_custom_call" | custom-call | flops 1700000000 | bytes 5000000 | tf_op jit(solution)/shard_map/forward/pallas_call | solution.py:135
  8.3 2.8 %collective-permute-start.2 = (bf16[288,256]{1,0:T(8,128)(2,1)}, bf16[288,256]{1,0:T(8,128)(2,1)S(1)}, u32[]{:S(2)}, u32[]{:S(2)}) collective-permute-start(bf16[288,256]{1,0:T(8,128)(2,1)} %forward.1), channel_id=1, source_target_pairs={{0,3},{1,0},{2,1},{3,2},{4,7},{5,4},{6,5},{7,6},{8,11},{9,8},{10,9... | collective-permute-start | bytes 442376 | tf_op jit(solution)/shard_map/ppermute | solution.py:260
  11.1 0.8 %collective-permute-start.1 = (bf16[288,256]{1,0:T(8,128)(2,1)}, bf16[288,256]{1,0:T(8,128)(2,1)S(1)}, u32[]{:S(2)}, u32[]{:S(2)}) collective-permute-start(bf16[288,256]{1,0:T(8,128)(2,1)} %forward.1), channel_id=1, source_target_pairs={{0,2},{1,3},{2,0},{3,1},{4,6},{5,7},{6,4},{7,5},{8,10},{9,11},{10,... | collective-permute-start | bytes 442376 | tf_op jit(solution)/shard_map/ppermute | solution.py:260
  11.9 0.9 %collective-permute-start = (bf16[288,256]{1,0:T(8,128)(2,1)}, bf16[288,256]{1,0:T(8,128)(2,1)S(1)}, u32[]{:S(2)}, u32[]{:S(2)}) collective-permute-start(bf16[288,256]{1,0:T(8,128)(2,1)} %forward.1), channel_id=1, source_target_pairs={{0,1},{1,2},{2,3},{3,0},{4,5},{5,6},{6,7},{7,4},{8,9},{9,10},{10,1... | collective-permute-start | bytes 442376 | tf_op jit(solution)/shard_map/ppermute | solution.py:260
  12.8 4.9 %collective-permute-done.2 = bf16[288,256]{1,0:T(8,128)(2,1)S(1)} collective-permute-done((bf16[288,256]{1,0:T(8,128)(2,1)}, bf16[288,256]{1,0:T(8,128)(2,1)S(1)}, u32[]{:S(2)}, u32[]{:S(2)}) %collective-permute-start.2) | collective-permute-done | bytes 147488 | tf_op jit(solution)/shard_map/ppermute | solution.py:260
  17.7 1.8 %collective-permute-done.1 = bf16[288,256]{1,0:T(8,128)(2,1)S(1)} collective-permute-done((bf16[288,256]{1,0:T(8,128)(2,1)}, bf16[288,256]{1,0:T(8,128)(2,1)S(1)}, u32[]{:S(2)}, u32[]{:S(2)}) %collective-permute-start.1) | collective-permute-done | bytes 147488 | tf_op jit(solution)/shard_map/ppermute | solution.py:260
  19.5 1.7 %collective-permute-done = bf16[288,256]{1,0:T(8,128)(2,1)S(1)} collective-permute-done((bf16[288,256]{1,0:T(8,128)(2,1)}, bf16[288,256]{1,0:T(8,128)(2,1)S(1)}, u32[]{:S(2)}, u32[]{:S(2)}) %collective-permute-start) | collective-permute-done | bytes 147488 | tf_op jit(solution)/shard_map/ppermute | solution.py:260
  21.3 1.0 %add_convert_fusion.mine = bf16[288,256]{1,0:T(8,128)(2,1)S(1)} fusion(bf16[288,256]{1,0:T(8,128)(2,1)S(1)} %collective-permute-done.2, bf16[288,256]{1,0:T(8,128)(2,1)S(1)} %collective-permute-done.1, bf16[288,256]{1,0:T(8,128)(2,1)S(1)} %collective-permute-done, bf16[288,256]{1,0:T(8,128)(2,1)} %forward.1), kind=kLoop, calls=%fused_computation | loop fusion | flops 589824 | bytes 737280 | tf_op jit(solution)/shard_map/convert_element_type | solution.py:261
  22.3 6.4 %collective-permute-start.3 = (bf16[288,256]{1,0:T(8,128)(2,1)S(1)}, bf16[288,256]{1,0:T(8,128)(2,1)S(1)}, u32[]{:S(2)}, u32[]{:S(2)}) collective-permute-start(bf16[288,256]{1,0:T(8,128)(2,1)S(1)} %add_convert_fusion.mine), channel_id=1, source_target_pairs={{0,4},{4,0},{1,5},{5,1},{2,6},{6,2},{3,7},{7,3},{8,12},{12,8},{9,1... | collective-permute-start | bytes 442376 | tf_op jit(solution)/shard_map/ppermute | solution.py:262
  28.7 0.9 %dynamic-slice_bitcast_fusion.left = bf16[256,256]{1,0:T(8,128)(2,1)S(1)} fusion(bf16[8,256,256]{2,1,0:T(8,128)(2,1)} %constant.25.clone, s32[]{:T(128)S(6)} %select_n.4), kind=kLoop, calls=%fused_computation.1 | loop fusion | bytes 262148 | tf_op jit(solution)/shard_map/jit(dynamic_index_in_dim)/squeeze | solution.py:254
  29.6 6.3 %collective-permute-done.3.other = bf16[288,256]{1,0:T(8,128)(2,1)S(1)} collective-permute-done((bf16[288,256]{1,0:T(8,128)(2,1)S(1)}, bf16[288,256]{1,0:T(8,128)(2,1)S(1)}, u32[]{:S(2)}, u32[]{:S(2)}) %collective-permute-start.3) | collective-permute-done | bytes 147488 | tf_op jit(solution)/shard_map/ppermute | solution.py:262
  35.9 0.0 copy-done
  35.9 7.4 %inverse.1 = f32[128,1024]{1,0:T(8,128)} custom-call(bf16[288,256]{1,0:T(8,128)(2,1)S(1)} %add_convert_fusion.mine, bf16[288,256]{1,0:T(8,128)(2,1)S(1)} %collective-permute-done.3.other, bf16[256,256]{1,0:T(8,128)(2,1)S(1)} %dynamic-slice_bitcast_fusion.left, bf16[2,512,1024]{2,1,0:T(8,128)(2,1)S(1)} %copy-done), custom_call_target="tpu_custom_call" | custom-call | flops 5400000000 | bytes 3000000 | tf_op jit(solution)/shard_map/inverse/pallas_call | solution.py:238
Async XLA Ops:
  0.0 35.9 %copy-start = (bf16[2,512,1024]{2,1,0:T(8,128)(2,1)S(1)}, bf16[2,512,1024]{2,1,0:T(8,128)(2,1)}, u32[]{:S(2)}) copy-start(bf16[2,512,1024]{2,1,0:T(8,128)(2,1)} %constant.28.clone.right) | copy-start | bytes 6291460
  8.3 9.4 %collective-permute-start.2 = (bf16[288,256]{1,0:T(8,128)(2,1)}, bf16[288,256]{1,0:T(8,128)(2,1)S(1)}, u32[]{:S(2)}, u32[]{:S(2)}) collective-permute-start(bf16[288,256]{1,0:T(8,128)(2,1)} %forward.1), channel_id=1, source_target_pairs={{0,3},{1,0},{2,1},{3,2},{4,7},{5,4},{6,5},{7,6},{8,11},{9,8},{10,9... | collective-permute-start | bytes 442376 | tf_op jit(solution)/shard_map/ppermute | solution.py:260
  11.1 8.4 %collective-permute-start.1 = (bf16[288,256]{1,0:T(8,128)(2,1)}, bf16[288,256]{1,0:T(8,128)(2,1)S(1)}, u32[]{:S(2)}, u32[]{:S(2)}) collective-permute-start(bf16[288,256]{1,0:T(8,128)(2,1)} %forward.1), channel_id=1, source_target_pairs={{0,2},{1,3},{2,0},{3,1},{4,6},{5,7},{6,4},{7,5},{8,10},{9,11},{10,... | collective-permute-start | bytes 442376 | tf_op jit(solution)/shard_map/ppermute | solution.py:260
  11.9 9.4 %collective-permute-start = (bf16[288,256]{1,0:T(8,128)(2,1)}, bf16[288,256]{1,0:T(8,128)(2,1)S(1)}, u32[]{:S(2)}, u32[]{:S(2)}) collective-permute-start(bf16[288,256]{1,0:T(8,128)(2,1)} %forward.1), channel_id=1, source_target_pairs={{0,1},{1,2},{2,3},{3,0},{4,5},{5,6},{6,7},{7,4},{8,9},{9,10},{10,1... | collective-permute-start | bytes 442376 | tf_op jit(solution)/shard_map/ppermute | solution.py:260
  22.3 13.6 %collective-permute-start.3 = (bf16[288,256]{1,0:T(8,128)(2,1)S(1)}, bf16[288,256]{1,0:T(8,128)(2,1)S(1)}, u32[]{:S(2)}, u32[]{:S(2)}) collective-permute-start(bf16[288,256]{1,0:T(8,128)(2,1)S(1)} %add_convert_fusion.mine), channel_id=1, source_target_pairs={{0,4},{4,0},{1,5},{5,1},{2,6},{6,2},{3,7},{7,3},{8,12},{12,8},{9,1... | collective-permute-start | bytes 442376 | tf_op jit(solution)/shard_map/ppermute | solution.py:262

commit v2 on v0

v2 whole, which is shorter than its diff:
```python
import jax
import jax.numpy as jnp
import numpy as np
from jax import lax
from jax.experimental import pallas as pl
from jax.experimental.pallas import tpu as pltpu
from jax.sharding import PartitionSpec as P

NM = 4096
NI = 1024
TILE = NM // 4
HALF = 128
CHUNKS = ((0, 512), (512, 1024), (1024, 2048))
COARSE = 256
NT = (((1,), (1,)), ((), ()))
F32 = jnp.float32
BF16 = jnp.bfloat16
VMEM = pl.BlockSpec(memory_space=pltpu.VMEM)


def forward_tables():
    freq = np.arange(HALF)
    pos = np.arange(TILE)
    angle = 2.0 * np.pi * ((freq[:, None] * pos[None, :]) % NM) / NM
    edge = 2.0 * np.pi * ((HALF * pos) % NM) / NM
    table = np.zeros((272, TILE), np.float64)
    table[:HALF] = np.cos(angle)
    table[HALF:256] = np.sin(angle)
    table[256] = np.cos(edge)
    table[257] = np.sin(edge)
    table[266, :HALF] = np.cos(edge[:HALF])
    table[267, :HALF] = np.sin(edge[:HALF])
    return (table / 64).astype(np.float32)


def inverse_tables():
    freq = np.concatenate([np.arange(HALF), -np.arange(HALF)])
    freq[HALF] = -HALF
    rows = np.arange(NI)
    angle = 2.0 * np.pi * ((rows[:, None] * freq[None, :]) % NI) / NI
    left = [np.stack([np.cos(angle[:HALF] + t), np.sin(angle[:HALF] + t)]) / 16 for t in (0.0, np.pi / 4)]
    left = np.stack(left)
    cos_y, sin_y = np.cos(angle[::4]).T / 16, np.sin(angle[::4]).T / 16
    right = np.stack([np.concatenate([cos_y, -sin_y], 0), np.concatenate([sin_y, cos_y], 0)])
    j = np.arange(COARSE)
    harmonic = np.arange(1, HALF)
    columns = np.arange(NI)
    distance = (columns[None, :] - 4 * j[:, None]) % NI
    lags = 2.0 * np.pi * ((np.arange(NI)[:, None] * harmonic[None, :]) % NI) / NI
    wave = (1.0 + 2.0 * np.cos(lags).sum(1) + np.cos(2.0 * np.pi * (np.arange(NI) * HALF % NI) / NI)) / COARSE
    spread = wave[distance]
    high = np.asarray(spread.astype(np.float32).astype(BF16), np.float64)
    spread = np.stack([high, spread - high])
    sine = np.zeros((8, NI), np.float64)
    sine[0] = -2.0 * np.sin(np.pi * (columns % 8) / 4) / 256
    return tuple(x.astype(np.float32) for x in (left, right, spread, sine))


def quarter(turns):
    q = jnp.bitwise_and(turns, 3)
    cos_q = jnp.where(q == 0, 1.0, jnp.where(q == 2, -1.0, 0.0)).astype(F32)
    sin_q = jnp.where(q == 1, 1.0, jnp.where(q == 3, -1.0, 0.0)).astype(F32)
    return cos_q, sin_q


def forward_kernel(shifts_in, weights_in, mask, table_in, own, one, two, three,
                   shifts, weights, block, table, half_way, folded, whole, edge, sem):
    small_copies = [
        pltpu.make_async_copy(table_in, table, sem.at[0]),
        pltpu.make_async_copy(shifts_in, shifts, sem.at[1]),
        pltpu.make_async_copy(weights_in, weights, sem.at[2]),
    ]
    copies = [
        pltpu.make_async_copy(mask.at[start:stop], block.at[start:stop], sem.at[3 + i])
        for i, (start, stop) in enumerate(CHUNKS)
    ]
    for copy in (small_copies[0], *copies, *small_copies[1:]):
        copy.start()
    row_id = lax.axis_index("row")
    src_id = lax.axis_index("src")
    f_col = lax.broadcasted_iota(jnp.int32, (HALF, 256), 0)
    cos_f, sin_f = quarter(f_col)
    sign, _ = quarter(f_col * 2 * row_id)
    cos_g, sin_g = quarter(lax.broadcasted_iota(jnp.int32, (HALF, HALF), 1) * src_id)

    def join_rows(a, b):
        top = (a[:HALF] + cos_f * b[:HALF] - sin_f * b[HALF:256]) * sign
        low = (a[HALF:256] + cos_f * b[HALF:256] + sin_f * b[:HALF]) * sign
        return top, low

    def turn_columns(x):
        c, s = cos_g[:x.shape[0]], sin_g[:x.shape[0]]
        return c * x[:, :HALF] - s * x[:, HALF:], c * x[:, HALF:] + s * x[:, :HALF]

    small_copies[0].wait()
    sums = []
    for copy, (start, stop) in zip(copies, CHUNKS):
        copy.wait()
        part, at = start // TILE, start % TILE
        half_way[start:stop] = lax.dot_general(
            block[start:stop], table[:256, :], NT, preferred_element_type=F32
        ).astype(BF16)
        for low in range(0, stop - start, 64):
            rows = slice(start + low, start + low + 64)
            tiles = [block[rows, tile * HALF:(tile + 1) * HALF] for tile in range(8)]
            while len(tiles) > 1:
                tiles = [tiles[t] + tiles[t + 1] for t in range(0, len(tiles), 2)]
            folded[at + low:at + low + 64, part * HALF:(part + 1) * HALF] = tiles[0]
        if start == TILE:
            sums.append(jnp.dot(table[:264], half_way[:TILE], preferred_element_type=F32))
    sums.append(jnp.dot(table[:264], half_way[TILE:], preferred_element_type=F32))
    sides = jnp.dot(table[:256, :], folded[...], preferred_element_type=F32)
    for copy in small_copies[1:]:
        copy.wait()
    a, b = sums
    for start, x in zip((0, HALF), join_rows(a, b)):
        x_cos, x_sin = turn_columns(x)
        whole[start:start + HALF, :HALF] = x_cos
        whole[start:start + HALF, HALF:] = x_sin
    e_cos, e_sin = turn_columns(a[256:] + b[256:])
    s_a, s_b = sides[:, :HALF], sides[:, HALF:]
    c, s, g = cos_f[:, :HALF], sin_f[:, :HALF], sign[:, :HALF]
    edges = jnp.concatenate(
        [
            (s_a[:HALF] + c * s_b[:HALF] - s * s_b[HALF:]) * g,
            (s_a[HALF:] + c * s_b[HALF:] + s * s_b[:HALF]) * g,
        ],
        0,
    ).astype(BF16)
    crossed = lax.dot_general(table[264:272, :HALF], edges, NT, preferred_element_type=F32)
    edge[:, :HALF] = e_cos + crossed[:, :HALF]
    edge[:, HALF:] = e_sin + crossed[:, HALF:]
    row = lax.broadcasted_iota(jnp.int32, (8, HALF), 0)
    first = jnp.zeros((8, HALF), F32)
    second = jnp.zeros((8, HALF), F32)
    for i in range(4):
        first = jnp.where(row == 1 + i, shifts[0, i].astype(F32), first)
        second = jnp.where(row == 1 + i, shifts[1, i].astype(F32), second)
        w = weights[i].astype(F32)
        if i % 2 == 0:
            first = jnp.where(row == 5 + i // 2, w, first)
        else:
            second = jnp.where(row == 5 + i // 2, w, second)
    sources = jnp.concatenate([first, second], 1)
    row = lax.broadcasted_iota(jnp.int32, (8, 256), 0)
    for k, out in enumerate((own, one, two, three)):
        q = lax.rem(src_id + k, 4)
        low = pl.ds(pl.multiple_of(q * 32, 32), 32)
        high = pl.ds(pl.multiple_of(HALF + q * 32, 32), 32)
        out[:32] = whole[low].astype(BF16)
        out[32:64] = whole[high].astype(BF16)
        line = edge[pl.ds(q, 1)]
        out[64:72] = jnp.where(row == 0, line, sources if k == 0 else 0.0).astype(BF16)


def forward(mask_clip, shifts, weights, table):
    quarter_shape = jax.ShapeDtypeStruct((72, 256), BF16)
    hbm = pl.BlockSpec(memory_space=pltpu.HBM)
    return pl.pallas_call(
        forward_kernel,
        in_specs=[hbm] * 4,
        out_specs=[VMEM] * 4,
        out_shape=[quarter_shape] * 4,
        scratch_shapes=[
            pltpu.SMEM((2, 4), jnp.int32),
            pltpu.SMEM((4,), jnp.int32),
            pltpu.VMEM((2 * TILE, TILE), BF16),
            pltpu.VMEM((272, TILE), BF16),
            pltpu.VMEM((2 * TILE, 256), BF16),
            pltpu.VMEM((TILE, 256), BF16),
            pltpu.VMEM((256, 256), F32),
            pltpu.VMEM((8, 256), F32),
            pltpu.SemaphoreType.DMA((3 + len(CHUNKS),)),
        ],
        compiler_params=pltpu.CompilerParams(vmem_limit_bytes=16 * 1024 * 1024),
        cost_estimate=pl.CostEstimate(flops=1_700_000_000, bytes_accessed=5_000_000, transcendentals=0),
        name="forward",
    )(*[pltpu.with_memory_space_constraint(x, pltpu.HBM) for x in (shifts, weights, mask_clip, table)])


def add_kernel(own, one, two, three, out):
    out[...] = (
        own[...].astype(F32) + one[...].astype(F32) + two[...].astype(F32) + three[...].astype(F32)
    ).astype(BF16)


def finish_kernel(mine, other, out):
    total = mine[...].astype(F32) + other[...].astype(F32)
    cc, cs = total[:32, :HALF], total[:32, HALF:]
    sc, ss = total[32:64, :HALF], total[32:64, HALF:]
    out[:32, :HALF] = (cc - ss).astype(BF16)
    out[:32, HALF:] = (cc + ss).astype(BF16)
    out[32:64, :HALF] = -(sc + cs).astype(BF16)
    out[32:64, HALF:] = (cs - sc).astype(BF16)
    row = lax.broadcasted_iota(jnp.int32, (8, 256), 0)
    out[64:72] = jnp.where(row == 0, total[64:72], total[64:72] * 0.5).astype(BF16)


def small(kernel, name, *args):
    return pl.pallas_call(
        kernel,
        in_specs=[VMEM] * len(args),
        out_specs=VMEM,
        out_shape=jax.ShapeDtypeStruct((72, 256), BF16),
        compiler_params=pltpu.CompilerParams(vmem_limit_bytes=4 * 1024 * 1024),
        name=name,
    )(*args)


def inverse_kernel(c0, c1, c2, c3, left, right, spread, sine, out, spec, edge, fields):
    src_id = lax.axis_index("src")
    quarters = (c0, c1, c2, c3)
    for k, chunk in enumerate(quarters):
        q = lax.rem(src_id + 4 - k, 4)
        low = pl.ds(pl.multiple_of(q * 32, 32), 32)
        high = pl.ds(pl.multiple_of(HALF + q * 32, 32), 32)
        re, im = chunk[:32], chunk[32:64]
        spec[low, :256] = re
        spec[low, 256:] = im
        spec[high, :HALF] = re[:, HALF:]
        spec[high, HALF:256] = re[:, :HALF]
        spec[high, 256:384] = -im[:, HALF:]
        spec[high, 384:] = -im[:, :HALF]
        edge[pl.ds(q, 1)] = chunk[64:72].astype(F32)[0:1]
    rc, rs, xc, xs = (edge[i:i + 1] for i in range(4))
    first_row = jnp.concatenate(
        [
            rc[:, :HALF] + rs[:, HALF:],
            rc[:, :HALF] - rs[:, HALF:],
            rs[:, :HALF] - rc[:, HALF:],
            rs[:, :HALF] + rc[:, HALF:],
        ],
        1,
    )
    col_re = jnp.concatenate([xc[:, :HALF] + xs[:, HALF:], xc[:, :HALF] - xs[:, HALF:]], 1)
    col_im = jnp.concatenate([xs[:, :HALF] - xc[:, HALF:], xs[:, :HALF] + xc[:, HALF:]], 1)
    row = lax.broadcasted_iota(jnp.int32, (16, 512), 0)
    spec[HALF:HALF + 16] = jnp.where(
        row == 0, first_row, spec[HALF:HALF + 16].astype(F32)
    ).astype(BF16)
    first_lane = lax.broadcasted_iota(jnp.int32, (HALF, HALF), 1) == 0
    for i in range(2):
        rows = slice(i * HALF, (i + 1) * HALF)
        for line, lanes in ((col_re, slice(128, 256)), (col_im, slice(384, 512))):
            stood = jnp.broadcast_to(line[:, rows], (HALF, HALF)).T
            spec[rows, lanes] = jnp.where(first_lane, stood, spec[rows, lanes].astype(F32)).astype(BF16)

    f_low = lax.broadcasted_iota(jnp.int32, (HALF, HALF), 0)
    g_low = lax.broadcasted_iota(jnp.int32, (1, HALF), 1)
    f_halves = (f_low.astype(F32), jnp.where(f_low == 0, -HALF, -f_low).astype(F32))
    g_halves = (g_low.astype(F32), jnp.where(g_low == 0, -HALF, -g_low).astype(F32))
    g_all = jnp.concatenate(g_halves, 1)
    zero = jnp.zeros((HALF, HALF), BF16)
    ends = [jnp.zeros((1, 1), F32)]

    def propagate(s):
        info = quarters[s // 4][64:72].astype(F32)
        i = s % 4
        a, b = info[1 + i:2 + i, :HALF], info[1 + i:2 + i, HALF:]
        w = jnp.sqrt(info[5 + i // 2:6 + i // 2, (i % 2) * HALF:(i % 2 + 1) * HALF]) * 0.25
        room = [4096.0 - (f + a) * (f + a) for f in f_halves]
        reach = [(g + b) * (g + b) for g in g_halves]
        inside = [[r >= q for q in reach] for r in room]
        passed = jnp.concatenate(
            [
                jnp.concatenate(
                    [
                        jnp.where(
                            inside[i][j % 2],
                            spec[i * HALF:(i + 1) * HALF, j * HALF:(j + 1) * HALF],
                            zero,
                        )
                        for j in range(4)
                    ],
                    1,
                )
                for i in range(2)
            ],
            0,
        )
        blocks = jnp.dot(left[...], passed, preferred_element_type=F32)
        w2 = jnp.concatenate([w, w], 1)
        k_re = (blocks[:HALF, :256] - blocks[HALF:, 256:]) * w2
        k_im = (blocks[:HALF, 256:] + blocks[HALF:, :256]) * w2
        fields[s * HALF:(s + 1) * HALF, :256] = k_re.astype(BF16)
        fields[s * HALF:(s + 1) * HALF, 256:] = k_im.astype(BF16)
        at = g_all + jnp.concatenate([b, b], 1)
        r, m = k_re[0:1], k_im[0:1]
        pick = lambda x, v: jnp.sum(jnp.where(at == v, x, 0.0), axis=1, keepdims=True)
        ends[0] = ends[0] + pick(m, 64.0) * pick(r, -64.0) - pick(r, 64.0) * pick(m, -64.0)

    def power(group):
        k = fields[group * 512:(group + 1) * 512, :]
        e_re = jnp.dot(k, right[0], preferred_element_type=F32)
        e_im = jnp.dot(k, right[1], preferred_element_type=F32)
        p = e_re * e_re + e_im * e_im
        return (p[:HALF] + p[HALF:256]) + (p[256:384] + p[384:])

    summed = None
    for group in range(4):
        for s in range(4):
            propagate(group * 4 + s)
        if group:
            p = power(group - 1)
            summed = p if summed is None else summed + p
    summed = summed + power(3)
    high = summed.astype(BF16)
    low = (summed - high.astype(F32)).astype(BF16)
    tail = ends[0] * sine[0:1]
    out[...] = (
        jnp.dot(high, spread[0], preferred_element_type=F32)
        + jnp.dot(low, spread[0], preferred_element_type=F32)
        + jnp.dot(high, spread[1], preferred_element_type=F32)
        + tail
    )


def inverse(*args):
    return pl.pallas_call(
        inverse_kernel,
        in_specs=[VMEM] * len(args),
        out_specs=VMEM,
        out_shape=jax.ShapeDtypeStruct((HALF, NI), F32),
        scratch_shapes=[
            pltpu.VMEM((256, 512), BF16),
            pltpu.VMEM((8, 256), F32),
            pltpu.VMEM((2048, 512), BF16),
        ],
        compiler_params=pltpu.CompilerParams(vmem_limit_bytes=24 * 1024 * 1024),
        cost_estimate=pl.CostEstimate(flops=2_500_000_000, bytes_accessed=3_000_000, transcendentals=0),
        name="inverse",
    )(*args)


def place_rows(left, place):
    freq = jnp.arange(256, dtype=jnp.int32)
    freq = jnp.where(freq < HALF, freq, jnp.where(freq == HALF, -HALF, HALF - freq))
    eighths = freq * place
    cos_q, sin_q = (x.astype(BF16) for x in quarter(jnp.right_shift(eighths, 1)))
    base = jnp.where(jnp.bitwise_and(eighths, 1) == 1, left[1], left[0])
    return jnp.concatenate([base[0] * cos_q - base[1] * sin_q, base[1] * cos_q + base[0] * sin_q], 0)


def ring(x, k):
    return lax.ppermute(x, "src", [(i, (i + k) % 4) for i in range(4)])


def body(mask_clip, source_shifts, source_weights):
    table = forward_tables()
    left, right, spread, sine = inverse_tables()
    place = lax.axis_index("row") * 4 + lax.axis_index("src")
    left_mine = place_rows(jnp.asarray(left, BF16), place)
    parts = forward(mask_clip, source_shifts.T, source_weights, jnp.asarray(table, BF16))
    mine = small(add_kernel, "add", parts[0], *[ring(parts[k], k) for k in (1, 2, 3)])
    other = lax.ppermute(mine, "row", [(0, 1), (1, 0)])
    whole = small(finish_kernel, "finish", mine, other)
    return inverse(
        whole,
        *[ring(whole, k) for k in (1, 2, 3)],
        left_mine,
        jnp.asarray(right, BF16),
        jnp.asarray(spread, BF16),
        jnp.asarray(sine, F32),
    )


def solution(mesh):
    placed = (P(("clip", "row"), "src"), P("src", None), P("src"))
    return jax.shard_map(
        body, mesh=mesh, in_specs=placed, out_specs=P(("clip", "row", "src"), None), check_vma=False
    )
```

time: 178 us -> 35.5 us (0.20)
  blocking collectives: 66 us -> 0 us
  other arithmetic: 42.6 us -> 0.07 us
  waiting for transfers between devices: 27.1 us -> 9.01 us
  starting transfers between devices: 0.01 us -> 16.7 us
  matrix products: 14.5 us -> 0 us
  between operations: 13.5 us -> 0.09 us
  local copies, waits for them, and re-layouts: 9.76 us -> 0.02 us
  Pallas kernels: 0 us -> 9.52 us
  loops' own time: 2.82 us -> 0 us
    psum x1 -> x0, blocking collectives: 66 us -> none  [body(): spectrum = lax.psum(partial_value, ('row', 'src')).astype(jnp.bfloat16)]
    reduce_scatter x1 -> x0, waiting for transfers between devices: 27 us -> none  [body(): lax.psum_scatter(image_rows_sum(spectrum, image_rows, source_shifts, sour...]
    another operation x10 -> x0, other arithmetic: 26.7 us -> none
    ppermute x0 -> x7, starting transfers between devices: none -> 16.7 us  [the longest x6 9.41 us: ring(): return lax.ppermute(x, 'src', [(i, (i + k) % 4) for i in range(4)])]
    dot_general x9 -> x0, matrix products: 14.5 us -> none  [the longest x1 7.46 us: tile_spectrum(): blocks = jnp.dot(row_table, half_way, preferred_element_type=jnp.float32)]
    pallas_call x0 -> x4, Pallas kernels: none -> 9.52 us  [the longest x1 5.04 us: forward(): pl.pallas_call(forward_kernel, in_specs=[hbm] * 4, out_specs=[VMEM] * 4,...]
    ppermute x0 -> x7, waiting for transfers between devices: none -> 9.01 us  [the longest x6 7.05 us: ring(): return lax.ppermute(x, 'src', [(i, (i + k) % 4) for i in range(4)])]
    mul x8 -> x0, other arithmetic: 5.24 us -> none  [the longest x4 4.79 us: source_image(): along_cols[None, :] * along_cols[None, :]]
  transfers between devices with their start and end apart: 1 -> 7, of which waited for: 1 -> 5; matrix products, arithmetic and copies ran while one was open for 0% -> 0% of each run, Pallas kernels for 0% -> 0%
where the time goes in v2:
time: 35.5 us; the launch traced here: 35.4 us
  starting transfers between devices  16.7 us (47%)
  Pallas kernels  9.52 us (27%)
  waiting for transfers between devices  9.01 us (25%)
    ppermute x6, starting transfers between devices, ring(): return lax.ppermute(x, 'src', [(i, (i + k) % 4) for i in range(4)])  9.41 us
    ppermute x1, starting transfers between devices, body(): other = lax.ppermute(mine, 'row', [(0, 1), (1, 0)])  7.28 us
    ppermute x6, waiting for transfers between devices, ring(): return lax.ppermute(x, 'src', [(i, (i + k) % 4) for i in range(4)])  7.05 us
    pallas_call x1, Pallas kernels, forward(): pl.pallas_call(forward_kernel, in_specs=[hbm] * 4, out_specs=[VMEM] * 4,...  5.04 us
    pallas_call x1, Pallas kernels, inverse(): pl.pallas_call(inverse_kernel, in_specs=[VMEM] * len(args), out_specs=VME...  4.44 us
    ppermute x1, waiting for transfers between devices, body(): other = lax.ppermute(mine, 'row', [(0, 1), (1, 0)])  1.96 us
  transfers between devices with their start and end apart: 7, of which 5 were waited for; matrix products, arithmetic and copies ran while one was open for 0% of the time, Pallas kernels for 0%

profile of v2, /device:TPU:8, one launch (start us, length us, event | category | flops | bytes accessed | tf_op | source)
XLA Modules:
  0.0 35.4 jit_solution(9150524939639399002)
XLA Ops:
  0.0 0.0 copy-start.3
  0.0 0.0 copy-start.4
  0.0 0.0 copy-start.2
  0.0 0.0 copy-start
  0.0 0.0 copy-start.1
  0.0 5.0 %forward.1 = (bf16[72,256]{1,0:T(8,128)(2,1)S(1)}, bf16[72,256]{1,0:T(8,128)(2,1)S(1)}, bf16[72,256]{1,0:T(8,128)(2,1)S(1)}, bf16[72,256]{1,0:T(8,128)(2,1)S(1)}) custom-call(s32[2,4]{1,0:T(2,128)} %bitcast.13, s32[4]{0:T(128)} %weights_in.1, bf16[2048,1024]{1,0:T(8,128)(2,1)} %mask.1, bf16[272,1024]{1,0:T(8,128)(2,1)} %constant.40.clone.table_in), custom_call_target="tpu_custom_call" | custom-call | flops 1700000000 | bytes 5000000 | tf_op jit(solution)/shard_map/forward/pallas_call | solution.py:159
  5.1 1.6 %collective-permute-start = (bf16[72,256]{1,0:T(8,128)(2,1)S(1)}, bf16[72,256]{1,0:T(8,128)(2,1)S(1)}, u32[]{:S(2)}, u32[]{:S(2)}) collective-permute-start(bf16[72,256]{1,0:T(8,128)(2,1)S(1)} %get-tuple-element.10), channel_id=1, source_target_pairs={{0,1},{1,2},{2,3},{3,0},{4,5},{5,6},{6,7},{7,4},{8,9},{9,10},{10,1... | collective-permute-start | bytes 110600 | tf_op jit(solution)/shard_map/ppermute | solution.py:345
  6.7 2.7 %collective-permute-start.1 = (bf16[72,256]{1,0:T(8,128)(2,1)S(1)}, bf16[72,256]{1,0:T(8,128)(2,1)S(1)}, u32[]{:S(2)}, u32[]{:S(2)}) collective-permute-start(bf16[72,256]{1,0:T(8,128)(2,1)S(1)} %get-tuple-element.11), channel_id=1, source_target_pairs={{0,2},{1,3},{2,0},{3,1},{4,6},{5,7},{6,4},{7,5},{8,10},{9,11},{10,... | collective-permute-start | bytes 110600 | tf_op jit(solution)/shard_map/ppermute | solution.py:345
  9.4 1.4 %collective-permute-start.2 = (bf16[72,256]{1,0:T(8,128)(2,1)S(1)}, bf16[72,256]{1,0:T(8,128)(2,1)S(1)}, u32[]{:S(2)}, u32[]{:S(2)}) collective-permute-start(bf16[72,256]{1,0:T(8,128)(2,1)S(1)} %get-tuple-element.12), channel_id=1, source_target_pairs={{0,3},{1,0},{2,1},{3,2},{4,7},{5,4},{6,5},{7,6},{8,11},{9,8},{10,9... | collective-permute-start | bytes 110600 | tf_op jit(solution)/shard_map/ppermute | solution.py:345
  10.8 0.0 copy-done.3
  10.8 0.0 copy-done.4
  10.9 0.0 collective-permute-done.one
  10.9 1.2 %collective-permute-done.1.two = bf16[72,256]{1,0:T(8,128)(2,1)S(1)} collective-permute-done((bf16[72,256]{1,0:T(8,128)(2,1)S(1)}, bf16[72,256]{1,0:T(8,128)(2,1)S(1)}, u32[]{:S(2)}, u32[]{:S(2)}) %collective-permute-start.1) | collective-permute-done | bytes 36896 | tf_op jit(solution)/shard_map/ppermute | solution.py:345
  12.1 1.2 %collective-permute-done.2.three = bf16[72,256]{1,0:T(8,128)(2,1)S(1)} collective-permute-done((bf16[72,256]{1,0:T(8,128)(2,1)S(1)}, bf16[72,256]{1,0:T(8,128)(2,1)S(1)}, u32[]{:S(2)}, u32[]{:S(2)}) %collective-permute-start.2) | collective-permute-done | bytes 36896 | tf_op jit(solution)/shard_map/ppermute | solution.py:345
  13.4 7.3 %collective-permute-start.3 = (bf16[72,256]{1,0:T(8,128)(2,1)S(1)}, bf16[72,256]{1,0:T(8,128)(2,1)S(1)}, u32[]{:S(2)}, u32[]{:S(2)}) collective-permute-start(bf16[72,256]{1,0:T(8,128)(2,1)S(1)} %add.10.mine), channel_id=1, source_target_pairs={{0,4},{4,0},{1,5},{5,1},{2,6},{6,2},{3,7},{7,3},{8,12},{12,8},{9,1... | collective-permute-start | bytes 110600 | tf_op jit(solution)/shard_map/ppermute | solution.py:355
  20.7 2.0 %collective-permute-done.3.other = bf16[72,256]{1,0:T(8,128)(2,1)S(1)} collective-permute-done((bf16[72,256]{1,0:T(8,128)(2,1)S(1)}, bf16[72,256]{1,0:T(8,128)(2,1)S(1)}, u32[]{:S(2)}, u32[]{:S(2)}) %collective-permute-start.3) | collective-permute-done | bytes 36896 | tf_op jit(solution)/shard_map/ppermute | solution.py:355
  22.6 2.7 %collective-permute-start.6 = (bf16[72,256]{1,0:T(8,128)(2,1)S(1)}, bf16[72,256]{1,0:T(8,128)(2,1)S(1)}, u32[]{:S(2)}, u32[]{:S(2)}) collective-permute-start(bf16[72,256]{1,0:T(8,128)(2,1)S(1)} %finish.1.c0), channel_id=1, source_target_pairs={{0,3},{1,0},{2,1},{3,2},{4,7},{5,4},{6,5},{7,6},{8,11},{9,8},{10,9... | collective-permute-start | bytes 110600 | tf_op jit(solution)/shard_map/ppermute | solution.py:345
  25.4 0.0 collective-permute-start.5
  25.4 1.0 %collective-permute-start.4 = (bf16[72,256]{1,0:T(8,128)(2,1)S(1)}, bf16[72,256]{1,0:T(8,128)(2,1)S(1)}, u32[]{:S(2)}, u32[]{:S(2)}) collective-permute-start(bf16[72,256]{1,0:T(8,128)(2,1)S(1)} %finish.1.c0), channel_id=1, source_target_pairs={{0,1},{1,2},{2,3},{3,0},{4,5},{5,6},{6,7},{7,4},{8,9},{9,10},{10,1... | collective-permute-start | bytes 110600 | tf_op jit(solution)/shard_map/ppermute | solution.py:345
  26.3 0.7 %collective-permute-done.6.c3 = bf16[72,256]{1,0:T(8,128)(2,1)S(1)} collective-permute-done((bf16[72,256]{1,0:T(8,128)(2,1)S(1)}, bf16[72,256]{1,0:T(8,128)(2,1)S(1)}, u32[]{:S(2)}, u32[]{:S(2)}) %collective-permute-start.6) | collective-permute-done | bytes 36896 | tf_op jit(solution)/shard_map/ppermute | solution.py:345
  27.0 3.9 %collective-permute-done.5.c2 = bf16[72,256]{1,0:T(8,128)(2,1)S(1)} collective-permute-done((bf16[72,256]{1,0:T(8,128)(2,1)S(1)}, bf16[72,256]{1,0:T(8,128)(2,1)S(1)}, u32[]{:S(2)}, u32[]{:S(2)}) %collective-permute-start.5) | collective-permute-done | bytes 36896 | tf_op jit(solution)/shard_map/ppermute | solution.py:345
  30.9 0.0 collective-permute-done.4.c1
  30.9 0.0 copy-done.2
  30.9 0.0 copy-done
  30.9 0.0 copy-done.1
  30.9 4.4 %inverse.1 = f32[128,1024]{1,0:T(8,128)} custom-call(bf16[72,256]{1,0:T(8,128)(2,1)S(1)} %finish.1.c0, bf16[72,256]{1,0:T(8,128)(2,1)S(1)} %collective-permute-done.4.c1, bf16[72,256]{1,0:T(8,128)(2,1)S(1)} %collective-permute-done.5.c2, bf16[72,256]{1,0:T(8,128)(2,1)S(1)} %collective-permute-done.6.c3, bf16[256,256]{1,0:T(8,128)(2,1)S(1)} %pad_maximum_fusion.left, ...), custom_call_target="tpu_custom_call" | custom-call | flops 2500000000 | bytes 3000000 | tf_op jit(solution)/shard_map/inverse/pallas_call | solution.py:319
  (7 shorter events, 0.1 us)
Async XLA Ops:
  0.0 10.8 %copy-start.3 = (bf16[2,128,256]{2,1,0:T(8,128)(2,1)S(1)}, bf16[2,128,256]{2,1,0:T(8,128)(2,1)}, u32[]{:S(2)}) copy-start(bf16[2,128,256]{2,1,0:T(8,128)(2,1)} %constant.47) | copy-start | bytes 393220
  0.0 10.8 %copy-start.4 = (bf16[2,128,256]{2,1,0:T(8,128)(2,1)S(1)}, bf16[2,128,256]{2,1,0:T(8,128)(2,1)}, u32[]{:S(2)}) copy-start(bf16[2,128,256]{2,1,0:T(8,128)(2,1)} %constant.45) | copy-start | bytes 393220
  0.0 30.9 %copy-start.2 = (f32[8,1024]{1,0:T(8,128)S(1)}, f32[8,1024]{1,0:T(8,128)}, u32[]{:S(2)}) copy-start(f32[8,1024]{1,0:T(8,128)} %constant.43.clone.sine) | copy-start | bytes 98308
  0.0 30.9 %copy-start = (bf16[2,256,1024]{2,1,0:T(8,128)(2,1)S(1)}, bf16[2,256,1024]{2,1,0:T(8,128)(2,1)}, u32[]{:S(2)}) copy-start(bf16[2,256,1024]{2,1,0:T(8,128)(2,1)} %constant.42.clone.spread) | copy-start | bytes 3145732
  0.0 30.9 %copy-start.1 = (bf16[2,512,256]{2,1,0:T(8,128)(2,1)S(1)}, bf16[2,512,256]{2,1,0:T(8,128)(2,1)}, u32[]{:S(2)}) copy-start(bf16[2,512,256]{2,1,0:T(8,128)(2,1)} %constant.41.clone.right) | copy-start | bytes 1572868
  5.1 5.8 %collective-permute-start = (bf16[72,256]{1,0:T(8,128)(2,1)S(1)}, bf16[72,256]{1,0:T(8,128)(2,1)S(1)}, u32[]{:S(2)}, u32[]{:S(2)}) collective-permute-start(bf16[72,256]{1,0:T(8,128)(2,1)S(1)} %get-tuple-element.10), channel_id=1, source_target_pairs={{0,1},{1,2},{2,3},{3,0},{4,5},{5,6},{6,7},{7,4},{8,9},{9,10},{10,1... | collective-permute-start | bytes 110600 | tf_op jit(solution)/shard_map/ppermute | solution.py:345
  6.7 5.5 %collective-permute-start.1 = (bf16[72,256]{1,0:T(8,128)(2,1)S(1)}, bf16[72,256]{1,0:T(8,128)(2,1)S(1)}, u32[]{:S(2)}, u32[]{:S(2)}) collective-permute-start(bf16[72,256]{1,0:T(8,128)(2,1)S(1)} %get-tuple-element.11), channel_id=1, source_target_pairs={{0,2},{1,3},{2,0},{3,1},{4,6},{5,7},{6,4},{7,5},{8,10},{9,11},{10,... | collective-permute-start | bytes 110600 | tf_op jit(solution)/shard_map/ppermute | solution.py:345
  9.4 4.0 %collective-permute-start.2 = (bf16[72,256]{1,0:T(8,128)(2,1)S(1)}, bf16[72,256]{1,0:T(8,128)(2,1)S(1)}, u32[]{:S(2)}, u32[]{:S(2)}) collective-permute-start(bf16[72,256]{1,0:T(8,128)(2,1)S(1)} %get-tuple-element.12), channel_id=1, source_target_pairs={{0,3},{1,0},{2,1},{3,2},{4,7},{5,4},{6,5},{7,6},{8,11},{9,8},{10,9... | collective-permute-start | bytes 110600 | tf_op jit(solution)/shard_map/ppermute | solution.py:345
  13.4 9.3 %collective-permute-start.3 = (bf16[72,256]{1,0:T(8,128)(2,1)S(1)}, bf16[72,256]{1,0:T(8,128)(2,1)S(1)}, u32[]{:S(2)}, u32[]{:S(2)}) collective-permute-start(bf16[72,256]{1,0:T(8,128)(2,1)S(1)} %add.10.mine), channel_id=1, source_target_pairs={{0,4},{4,0},{1,5},{5,1},{2,6},{6,2},{3,7},{7,3},{8,12},{12,8},{9,1... | collective-permute-start | bytes 110600 | tf_op jit(solution)/shard_map/ppermute | solution.py:355
  22.6 4.4 %collective-permute-start.6 = (bf16[72,256]{1,0:T(8,128)(2,1)S(1)}, bf16[72,256]{1,0:T(8,128)(2,1)S(1)}, u32[]{:S(2)}, u32[]{:S(2)}) collective-permute-start(bf16[72,256]{1,0:T(8,128)(2,1)S(1)} %finish.1.c0), channel_id=1, source_target_pairs={{0,3},{1,0},{2,1},{3,2},{4,7},{5,4},{6,5},{7,6},{8,11},{9,8},{10,9... | collective-permute-start | bytes 110600 | tf_op jit(solution)/shard_map/ppermute | solution.py:345
  25.4 5.6 %collective-permute-start.5 = (bf16[72,256]{1,0:T(8,128)(2,1)S(1)}, bf16[72,256]{1,0:T(8,128)(2,1)S(1)}, u32[]{:S(2)}, u32[]{:S(2)}) collective-permute-start(bf16[72,256]{1,0:T(8,128)(2,1)S(1)} %finish.1.c0), channel_id=1, source_target_pairs={{0,2},{1,3},{2,0},{3,1},{4,6},{5,7},{6,4},{7,5},{8,10},{9,11},{10,... | collective-permute-start | bytes 110600 | tf_op jit(solution)/shard_map/ppermute | solution.py:345
  25.4 5.6 %collective-permute-start.4 = (bf16[72,256]{1,0:T(8,128)(2,1)S(1)}, bf16[72,256]{1,0:T(8,128)(2,1)S(1)}, u32[]{:S(2)}, u32[]{:S(2)}) collective-permute-start(bf16[72,256]{1,0:T(8,128)(2,1)S(1)} %finish.1.c0), channel_id=1, source_target_pairs={{0,1},{1,2},{2,3},{3,0},{4,5},{5,6},{6,7},{7,4},{8,9},{9,10},{10,1... | collective-permute-start | bytes 110600 | tf_op jit(solution)/shard_map/ppermute | solution.py:345

commit v3 on v2

v3 whole, which is shorter than its diff:
```python
import jax
import jax.numpy as jnp
import numpy as np
from jax import lax
from jax.experimental import pallas as pl
from jax.experimental.pallas import tpu as pltpu
from jax.sharding import PartitionSpec as P

NM = 4096
NI = 1024
TILE = NM // 4
HALF = 128
CHUNKS = ((0, 512), (512, 1024), (1024, 1536), (1536, 2048))
SENT = 272
SUMMED = 264
COARSE = 256
NT = (((1,), (1,)), ((), ()))
F32 = jnp.float32
BF16 = jnp.bfloat16
VMEM = pl.BlockSpec(memory_space=pltpu.VMEM)


def forward_tables():
    freq = np.arange(HALF)
    pos = np.arange(TILE)
    angle = 2.0 * np.pi * ((freq[:, None] * pos[None, :]) % NM) / NM
    edge = 2.0 * np.pi * ((HALF * pos) % NM) / NM
    table = np.zeros((272, TILE), np.float64)
    table[:HALF] = np.cos(angle)
    table[HALF:256] = np.sin(angle)
    table[256] = np.cos(edge)
    table[257] = np.sin(edge)
    table[266, :HALF] = np.cos(edge[:HALF])
    table[267, :HALF] = np.sin(edge[:HALF])
    return (table / 64).astype(np.float32)


def inverse_tables():
    freq = np.concatenate([np.arange(HALF), -np.arange(HALF)])
    freq[HALF] = -HALF
    rows = np.arange(NI)
    angle = 2.0 * np.pi * ((rows[:, None] * freq[None, :]) % NI) / NI
    left = [np.stack([np.cos(angle[:HALF] + t), np.sin(angle[:HALF] + t)]) / 16 for t in (0.0, np.pi / 4)]
    left = np.stack(left)
    cos_y, sin_y = np.cos(angle[::4]).T / 64, np.sin(angle[::4]).T / 64
    right = np.stack([np.concatenate([cos_y, -sin_y], 0), np.concatenate([sin_y, cos_y], 0)])
    j = np.arange(COARSE)
    harmonic = np.arange(1, HALF)
    columns = np.arange(NI)
    distance = (columns[None, :] - 4 * j[:, None]) % NI
    lags = 2.0 * np.pi * ((np.arange(NI)[:, None] * harmonic[None, :]) % NI) / NI
    wave = (1.0 + 2.0 * np.cos(lags).sum(1) + np.cos(2.0 * np.pi * (np.arange(NI) * HALF % NI) / NI)) / COARSE
    spread = wave[distance]
    high = np.asarray(spread.astype(np.float32).astype(BF16), np.float64)
    spread = np.stack([high, spread - high])
    sine = np.zeros((8, NI), np.float64)
    sine[0] = -2.0 * np.sin(np.pi * (columns % 8) / 4) / 4096
    return tuple(x.astype(np.float32) for x in (left, right, spread, sine))


def quarter(turns):
    q = jnp.bitwise_and(turns, 3)
    cos_q = jnp.where(q == 0, 1.0, jnp.where(q == 2, -1.0, 0.0)).astype(F32)
    sin_q = jnp.where(q == 1, 1.0, jnp.where(q == 3, -1.0, 0.0)).astype(F32)
    return cos_q, sin_q


def forward_kernel(shifts_in, weights_in, mask, table_in, out,
                   shifts, weights, block, table, half_way, folded, sem):
    small_copies = [
        pltpu.make_async_copy(table_in, table, sem.at[0]),
        pltpu.make_async_copy(shifts_in, shifts, sem.at[1]),
        pltpu.make_async_copy(weights_in, weights, sem.at[2]),
    ]
    copies = [
        pltpu.make_async_copy(mask.at[start:stop], block.at[start:stop], sem.at[3 + i])
        for i, (start, stop) in enumerate(CHUNKS)
    ]
    for copy in (small_copies[0], *copies, *small_copies[1:]):
        copy.start()
    row_id = lax.axis_index("row")
    src_id = lax.axis_index("src")
    f_col = lax.broadcasted_iota(jnp.int32, (HALF, 256), 0)
    cos_f, sin_f = quarter(f_col)
    sign, _ = quarter(f_col * 2 * row_id)
    cos_g, sin_g = quarter(lax.broadcasted_iota(jnp.int32, (HALF, HALF), 1) * src_id)

    def join_rows(a, b):
        top = (a[:HALF] + cos_f * b[:HALF] - sin_f * b[HALF:256]) * sign
        low = (a[HALF:256] + cos_f * b[HALF:256] + sin_f * b[:HALF]) * sign
        return top, low

    def turn_columns(x):
        c, s = cos_g[:x.shape[0]], sin_g[:x.shape[0]]
        return c * x[:, :HALF] - s * x[:, HALF:], c * x[:, HALF:] + s * x[:, :HALF]

    small_copies[0].wait()
    sums = []
    for copy, (start, stop) in zip(copies, CHUNKS):
        copy.wait()
        part, at = start // TILE, start % TILE
        half_way[start:stop] = lax.dot_general(
            block[start:stop], table[:256, :], NT, preferred_element_type=F32
        ).astype(BF16)
        for low in range(0, stop - start, 64):
            rows = slice(start + low, start + low + 64)
            tiles = [block[rows, tile * HALF:(tile + 1) * HALF] for tile in range(8)]
            while len(tiles) > 1:
                tiles = [tiles[t] + tiles[t + 1] for t in range(0, len(tiles), 2)]
            folded[at + low:at + low + 64, part * HALF:(part + 1) * HALF] = tiles[0]
        if start == TILE:
            sums.append(jnp.dot(table[:264], half_way[:TILE], preferred_element_type=F32))
    sums.append(jnp.dot(table[:264], half_way[TILE:], preferred_element_type=F32))
    sides = jnp.dot(table[:256, :], folded[...], preferred_element_type=F32)
    for copy in small_copies[1:]:
        copy.wait()
    a, b = sums
    for start, x in zip((0, HALF), join_rows(a, b)):
        x_cos, x_sin = turn_columns(x)
        out[start:start + HALF, :HALF] = x_cos.astype(BF16)
        out[start:start + HALF, HALF:] = x_sin.astype(BF16)
    e_cos, e_sin = turn_columns(a[256:] + b[256:])
    s_a, s_b = sides[:, :HALF], sides[:, HALF:]
    c, s, g = cos_f[:, :HALF], sin_f[:, :HALF], sign[:, :HALF]
    edges = jnp.concatenate(
        [
            (s_a[:HALF] + c * s_b[:HALF] - s * s_b[HALF:]) * g,
            (s_a[HALF:] + c * s_b[HALF:] + s * s_b[:HALF]) * g,
        ],
        0,
    ).astype(BF16)
    crossed = lax.dot_general(table[264:272, :HALF], edges, NT, preferred_element_type=F32)
    pad = jnp.zeros((8, HALF), F32)
    first = jnp.concatenate([e_cos + crossed[:, :HALF], pad], 0)
    second = jnp.concatenate([e_sin + crossed[:, HALF:], pad], 0)
    row = lax.broadcasted_iota(jnp.int32, (16, HALF), 0)
    for i in range(4):
        first = jnp.where(row == 4 + i, shifts[0, i].astype(F32), first)
        second = jnp.where(row == 4 + i, shifts[1, i].astype(F32), second)
        w = weights[i].astype(F32)
        if i % 2 == 0:
            first = jnp.where(row == 8 + i // 2, w, first)
        else:
            second = jnp.where(row == 8 + i // 2, w, second)
    out[256:SENT, :HALF] = first.astype(BF16)
    out[256:SENT, HALF:] = second.astype(BF16)


def forward(mask_clip, shifts, weights, table):
    hbm = pl.BlockSpec(memory_space=pltpu.HBM)
    return pl.pallas_call(
        forward_kernel,
        in_specs=[hbm] * 4,
        out_specs=VMEM,
        out_shape=jax.ShapeDtypeStruct((SENT, 256), BF16),
        scratch_shapes=[
            pltpu.SMEM((2, 4), jnp.int32),
            pltpu.SMEM((4,), jnp.int32),
            pltpu.VMEM((2 * TILE, TILE), BF16),
            pltpu.VMEM((272, TILE), BF16),
            pltpu.VMEM((2 * TILE, 256), BF16),
            pltpu.VMEM((TILE, 256), BF16),
            pltpu.SemaphoreType.DMA((3 + len(CHUNKS),)),
        ],
        compiler_params=pltpu.CompilerParams(vmem_limit_bytes=16 * 1024 * 1024),
        cost_estimate=pl.CostEstimate(flops=1_700_000_000, bytes_accessed=5_000_000, transcendentals=0),
        name="forward",
    )(*[pltpu.with_memory_space_constraint(x, pltpu.HBM) for x in (shifts, weights, mask_clip, table)])


def add_kernel(own, one, two, three, out):
    out[...] = (
        own[:SUMMED].astype(F32) + one[:SUMMED].astype(F32)
        + two[:SUMMED].astype(F32) + three[:SUMMED].astype(F32)
    ).astype(BF16)


def add(*args):
    return pl.pallas_call(
        add_kernel,
        in_specs=[VMEM] * 4,
        out_specs=VMEM,
        out_shape=jax.ShapeDtypeStruct((SUMMED, 256), BF16),
        compiler_params=pltpu.CompilerParams(vmem_limit_bytes=4 * 1024 * 1024),
        name="add",
    )(*args)


def pupil_kernel(c0, c1, c2, c3, out):
    f_low = lax.broadcasted_iota(jnp.int32, (HALF, HALF), 0)
    g_low = lax.broadcasted_iota(jnp.int32, (1, HALF), 1)
    f_halves = (f_low.astype(F32), jnp.where(f_low == 0, -HALF, -f_low).astype(F32))
    g_halves = (g_low.astype(F32), jnp.where(g_low == 0, -HALF, -g_low).astype(F32))
    for s in range(16):
        info = (c0, c1, c2, c3)[s // 4][256:SENT].astype(F32)
        i = 4 + s % 4
        a, b = info[i:i + 1, :HALF], info[i:i + 1, HALF:]
        for i, f in enumerate(f_halves):
            room = 4096.0 - (f + a) * (f + a)
            for j, g in enumerate(g_halves):
                reach = (g + b) * (g + b)
                out[s, i * HALF:(i + 1) * HALF, j * HALF:(j + 1) * HALF] = jnp.where(
                    room >= reach, 1.0, 0.0
                ).astype(BF16)


def pupils(*args):
    return pl.pallas_call(
        pupil_kernel,
        in_specs=[VMEM] * 4,
        out_specs=VMEM,
        out_shape=jax.ShapeDtypeStruct((16, 256, 256), BF16),
        compiler_params=pltpu.CompilerParams(vmem_limit_bytes=8 * 1024 * 1024),
        cost_estimate=pl.CostEstimate(flops=10_000_000, bytes_accessed=2_000_000, transcendentals=0),
        name="pupils",
    )(*args)


def inverse_kernel(mine, other, c0, c1, c2, c3, pupil, left, right, spread, sine, out, spec, fields):
    total = mine[:256].astype(F32) + other[:256].astype(F32)
    cc, cs = total[:HALF, :HALF], total[:HALF, HALF:]
    sc, ss = total[HALF:, :HALF], total[HALF:, HALF:]
    edge = mine[256:SUMMED].astype(F32) + other[256:SUMMED].astype(F32)
    rc, rs, xc, xs = (edge[i:i + 1] for i in range(4))
    row_re = (rc[:, :HALF] + rs[:, HALF:], rc[:, :HALF] - rs[:, HALF:])
    row_im = (rs[:, :HALF] - rc[:, HALF:], rs[:, :HALF] + rc[:, HALF:])
    col_re = (xc[:, :HALF] + xs[:, HALF:], xc[:, :HALF] - xs[:, HALF:])
    col_im = (xs[:, :HALF] - xc[:, HALF:], xs[:, :HALF] + xc[:, HALF:])
    first_row = lax.broadcasted_iota(jnp.int32, (HALF, HALF), 0) == 0
    first_lane = lax.broadcasted_iota(jnp.int32, (HALF, HALF), 1) == 0
    quads = {
        (0, 0): (cc - ss, -(sc + cs)),
        (0, 1): (cc + ss, cs - sc),
        (1, 0): (cc + ss, sc - cs),
        (1, 1): (cc - ss, sc + cs),
    }
    for (i, j), parts in quads.items():
        for at, x, row, col in zip((0, 256), parts, (row_re, row_im), (col_re, col_im)):
            if i == 1:
                x = jnp.where(first_row, row[j], x)
            if j == 1:
                x = jnp.where(first_lane, jnp.broadcast_to(col[i], (HALF, HALF)).T, x)
            spec[at + i * HALF:at + (i + 1) * HALF, j * HALF:(j + 1) * HALF] = x.astype(BF16)

    g_low = lax.broadcasted_iota(jnp.int32, (1, HALF), 1)
    g_all = jnp.concatenate([g_low, jnp.where(g_low == 0, -HALF, -g_low)], 1).astype(F32)
    infos = [c[256:SENT].astype(F32) for c in (c0, c1, c2, c3)]
    ends = [jnp.zeros((1, 1), F32)]

    def weight(s):
        i = s % 4
        return infos[s // 4][8 + i // 2:9 + i // 2, (i % 2) * HALF:(i % 2 + 1) * HALF]

    def propagate(s):
        passed = jnp.concatenate([spec[:256] * pupil[s], spec[256:] * pupil[s]], 0)
        k = jnp.dot(left[...], passed, preferred_element_type=F32)
        fields[s * HALF:(s + 1) * HALF, :256] = k[:HALF].astype(BF16)
        fields[s * HALF:(s + 1) * HALF, 256:] = k[HALF:].astype(BF16)
        b = infos[s // 4][4 + s % 4:5 + s % 4, HALF:]
        at = g_all + jnp.concatenate([b, b], 1)
        r, m = k[0:1], k[HALF:HALF + 1]
        pick = lambda x, v: jnp.sum(jnp.where(at == v, x, 0.0), axis=1, keepdims=True)
        z = pick(m, 64.0) * pick(r, -64.0) - pick(r, 64.0) * pick(m, -64.0)
        ends[0] = ends[0] + weight(s)[:, :1] * z

    def power(group):
        k = fields[group * 512:(group + 1) * 512, :]
        e_re = jnp.dot(k, right[0], preferred_element_type=F32)
        e_im = jnp.dot(k, right[1], preferred_element_type=F32)
        p = e_re * e_re + e_im * e_im
        parts = []
        for i in range(4):
            w = weight(group * 4 + i)
            parts.append(p[i * HALF:(i + 1) * HALF] * jnp.concatenate([w, w], 1))
        return (parts[0] + parts[1]) + (parts[2] + parts[3])

    summed = None
    for group in range(4):
        for s in range(4):
            propagate(group * 4 + s)
        if group:
            p = power(group - 1)
            summed = p if summed is None else summed + p
    summed = summed + power(3)
    high = summed.astype(BF16)
    low = (summed - high.astype(F32)).astype(BF16)
    tail = ends[0] * sine[0:1]
    out[...] = (
        jnp.dot(high, spread[0], preferred_element_type=F32)
        + jnp.dot(low, spread[0], preferred_element_type=F32)
        + jnp.dot(high, spread[1], preferred_element_type=F32)
        + tail
    )


def inverse(*args):
    return pl.pallas_call(
        inverse_kernel,
        in_specs=[VMEM] * len(args),
        out_specs=VMEM,
        out_shape=jax.ShapeDtypeStruct((HALF, NI), F32),
        scratch_shapes=[
            pltpu.VMEM((512, 256), BF16),
            pltpu.VMEM((2048, 512), BF16),
        ],
        compiler_params=pltpu.CompilerParams(vmem_limit_bytes=24 * 1024 * 1024),
        cost_estimate=pl.CostEstimate(flops=2_500_000_000, bytes_accessed=3_000_000, transcendentals=0),
        name="inverse",
    )(*args)


def place_rows(left, place):
    freq = jnp.arange(256, dtype=jnp.int32)
    freq = jnp.where(freq < HALF, freq, jnp.where(freq == HALF, -HALF, HALF - freq))
    eighths = freq * place
    cos_q, sin_q = (x.astype(BF16) for x in quarter(jnp.right_shift(eighths, 1)))
    base = jnp.where(jnp.bitwise_and(eighths, 1) == 1, left[1], left[0])
    c, s = base[0] * cos_q - base[1] * sin_q, base[1] * cos_q + base[0] * sin_q
    return jnp.concatenate([jnp.concatenate([c, -s], 1), jnp.concatenate([s, c], 1)], 0)


def ring(x, k):
    return lax.ppermute(x, "src", [(i, (i + k) % 4) for i in range(4)])


def body(mask_clip, source_shifts, source_weights):
    table = forward_tables()
    left, right, spread, sine = inverse_tables()
    place = lax.axis_index("row") * 4 + lax.axis_index("src")
    left_mine = place_rows(jnp.asarray(left, BF16), place)
    own = forward(mask_clip, source_shifts.T, source_weights, jnp.asarray(table, BF16))
    parts = [own] + [ring(own, k) for k in (2, 1, 3)]
    mine = add(*parts)
    other = lax.ppermute(mine, "row", [(0, 1), (1, 0)])
    return inverse(
        mine,
        other,
        *parts,
        pupils(*parts),
        left_mine,
        jnp.asarray(right, BF16),
        jnp.asarray(spread, BF16),
        jnp.asarray(sine, F32),
    )


def solution(mesh):
    placed = (P(("clip", "row"), "src"), P("src", None), P("src"))
    return jax.shard_map(
        body, mesh=mesh, in_specs=placed, out_specs=P(("clip", "row", "src"), None), check_vma=False
    )
```

time: 35.5 us -> 32.8 us (0.924)
  starting transfers between devices: 16.7 us -> 12.4 us
  waiting for transfers between devices: 9.01 us -> 10.3 us
    ppermute x6 -> x3, starting transfers between devices: 9.41 us -> 5.13 us  [ring(): return lax.ppermute(x, 'src', [(i, (i + k) % 4) for i in range(4)])]
    ppermute x1, waiting for transfers between devices: 1.96 us -> 3.29 us  [body(): other = lax.ppermute(mine, 'row', [(0, 1), (1, 0)])]
    pallas_call x3, Pallas kernels: 5.08 us -> 6.06 us  [the longest x1 5.26 us: forward(): pl.pallas_call(forward_kernel, in_specs=[hbm] * 4, out_specs=VMEM, out_sh...]
    pallas_call x1, Pallas kernels: 4.44 us -> 3.78 us  [inverse(): pl.pallas_call(inverse_kernel, in_specs=[VMEM] * len(args), out_specs=VME...]
    ppermute x6 -> x3, waiting for transfers between devices: 7.05 us -> 6.97 us  [ring(): return lax.ppermute(x, 'src', [(i, (i + k) % 4) for i in range(4)])]
  transfers between devices with their start and end apart: 7 -> 4, of which waited for: 5 -> 3; matrix products, arithmetic and copies ran while one was open for 0% -> 0% of each run, Pallas kernels for 0% -> 2%
where the time goes in v3:
time: 32.8 us; the launch traced here: 32.7 us
  starting transfers between devices  12.4 us (38%)
  waiting for transfers between devices  10.3 us (31%)
  Pallas kernels  9.85 us (30%)
    ppermute x1, starting transfers between devices, body(): other = lax.ppermute(mine, 'row', [(0, 1), (1, 0)])  7.28 us
    ppermute x3, waiting for transfers between devices, ring(): return lax.ppermute(x, 'src', [(i, (i + k) % 4) for i in range(4)])  6.97 us
    pallas_call x1, Pallas kernels, forward(): pl.pallas_call(forward_kernel, in_specs=[hbm] * 4, out_specs=VMEM, out_sh...  5.26 us
    ppermute x3, starting transfers between devices, ring(): return lax.ppermute(x, 'src', [(i, (i + k) % 4) for i in range(4)])  5.13 us
    pallas_call x1, Pallas kernels, inverse(): pl.pallas_call(inverse_kernel, in_specs=[VMEM] * len(args), out_specs=VME...  3.78 us
    ppermute x1, waiting for transfers between devices, body(): other = lax.ppermute(mine, 'row', [(0, 1), (1, 0)])  3.29 us
    pallas_call x1, Pallas kernels, pupils(): pl.pallas_call(pupil_kernel, in_specs=[VMEM] * 4, out_specs=VMEM, out_sha...  0.74 us
  transfers between devices with their start and end apart: 4, of which 3 were waited for; matrix products, arithmetic and copies ran while one was open for 0% of the time, Pallas kernels for 2%

profile of v3, /device:TPU:8, one launch (start us, length us, event | category | flops | bytes accessed | tf_op | source)
XLA Modules:
  0.0 32.7 jit_solution(1256748290051745688)
XLA Ops:
  0.0 0.0 copy-start.3
  0.0 0.0 copy-start.4
  0.0 0.0 copy-start
  0.0 0.0 copy-start.1
  0.0 0.0 copy-start.2
  0.0 5.3 %forward.1.own.c0 = bf16[272,256]{1,0:T(8,128)(2,1)S(1)} custom-call(s32[2,4]{1,0:T(2,128)} %bitcast.15, s32[4]{0:T(128)} %weights_in.1, bf16[2048,1024]{1,0:T(8,128)(2,1)} %mask.1, bf16[272,1024]{1,0:T(8,128)(2,1)} %constant.40.clone.table_in), custom_call_target="tpu_custom_call" | custom-call | flops 1700000000 | bytes 5000000 | tf_op jit(solution)/shard_map/forward/pallas_call | solution.py:151
  5.3 2.8 %collective-permute-start.2 = (bf16[272,256]{1,0:T(8,128)(2,1)S(1)}, bf16[272,256]{1,0:T(8,128)(2,1)S(1)}, u32[]{:S(2)}, u32[]{:S(2)}) collective-permute-start(bf16[272,256]{1,0:T(8,128)(2,1)S(1)} %forward.1.own.c0), channel_id=1, source_target_pairs={{0,3},{1,0},{2,1},{3,2},{4,7},{5,4},{6,5},{7,6},{8,11},{9,8},{10,9... | collective-permute-start | bytes 417800 | tf_op jit(solution)/shard_map/ppermute | solution.py:323
  8.1 0.0 collective-permute-start.1
  8.1 2.3 %collective-permute-start = (bf16[272,256]{1,0:T(8,128)(2,1)S(1)}, bf16[272,256]{1,0:T(8,128)(2,1)S(1)}, u32[]{:S(2)}, u32[]{:S(2)}) collective-permute-start(bf16[272,256]{1,0:T(8,128)(2,1)S(1)} %forward.1.own.c0), channel_id=1, source_target_pairs={{0,2},{1,3},{2,0},{3,1},{4,6},{5,7},{6,4},{7,5},{8,10},{9,11},{10,... | collective-permute-start | bytes 417800 | tf_op jit(solution)/shard_map/ppermute | solution.py:323
  10.4 0.0 copy-done.3
  10.4 0.0 copy-done.4
  10.5 0.6 %collective-permute-done.2.three.c3 = bf16[272,256]{1,0:T(8,128)(2,1)S(1)} collective-permute-done((bf16[272,256]{1,0:T(8,128)(2,1)S(1)}, bf16[272,256]{1,0:T(8,128)(2,1)S(1)}, u32[]{:S(2)}, u32[]{:S(2)}) %collective-permute-start.2) | collective-permute-done | bytes 139296 | tf_op jit(solution)/shard_map/ppermute | solution.py:323
  11.1 6.4 %collective-permute-done.1.two.c2 = bf16[272,256]{1,0:T(8,128)(2,1)S(1)} collective-permute-done((bf16[272,256]{1,0:T(8,128)(2,1)S(1)}, bf16[272,256]{1,0:T(8,128)(2,1)S(1)}, u32[]{:S(2)}, u32[]{:S(2)}) %collective-permute-start.1) | collective-permute-done | bytes 139296 | tf_op jit(solution)/shard_map/ppermute | solution.py:323
  17.5 0.0 collective-permute-done.one.c1
  17.5 0.1 add.11.mine
  17.5 7.3 %collective-permute-start.3 = (bf16[264,256]{1,0:T(8,128)(2,1)S(1)}, bf16[264,256]{1,0:T(8,128)(2,1)S(1)}, u32[]{:S(2)}, u32[]{:S(2)}) collective-permute-start(bf16[264,256]{1,0:T(8,128)(2,1)S(1)} %add.11.mine), channel_id=1, source_target_pairs={{0,4},{4,0},{1,5},{5,1},{2,6},{6,2},{3,7},{7,3},{8,12},{12,8},{9,1... | collective-permute-start | bytes 405512 | tf_op jit(solution)/shard_map/ppermute | solution.py:334
  24.9 0.7 %pupils.1.pupil = bf16[16,256,256]{2,1,0:T(8,128)(2,1)S(1)} custom-call(bf16[272,256]{1,0:T(8,128)(2,1)S(1)} %forward.1.own.c0, bf16[272,256]{1,0:T(8,128)(2,1)S(1)} %collective-permute-done.one.c1, bf16[272,256]{1,0:T(8,128)(2,1)S(1)} %collective-permute-done.1.two.c2, bf16[272,256]{1,0:T(8,128)(2,1)S(1)} %collective-permute-done.2.three.c3), custom_call_target="tpu_custom_call" | custom-call | flops 10000000 | bytes 2000000 | tf_op jit(solution)/shard_map/pupils/pallas_call | solution.py:208
  25.6 3.3 %collective-permute-done.3.other = bf16[264,256]{1,0:T(8,128)(2,1)S(1)} collective-permute-done((bf16[264,256]{1,0:T(8,128)(2,1)S(1)}, bf16[264,256]{1,0:T(8,128)(2,1)S(1)}, u32[]{:S(2)}, u32[]{:S(2)}) %collective-permute-start.3) | collective-permute-done | bytes 135200 | tf_op jit(solution)/shard_map/ppermute | solution.py:334
  28.9 0.0 copy-done
  28.9 0.0 copy-done.1
  28.9 0.0 copy-done.2
  28.9 3.8 %inverse.1 = f32[128,1024]{1,0:T(8,128)} custom-call(bf16[264,256]{1,0:T(8,128)(2,1)S(1)} %add.11.mine, bf16[264,256]{1,0:T(8,128)(2,1)S(1)} %collective-permute-done.3.other, bf16[272,256]{1,0:T(8,128)(2,1)S(1)} %forward.1.own.c0, bf16[272,256]{1,0:T(8,128)(2,1)S(1)} %collective-permute-done.one.c1, bf16[272,256]{1,0:T(8,128)(2,1)S(1)} %collective-permute-done.1.two.c2, ...), custom_call_target="tpu_custom_call" | custom-call | flops 2500000000 | bytes 3000000 | tf_op jit(solution)/shard_map/inverse/pallas_call | solution.py:297
  (5 shorter events, 0.1 us)
Async XLA Ops:
  0.0 10.4 %copy-start.3 = (bf16[2,128,256]{2,1,0:T(8,128)(2,1)S(1)}, bf16[2,128,256]{2,1,0:T(8,128)(2,1)}, u32[]{:S(2)}) copy-start(bf16[2,128,256]{2,1,0:T(8,128)(2,1)} %constant.47) | copy-start | bytes 393220
  0.0 10.4 %copy-start.4 = (bf16[2,128,256]{2,1,0:T(8,128)(2,1)S(1)}, bf16[2,128,256]{2,1,0:T(8,128)(2,1)}, u32[]{:S(2)}) copy-start(bf16[2,128,256]{2,1,0:T(8,128)(2,1)} %constant.45) | copy-start | bytes 393220
  0.0 28.9 %copy-start = (bf16[2,256,1024]{2,1,0:T(8,128)(2,1)S(1)}, bf16[2,256,1024]{2,1,0:T(8,128)(2,1)}, u32[]{:S(2)}) copy-start(bf16[2,256,1024]{2,1,0:T(8,128)(2,1)} %constant.42.clone.spread) | copy-start | bytes 3145732
  0.0 28.9 %copy-start.1 = (bf16[2,512,256]{2,1,0:T(8,128)(2,1)S(1)}, bf16[2,512,256]{2,1,0:T(8,128)(2,1)}, u32[]{:S(2)}) copy-start(bf16[2,512,256]{2,1,0:T(8,128)(2,1)} %constant.41.clone.right) | copy-start | bytes 1572868
  0.0 28.9 %copy-start.2 = (f32[8,1024]{1,0:T(8,128)S(1)}, f32[8,1024]{1,0:T(8,128)}, u32[]{:S(2)}) copy-start(f32[8,1024]{1,0:T(8,128)} %constant.43.clone.sine) | copy-start | bytes 98308
  5.3 5.8 %collective-permute-start.2 = (bf16[272,256]{1,0:T(8,128)(2,1)S(1)}, bf16[272,256]{1,0:T(8,128)(2,1)S(1)}, u32[]{:S(2)}, u32[]{:S(2)}) collective-permute-start(bf16[272,256]{1,0:T(8,128)(2,1)S(1)} %forward.1.own.c0), channel_id=1, source_target_pairs={{0,3},{1,0},{2,1},{3,2},{4,7},{5,4},{6,5},{7,6},{8,11},{9,8},{10,9... | collective-permute-start | bytes 417800 | tf_op jit(solution)/shard_map/ppermute | solution.py:323
  8.1 9.3 %collective-permute-start.1 = (bf16[272,256]{1,0:T(8,128)(2,1)S(1)}, bf16[272,256]{1,0:T(8,128)(2,1)S(1)}, u32[]{:S(2)}, u32[]{:S(2)}) collective-permute-start(bf16[272,256]{1,0:T(8,128)(2,1)S(1)} %forward.1.own.c0), channel_id=1, source_target_pairs={{0,1},{1,2},{2,3},{3,0},{4,5},{5,6},{6,7},{7,4},{8,9},{9,10},{10,1... | collective-permute-start | bytes 417800 | tf_op jit(solution)/shard_map/ppermute | solution.py:323
  8.1 9.3 %collective-permute-start = (bf16[272,256]{1,0:T(8,128)(2,1)S(1)}, bf16[272,256]{1,0:T(8,128)(2,1)S(1)}, u32[]{:S(2)}, u32[]{:S(2)}) collective-permute-start(bf16[272,256]{1,0:T(8,128)(2,1)S(1)} %forward.1.own.c0), channel_id=1, source_target_pairs={{0,2},{1,3},{2,0},{3,1},{4,6},{5,7},{6,4},{7,5},{8,10},{9,11},{10,... | collective-permute-start | bytes 417800 | tf_op jit(solution)/shard_map/ppermute | solution.py:323
  17.5 11.4 %collective-permute-start.3 = (bf16[264,256]{1,0:T(8,128)(2,1)S(1)}, bf16[264,256]{1,0:T(8,128)(2,1)S(1)}, u32[]{:S(2)}, u32[]{:S(2)}) collective-permute-start(bf16[264,256]{1,0:T(8,128)(2,1)S(1)} %add.11.mine), channel_id=1, source_target_pairs={{0,4},{4,0},{1,5},{5,1},{2,6},{6,2},{3,7},{7,3},{8,12},{12,8},{9,1... | collective-permute-start | bytes 405512 | tf_op jit(solution)/shard_map/ppermute | solution.py:334

commit v4 on v3

--- a/solution.py
+++ b/solution.py
@@ -186,7 +186,13 @@
     )(*args)
 
 
-def pupil_kernel(c0, c1, c2, c3, out):
+def pupil_kernel(c0, c1, c2, c3, right_in, spread_in, out, right, spread, sem):
+    copies = [
+        pltpu.make_async_copy(right_in, right, sem.at[0]),
+        pltpu.make_async_copy(spread_in, spread, sem.at[1]),
+    ]
+    for copy in copies:
+        copy.start()
     f_low = lax.broadcasted_iota(jnp.int32, (HALF, HALF), 0)
     g_low = lax.broadcasted_iota(jnp.int32, (1, HALF), 1)
     f_halves = (f_low.astype(F32), jnp.where(f_low == 0, -HALF, -f_low).astype(F32))
@@ -202,18 +208,26 @@
                 out[s, i * HALF:(i + 1) * HALF, j * HALF:(j + 1) * HALF] = jnp.where(
                     room >= reach, 1.0, 0.0
                 ).astype(BF16)
-
-
-def pupils(*args):
+    for copy in copies:
+        copy.wait()
+
+
+def pupils(parts, right, spread):
+    tables = [pltpu.with_memory_space_constraint(x, pltpu.HBM) for x in (right, spread)]
     return pl.pallas_call(
         pupil_kernel,
-        in_specs=[VMEM] * 4,
-        out_specs=VMEM,
-        out_shape=jax.ShapeDtypeStruct((16, 256, 256), BF16),
+        in_specs=[VMEM] * 4 + [pl.BlockSpec(memory_space=pltpu.HBM)] * 2,
+        out_specs=[VMEM] * 3,
+        out_shape=[
+            jax.ShapeDtypeStruct((16, 256, 256), BF16),
+            jax.ShapeDtypeStruct(right.shape, BF16),
+            jax.ShapeDtypeStruct(spread.shape, BF16),
+        ],
+        scratch_shapes=[pltpu.SemaphoreType.DMA((2,))],
         compiler_params=pltpu.CompilerParams(vmem_limit_bytes=8 * 1024 * 1024),
-        cost_estimate=pl.CostEstimate(flops=10_000_000, bytes_accessed=2_000_000, transcendentals=0),
+        cost_estimate=pl.CostEstimate(flops=10_000_000, bytes_accessed=4_000_000, transcendentals=0),
         name="pupils",
-    )(*args)
+    )(*parts, *tables)
 
 
 def inverse_kernel(mine, other, c0, c1, c2, c3, pupil, left, right, spread, sine, out, spec, fields):
@@ -329,19 +343,11 @@
     place = lax.axis_index("row") * 4 + lax.axis_index("src")
     left_mine = place_rows(jnp.asarray(left, BF16), place)
     own = forward(mask_clip, source_shifts.T, source_weights, jnp.asarray(table, BF16))
-    parts = [own] + [ring(own, k) for k in (2, 1, 3)]
+    parts = [own] + [ring(own, k) for k in (1, 3, 2)]
     mine = add(*parts)
     other = lax.ppermute(mine, "row", [(0, 1), (1, 0)])
-    return inverse(
-        mine,
-        other,
-        *parts,
-        pupils(*parts),
-        left_mine,
-        jnp.asarray(right, BF16),
-        jnp.asarray(spread, BF16),
-        jnp.asarray(sine, F32),
-    )
+    pupil, right, spread = pupils(parts, jnp.asarray(right, BF16), jnp.asarray(spread, BF16))
+    return inverse(mine, other, *parts, pupil, left_mine, right, spread, jnp.asarray(sine, F32))
 
 
 def solution(mesh):

time: 32.8 us -> 32.2 us (0.982)
  the two profiles are of different devices: /device:TPU:8 before, /device:TPU:34 now
where the time goes in v4:
time: 32.2 us; the launch traced here: 32.1 us
  waiting for transfers between devices  10.9 us (34%)
  starting transfers between devices  10.6 us (33%)
  Pallas kernels  10.4 us (32%)
    ppermute x1, starting transfers between devices, body(): other = lax.ppermute(mine, 'row', [(0, 1), (1, 0)])  6.38 us
    ppermute x3, waiting for transfers between devices, ring(): return lax.ppermute(x, 'src', [(i, (i + k) % 4) for i in range(4)])  5.71 us
    ppermute x1, waiting for transfers between devices, body(): other = lax.ppermute(mine, 'row', [(0, 1), (1, 0)])  5.22 us
    pallas_call x1, Pallas kernels, forward(): pl.pallas_call(forward_kernel, in_specs=[hbm] * 4, out_specs=VMEM, out_sh...  5.17 us
    ppermute x3, starting transfers between devices, ring(): return lax.ppermute(x, 'src', [(i, (i + k) % 4) for i in range(4)])  4.24 us
    pallas_call x1, Pallas kernels, inverse(): pl.pallas_call(inverse_kernel, in_specs=[VMEM] * len(args), out_specs=VME...  3.79 us
    pallas_call x1, Pallas kernels, pupils(): pl.pallas_call(pupil_kernel, in_specs=[VMEM] * 4 + [pl.BlockSpec(memory_s...  1.41 us
  transfers between devices with their start and end apart: 4, of which 3 were waited for; matrix products, arithmetic and copies ran while one was open for 0% of the time, Pallas kernels for 4%

profile of v4, /device:TPU:34, one launch (start us, length us, event | category | flops | bytes accessed | tf_op | source)
XLA Modules:
  0.0 32.1 jit_solution(1800502389449930259)
XLA Ops:
  0.0 0.0 copy-start.1
  0.0 0.0 copy-start.2
  0.0 0.0 copy-start
  0.0 5.2 %forward.1.own.c0 = bf16[272,256]{1,0:T(8,128)(2,1)S(1)} custom-call(s32[2,4]{1,0:T(2,128)} %bitcast.15, s32[4]{0:T(128)} %weights_in.1, bf16[2048,1024]{1,0:T(8,128)(2,1)} %mask.1, bf16[272,1024]{1,0:T(8,128)(2,1)} %constant.40.clone.table_in), custom_call_target="tpu_custom_call" | custom-call | flops 1700000000 | bytes 5000000 | tf_op jit(solution)/shard_map/forward/pallas_call | solution.py:151
  5.2 2.2 %collective-permute-start.2 = (bf16[272,256]{1,0:T(8,128)(2,1)S(1)}, bf16[272,256]{1,0:T(8,128)(2,1)S(1)}, u32[]{:S(2)}, u32[]{:S(2)}) collective-permute-start(bf16[272,256]{1,0:T(8,128)(2,1)S(1)} %forward.1.own.c0), channel_id=1, source_target_pairs={{0,2},{1,3},{2,0},{3,1},{4,6},{5,7},{6,4},{7,5},{8,10},{9,11},{10,... | collective-permute-start | bytes 417800 | tf_op jit(solution)/shard_map/ppermute | solution.py:337
  7.4 1.4 %collective-permute-start.1 = (bf16[272,256]{1,0:T(8,128)(2,1)S(1)}, bf16[272,256]{1,0:T(8,128)(2,1)S(1)}, u32[]{:S(2)}, u32[]{:S(2)}) collective-permute-start(bf16[272,256]{1,0:T(8,128)(2,1)S(1)} %forward.1.own.c0), channel_id=1, source_target_pairs={{0,3},{1,0},{2,1},{3,2},{4,7},{5,4},{6,5},{7,6},{8,11},{9,8},{10,9... | collective-permute-start | bytes 417800 | tf_op jit(solution)/shard_map/ppermute | solution.py:337
  8.8 0.6 %collective-permute-start = (bf16[272,256]{1,0:T(8,128)(2,1)S(1)}, bf16[272,256]{1,0:T(8,128)(2,1)S(1)}, u32[]{:S(2)}, u32[]{:S(2)}) collective-permute-start(bf16[272,256]{1,0:T(8,128)(2,1)S(1)} %forward.1.own.c0), channel_id=1, source_target_pairs={{0,1},{1,2},{2,3},{3,0},{4,5},{5,6},{6,7},{7,4},{8,9},{9,10},{10,1... | collective-permute-start | bytes 417800 | tf_op jit(solution)/shard_map/ppermute | solution.py:337
  9.4 0.0 copy-done.1
  9.4 0.0 copy-done.2
  9.5 3.8 %collective-permute-done.2.three.c3 = bf16[272,256]{1,0:T(8,128)(2,1)S(1)} collective-permute-done((bf16[272,256]{1,0:T(8,128)(2,1)S(1)}, bf16[272,256]{1,0:T(8,128)(2,1)S(1)}, u32[]{:S(2)}, u32[]{:S(2)}) %collective-permute-start.2) | collective-permute-done | bytes 139296 | tf_op jit(solution)/shard_map/ppermute | solution.py:337
  13.3 1.8 %collective-permute-done.1.two.c2 = bf16[272,256]{1,0:T(8,128)(2,1)S(1)} collective-permute-done((bf16[272,256]{1,0:T(8,128)(2,1)S(1)}, bf16[272,256]{1,0:T(8,128)(2,1)S(1)}, u32[]{:S(2)}, u32[]{:S(2)}) %collective-permute-start.1) | collective-permute-done | bytes 139296 | tf_op jit(solution)/shard_map/ppermute | solution.py:337
  15.2 0.0 collective-permute-done.one.c1
  15.2 0.1 add.11.mine
  15.3 6.4 %collective-permute-start.3 = (bf16[264,256]{1,0:T(8,128)(2,1)S(1)}, bf16[264,256]{1,0:T(8,128)(2,1)S(1)}, u32[]{:S(2)}, u32[]{:S(2)}) collective-permute-start(bf16[264,256]{1,0:T(8,128)(2,1)S(1)} %add.11.mine), channel_id=1, source_target_pairs={{0,4},{4,0},{1,5},{5,1},{2,6},{6,2},{3,7},{7,3},{8,12},{12,8},{9,1... | collective-permute-start | bytes 405512 | tf_op jit(solution)/shard_map/ppermute | solution.py:348
  21.7 1.4 %pupils.1 = (bf16[16,256,256]{2,1,0:T(8,128)(2,1)S(1)}, bf16[2,512,256]{2,1,0:T(8,128)(2,1)S(1)}, bf16[2,256,1024]{2,1,0:T(8,128)(2,1)S(1)}) custom-call(bf16[272,256]{1,0:T(8,128)(2,1)S(1)} %forward.1.own.c0, bf16[272,256]{1,0:T(8,128)(2,1)S(1)} %collective-permute-done.one.c1, bf16[272,256]{1,0:T(8,128)(2,1)S(1)} %collective-permute-done.1.two.c2, ...), custom_call_target="tpu_custom_call" | custom-call | flops 10000000 | bytes 4000000 | tf_op jit(solution)/shard_map/pupils/pallas_call | solution.py:217
  23.1 5.2 %collective-permute-done.3.other = bf16[264,256]{1,0:T(8,128)(2,1)S(1)} collective-permute-done((bf16[264,256]{1,0:T(8,128)(2,1)S(1)}, bf16[264,256]{1,0:T(8,128)(2,1)S(1)}, u32[]{:S(2)}, u32[]{:S(2)}) %collective-permute-start.3) | collective-permute-done | bytes 135200 | tf_op jit(solution)/shard_map/ppermute | solution.py:348
  28.3 0.0 copy-done
  28.3 3.8 %inverse.1 = f32[128,1024]{1,0:T(8,128)} custom-call(bf16[264,256]{1,0:T(8,128)(2,1)S(1)} %add.11.mine, bf16[264,256]{1,0:T(8,128)(2,1)S(1)} %collective-permute-done.3.other, bf16[272,256]{1,0:T(8,128)(2,1)S(1)} %forward.1.own.c0, bf16[272,256]{1,0:T(8,128)(2,1)S(1)} %collective-permute-done.one.c1, bf16[272,256]{1,0:T(8,128)(2,1)S(1)} %collective-permute-done.1.two.c2, ...), custom_call_target="tpu_custom_call" | custom-call | flops 2500000000 | bytes 3000000 | tf_op jit(solution)/shard_map/inverse/pallas_call | solution.py:311
  (5 shorter events, 0.1 us)
Async XLA Ops:
  0.0 9.4 %copy-start.1 = (bf16[2,128,256]{2,1,0:T(8,128)(2,1)S(1)}, bf16[2,128,256]{2,1,0:T(8,128)(2,1)}, u32[]{:S(2)}) copy-start(bf16[2,128,256]{2,1,0:T(8,128)(2,1)} %constant.47) | copy-start | bytes 393220
  0.0 9.4 %copy-start.2 = (bf16[2,128,256]{2,1,0:T(8,128)(2,1)S(1)}, bf16[2,128,256]{2,1,0:T(8,128)(2,1)}, u32[]{:S(2)}) copy-start(bf16[2,128,256]{2,1,0:T(8,128)(2,1)} %constant.45) | copy-start | bytes 393220
  0.0 28.3 %copy-start = (f32[8,1024]{1,0:T(8,128)S(1)}, f32[8,1024]{1,0:T(8,128)}, u32[]{:S(2)}) copy-start(f32[8,1024]{1,0:T(8,128)} %constant.43.clone.sine) | copy-start | bytes 98308
  5.2 8.1 %collective-permute-start.2 = (bf16[272,256]{1,0:T(8,128)(2,1)S(1)}, bf16[272,256]{1,0:T(8,128)(2,1)S(1)}, u32[]{:S(2)}, u32[]{:S(2)}) collective-permute-start(bf16[272,256]{1,0:T(8,128)(2,1)S(1)} %forward.1.own.c0), channel_id=1, source_target_pairs={{0,2},{1,3},{2,0},{3,1},{4,6},{5,7},{6,4},{7,5},{8,10},{9,11},{10,... | collective-permute-start | bytes 417800 | tf_op jit(solution)/shard_map/ppermute | solution.py:337
  7.4 7.8 %collective-permute-start.1 = (bf16[272,256]{1,0:T(8,128)(2,1)S(1)}, bf16[272,256]{1,0:T(8,128)(2,1)S(1)}, u32[]{:S(2)}, u32[]{:S(2)}) collective-permute-start(bf16[272,256]{1,0:T(8,128)(2,1)S(1)} %forward.1.own.c0), channel_id=1, source_target_pairs={{0,3},{1,0},{2,1},{3,2},{4,7},{5,4},{6,5},{7,6},{8,11},{9,8},{10,9... | collective-permute-start | bytes 417800 | tf_op jit(solution)/shard_map/ppermute | solution.py:337
  8.8 6.4 %collective-permute-start = (bf16[272,256]{1,0:T(8,128)(2,1)S(1)}, bf16[272,256]{1,0:T(8,128)(2,1)S(1)}, u32[]{:S(2)}, u32[]{:S(2)}) collective-permute-start(bf16[272,256]{1,0:T(8,128)(2,1)S(1)} %forward.1.own.c0), channel_id=1, source_target_pairs={{0,1},{1,2},{2,3},{3,0},{4,5},{5,6},{6,7},{7,4},{8,9},{9,10},{10,1... | collective-permute-start | bytes 417800 | tf_op jit(solution)/shard_map/ppermute | solution.py:337
  15.3 13.1 %collective-permute-start.3 = (bf16[264,256]{1,0:T(8,128)(2,1)S(1)}, bf16[264,256]{1,0:T(8,128)(2,1)S(1)}, u32[]{:S(2)}, u32[]{:S(2)}) collective-permute-start(bf16[264,256]{1,0:T(8,128)(2,1)S(1)} %add.11.mine), channel_id=1, source_target_pairs={{0,4},{4,0},{1,5},{5,1},{2,6},{6,2},{3,7},{7,3},{8,12},{12,8},{9,1... | collective-permute-start | bytes 405512 | tf_op jit(solution)/shard_map/ppermute | solution.py:348

commit v5 on v4

--- a/solution.py
+++ b/solution.py
@@ -10,9 +10,9 @@
 NI = 1024
 TILE = NM // 4
 HALF = 128
-CHUNKS = ((0, 512), (512, 1024), (1024, 1536), (1536, 2048))
-SENT = 272
-SUMMED = 264
+CHUNK = 512
+QUARTER = 64
+SENT = 144
 COARSE = 256
 NT = (((1,), (1,)), ((), ()))
 F32 = jnp.float32
@@ -65,16 +65,18 @@
     return cos_q, sin_q
 
 
-def forward_kernel(shifts_in, weights_in, mask, table_in, out,
-                   shifts, weights, block, table, half_way, folded, sem):
+def forward_kernel(shifts_in, weights_in, mask, table_in, keep, give,
+                   shifts, weights, block, table, half_way, folded, whole, sem):
     small_copies = [
         pltpu.make_async_copy(table_in, table, sem.at[0]),
         pltpu.make_async_copy(shifts_in, shifts, sem.at[1]),
         pltpu.make_async_copy(weights_in, weights, sem.at[2]),
     ]
     copies = [
-        pltpu.make_async_copy(mask.at[start:stop], block.at[start:stop], sem.at[3 + i])
-        for i, (start, stop) in enumerate(CHUNKS)
+        pltpu.make_async_copy(
+            mask.at[i * CHUNK:(i + 1) * CHUNK], block.at[i * CHUNK:(i + 1) * CHUNK], sem.at[3 + i]
+        )
+        for i in range(4)
     ]
     for copy in (small_copies[0], *copies, *small_copies[1:]):
         copy.start()
@@ -95,30 +97,34 @@
         return c * x[:, :HALF] - s * x[:, HALF:], c * x[:, HALF:] + s * x[:, :HALF]
 
     small_copies[0].wait()
-    sums = []
-    for copy, (start, stop) in zip(copies, CHUNKS):
-        copy.wait()
-        part, at = start // TILE, start % TILE
-        half_way[start:stop] = lax.dot_general(
-            block[start:stop], table[:256, :], NT, preferred_element_type=F32
+
+    @pl.loop(0, 4)
+    def _(i):
+        rows = pl.ds(pl.multiple_of(i * CHUNK, CHUNK), CHUNK)
+        pltpu.make_async_copy(mask.at[rows], block.at[rows], sem.at[3 + i]).wait()
+        half_way[rows] = lax.dot_general(
+            block[rows], table[:256, :], NT, preferred_element_type=F32
         ).astype(BF16)
-        for low in range(0, stop - start, 64):
-            rows = slice(start + low, start + low + 64)
-            tiles = [block[rows, tile * HALF:(tile + 1) * HALF] for tile in range(8)]
+        lanes = pl.ds(pl.multiple_of((i // 2) * HALF, HALF), HALF)
+        for low in range(0, CHUNK, 64):
+            strip = pl.ds(pl.multiple_of(i * CHUNK + low, 64), 64)
+            tiles = [block[strip, tile * HALF:(tile + 1) * HALF] for tile in range(8)]
             while len(tiles) > 1:
                 tiles = [tiles[t] + tiles[t + 1] for t in range(0, len(tiles), 2)]
-            folded[at + low:at + low + 64, part * HALF:(part + 1) * HALF] = tiles[0]
-        if start == TILE:
-            sums.append(jnp.dot(table[:264], half_way[:TILE], preferred_element_type=F32))
-    sums.append(jnp.dot(table[:264], half_way[TILE:], preferred_element_type=F32))
+            folded[pl.ds(pl.multiple_of(lax.rem(i, 2) * CHUNK + low, 64), 64), lanes] = tiles[0]
+
+    sums = [
+        jnp.dot(table[:264], half_way[h * TILE:(h + 1) * TILE], preferred_element_type=F32)
+        for h in range(2)
+    ]
     sides = jnp.dot(table[:256, :], folded[...], preferred_element_type=F32)
     for copy in small_copies[1:]:
         copy.wait()
     a, b = sums
     for start, x in zip((0, HALF), join_rows(a, b)):
         x_cos, x_sin = turn_columns(x)
-        out[start:start + HALF, :HALF] = x_cos.astype(BF16)
-        out[start:start + HALF, HALF:] = x_sin.astype(BF16)
+        whole[start:start + HALF, :HALF] = x_cos
+        whole[start:start + HALF, HALF:] = x_sin
     e_cos, e_sin = turn_columns(a[256:] + b[256:])
     s_a, s_b = sides[:, :HALF], sides[:, HALF:]
     c, s, g = cos_f[:, :HALF], sin_f[:, :HALF], sign[:, :HALF]
@@ -130,20 +136,28 @@
         0,
     ).astype(BF16)
     crossed = lax.dot_general(table[264:272, :HALF], edges, NT, preferred_element_type=F32)
-    pad = jnp.zeros((8, HALF), F32)
-    first = jnp.concatenate([e_cos + crossed[:, :HALF], pad], 0)
-    second = jnp.concatenate([e_sin + crossed[:, HALF:], pad], 0)
+    edges = jnp.concatenate([e_cos + crossed[:, :HALF], e_sin + crossed[:, HALF:]], 1)
     row = lax.broadcasted_iota(jnp.int32, (16, HALF), 0)
+    first = jnp.zeros((16, HALF), F32)
+    second = jnp.zeros((16, HALF), F32)
     for i in range(4):
-        first = jnp.where(row == 4 + i, shifts[0, i].astype(F32), first)
-        second = jnp.where(row == 4 + i, shifts[1, i].astype(F32), second)
+        first = jnp.where(row == 2 + i, shifts[0, i].astype(F32), first)
+        second = jnp.where(row == 2 + i, shifts[1, i].astype(F32), second)
         w = weights[i].astype(F32)
         if i % 2 == 0:
-            first = jnp.where(row == 8 + i // 2, w, first)
+            first = jnp.where(row == 6 + i // 2, w, first)
         else:
-            second = jnp.where(row == 8 + i // 2, w, second)
-    out[256:SENT, :HALF] = first.astype(BF16)
-    out[256:SENT, HALF:] = second.astype(BF16)
+            second = jnp.where(row == 6 + i // 2, w, second)
+    sources = jnp.concatenate([first, second], 1)
+    row = lax.broadcasted_iota(jnp.int32, (16, 256), 0)
+    for out, odd in ((keep, lax.rem(src_id, 2)), (give, lax.rem(src_id + 1, 2))):
+        at = pl.multiple_of(odd * QUARTER, QUARTER)
+        out[:QUARTER] = whole[pl.ds(at, QUARTER)].astype(BF16)
+        out[QUARTER:HALF] = whole[pl.ds(HALF + at, QUARTER)].astype(BF16)
+        lines = [jnp.where(odd == 1, edges[2 + i:3 + i], edges[i:i + 1]) for i in range(2)]
+        out[HALF:SENT] = jnp.where(
+            row == 0, lines[0], jnp.where(row == 1, lines[1], sources)
+        ).astype(BF16)
 
 
 def forward(mask_clip, shifts, weights, table):
@@ -151,8 +165,8 @@
     return pl.pallas_call(
         forward_kernel,
         in_specs=[hbm] * 4,
-        out_specs=VMEM,
-        out_shape=jax.ShapeDtypeStruct((SENT, 256), BF16),
+        out_specs=[VMEM] * 2,
+        out_shape=[jax.ShapeDtypeStruct((SENT, 256), BF16)] * 2,
         scratch_shapes=[
             pltpu.SMEM((2, 4), jnp.int32),
             pltpu.SMEM((4,), jnp.int32),
@@ -160,7 +174,8 @@
             pltpu.VMEM((272, TILE), BF16),
             pltpu.VMEM((2 * TILE, 256), BF16),
             pltpu.VMEM((TILE, 256), BF16),
-            pltpu.SemaphoreType.DMA((3 + len(CHUNKS),)),
+            pltpu.VMEM((256, 256), F32),
+            pltpu.SemaphoreType.DMA((7,)),
         ],
         compiler_params=pltpu.CompilerParams(vmem_limit_bytes=16 * 1024 * 1024),
         cost_estimate=pl.CostEstimate(flops=1_700_000_000, bytes_accessed=5_000_000, transcendentals=0),
@@ -170,19 +185,29 @@
 
 def add_kernel(own, one, two, three, out):
     out[...] = (
-        own[:SUMMED].astype(F32) + one[:SUMMED].astype(F32)
-        + two[:SUMMED].astype(F32) + three[:SUMMED].astype(F32)
+        own[...].astype(F32) + one[...].astype(F32) + two[...].astype(F32) + three[...].astype(F32)
     ).astype(BF16)
 
 
-def add(*args):
+def finish_kernel(mine, other, out):
+    total = mine[...].astype(F32) + other[...].astype(F32)
+    cc, cs = total[:QUARTER, :HALF], total[:QUARTER, HALF:]
+    sc, ss = total[QUARTER:HALF, :HALF], total[QUARTER:HALF, HALF:]
+    out[:QUARTER, :HALF] = (cc - ss).astype(BF16)
+    out[:QUARTER, HALF:] = (cc + ss).astype(BF16)
+    out[QUARTER:HALF, :HALF] = (-(sc + cs)).astype(BF16)
+    out[QUARTER:HALF, HALF:] = (cs - sc).astype(BF16)
+    out[HALF:] = total[HALF:].astype(BF16)
+
+
+def small(kernel, name, *args):
     return pl.pallas_call(
-        add_kernel,
-        in_specs=[VMEM] * 4,
+        kernel,
+        in_specs=[VMEM] * len(args),
         out_specs=VMEM,
-        out_shape=jax.ShapeDtypeStruct((SUMMED, 256), BF16),
+        out_shape=jax.ShapeDtypeStruct((SENT, 256), BF16),
         compiler_params=pltpu.CompilerParams(vmem_limit_bytes=4 * 1024 * 1024),
-        name="add",
+        name=name,
     )(*args)
 
 
@@ -198,8 +223,8 @@
     f_halves = (f_low.astype(F32), jnp.where(f_low == 0, -HALF, -f_low).astype(F32))
     g_halves = (g_low.astype(F32), jnp.where(g_low == 0, -HALF, -g_low).astype(F32))
     for s in range(16):
-        info = (c0, c1, c2, c3)[s // 4][256:SENT].astype(F32)
-        i = 4 + s % 4
+        info = (c0, c1, c2, c3)[s // 4][HALF:SENT].astype(F32)
+        i = 2 + s % 4
         a, b = info[i:i + 1, :HALF], info[i:i + 1, HALF:]
         for i, f in enumerate(f_halves):
             room = 4096.0 - (f + a) * (f + a)
@@ -230,47 +255,51 @@
     )(*parts, *tables)
 
 
-def inverse_kernel(mine, other, c0, c1, c2, c3, pupil, left, right, spread, sine, out, spec, fields):
-    total = mine[:256].astype(F32) + other[:256].astype(F32)
-    cc, cs = total[:HALF, :HALF], total[:HALF, HALF:]
-    sc, ss = total[HALF:, :HALF], total[HALF:, HALF:]
-    edge = mine[256:SUMMED].astype(F32) + other[256:SUMMED].astype(F32)
+def inverse_kernel(mine, other, c0, c1, c2, c3, pupil, left, right, spread, sine, out,
+                   spec, edge, fields):
+    src_id = lax.axis_index("src")
+    for chunk, odd in ((mine, lax.rem(src_id, 2)), (other, lax.rem(src_id + 1, 2))):
+        at = pl.multiple_of(odd * QUARTER, QUARTER)
+        re, im = chunk[:QUARTER], chunk[QUARTER:HALF]
+        spec[pl.ds(at, QUARTER)] = re
+        spec[pl.ds(256 + at, QUARTER)] = im
+        spec[pl.ds(HALF + at, QUARTER), :HALF] = re[:, HALF:]
+        spec[pl.ds(HALF + at, QUARTER), HALF:] = re[:, :HALF]
+        spec[pl.ds(384 + at, QUARTER), :HALF] = -im[:, HALF:]
+        spec[pl.ds(384 + at, QUARTER), HALF:] = -im[:, :HALF]
+        lines = chunk[HALF:SENT].astype(F32)
+        edge[pl.ds(odd * 2, 1)] = lines[0:1]
+        edge[pl.ds(odd * 2 + 1, 1)] = lines[1:2]
     rc, rs, xc, xs = (edge[i:i + 1] for i in range(4))
-    row_re = (rc[:, :HALF] + rs[:, HALF:], rc[:, :HALF] - rs[:, HALF:])
-    row_im = (rs[:, :HALF] - rc[:, HALF:], rs[:, :HALF] + rc[:, HALF:])
-    col_re = (xc[:, :HALF] + xs[:, HALF:], xc[:, :HALF] - xs[:, HALF:])
-    col_im = (xs[:, :HALF] - xc[:, HALF:], xs[:, :HALF] + xc[:, HALF:])
-    first_row = lax.broadcasted_iota(jnp.int32, (HALF, HALF), 0) == 0
+    row_re = jnp.concatenate([rc[:, :HALF] + rs[:, HALF:], rc[:, :HALF] - rs[:, HALF:]], 1)
+    row_im = jnp.concatenate([rs[:, :HALF] - rc[:, HALF:], rs[:, :HALF] + rc[:, HALF:]], 1)
+    col_re = jnp.concatenate([xc[:, :HALF] + xs[:, HALF:], xc[:, :HALF] - xs[:, HALF:]], 1)
+    col_im = jnp.concatenate([xs[:, :HALF] - xc[:, HALF:], xs[:, :HALF] + xc[:, HALF:]], 1)
+    top = lax.broadcasted_iota(jnp.int32, (16, 256), 0) == 0
     first_lane = lax.broadcasted_iota(jnp.int32, (HALF, HALF), 1) == 0
-    quads = {
-        (0, 0): (cc - ss, -(sc + cs)),
-        (0, 1): (cc + ss, cs - sc),
-        (1, 0): (cc + ss, sc - cs),
-        (1, 1): (cc - ss, sc + cs),
-    }
-    for (i, j), parts in quads.items():
-        for at, x, row, col in zip((0, 256), parts, (row_re, row_im), (col_re, col_im)):
-            if i == 1:
-                x = jnp.where(first_row, row[j], x)
-            if j == 1:
-                x = jnp.where(first_lane, jnp.broadcast_to(col[i], (HALF, HALF)).T, x)
-            spec[at + i * HALF:at + (i + 1) * HALF, j * HALF:(j + 1) * HALF] = x.astype(BF16)
+    for at, row, col in ((0, row_re, col_re), (256, row_im, col_im)):
+        low = slice(at + HALF, at + HALF + 16)
+        spec[low] = jnp.where(top, row, spec[low].astype(F32)).astype(BF16)
+        for i in range(2):
+            rows = slice(at + i * HALF, at + (i + 1) * HALF)
+            stood = jnp.broadcast_to(col[:, i * HALF:(i + 1) * HALF], (HALF, HALF)).T
+            spec[rows, HALF:] = jnp.where(first_lane, stood, spec[rows, HALF:].astype(F32)).astype(BF16)
 
     g_low = lax.broadcasted_iota(jnp.int32, (1, HALF), 1)
     g_all = jnp.concatenate([g_low, jnp.where(g_low == 0, -HALF, -g_low)], 1).astype(F32)
-    infos = [c[256:SENT].astype(F32) for c in (c0, c1, c2, c3)]
+    infos = [c[HALF:SENT].astype(F32) for c in (c0, c1, c2, c3)]
     ends = [jnp.zeros((1, 1), F32)]
 
     def weight(s):
         i = s % 4
-        return infos[s // 4][8 + i // 2:9 + i // 2, (i % 2) * HALF:(i % 2 + 1) * HALF]
+        return infos[s // 4][6 + i // 2:7 + i // 2, (i % 2) * HALF:(i % 2 + 1) * HALF]
 
     def propagate(s):
         passed = jnp.concatenate([spec[:256] * pupil[s], spec[256:] * pupil[s]], 0)
         k = jnp.dot(left[...], passed, preferred_element_type=F32)
         fields[s * HALF:(s + 1) * HALF, :256] = k[:HALF].astype(BF16)
         fields[s * HALF:(s + 1) * HALF, 256:] = k[HALF:].astype(BF16)
-        b = infos[s // 4][4 + s % 4:5 + s % 4, HALF:]
+        b = infos[s // 4][2 + s % 4:3 + s % 4, HALF:]
         at = g_all + jnp.concatenate([b, b], 1)
         r, m = k[0:1], k[HALF:HALF + 1]
         pick = lambda x, v: jnp.sum(jnp.where(at == v, x, 0.0), axis=1, keepdims=True)
@@ -315,6 +344,7 @@
         out_shape=jax.ShapeDtypeStruct((HALF, NI), F32),
         scratch_shapes=[
             pltpu.VMEM((512, 256), BF16),
+            pltpu.VMEM((8, 256), F32),
             pltpu.VMEM((2048, 512), BF16),
         ],
         compiler_params=pltpu.CompilerParams(vmem_limit_bytes=24 * 1024 * 1024),
@@ -342,10 +372,11 @@
     left, right, spread, sine = inverse_tables()
     place = lax.axis_index("row") * 4 + lax.axis_index("src")
     left_mine = place_rows(jnp.asarray(left, BF16), place)
-    own = forward(mask_clip, source_shifts.T, source_weights, jnp.asarray(table, BF16))
-    parts = [own] + [ring(own, k) for k in (1, 3, 2)]
-    mine = add(*parts)
-    other = lax.ppermute(mine, "row", [(0, 1), (1, 0)])
+    keep, give = forward(mask_clip, source_shifts.T, source_weights, jnp.asarray(table, BF16))
+    parts = [keep, ring(give, 1), ring(give, 3), ring(keep, 2)]
+    summed = small(add_kernel, "add", *parts)
+    mine = small(finish_kernel, "finish", summed, lax.ppermute(summed, "row", [(0, 1), (1, 0)]))
+    other = lax.ppermute(mine, "src", [(0, 1), (1, 0), (2, 3), (3, 2)])
     pupil, right, spread = pupils(parts, jnp.asarray(right, BF16), jnp.asarray(spread, BF16))
     return inverse(mine, other, *parts, pupil, left_mine, right, spread, jnp.asarray(sine, F32))
 

time: 32.2 us -> 31.8 us (0.988)
  the two profiles are of different devices: /device:TPU:34 before, /device:TPU:8 now
where the time goes in v5:
time: 31.8 us; the launch traced here: 31.7 us
  starting transfers between devices  12.6 us (40%)
  Pallas kernels  9.58 us (30%)
  waiting for transfers between devices  9.39 us (30%)
    ppermute x1, starting transfers between devices, body(): lax.ppermute(summed, 'row', [(0, 1), (1, 0)])  7.28 us
    ppermute x3, starting transfers between devices, ring(): return lax.ppermute(x, 'src', [(i, (i + k) % 4) for i in range(4)])  5.13 us
    pallas_call x1, Pallas kernels, forward(): pl.pallas_call(forward_kernel, in_specs=[hbm] * 4, out_specs=[VMEM] * 2,...  4.33 us
    ppermute x3, waiting for transfers between devices, ring(): return lax.ppermute(x, 'src', [(i, (i + k) % 4) for i in range(4)])  4.16 us
    pallas_call x1, Pallas kernels, inverse(): pl.pallas_call(inverse_kernel, in_specs=[VMEM] * len(args), out_specs=VME...  3.77 us
    ppermute x1, waiting for transfers between devices, body(): other = lax.ppermute(mine, 'src', [(0, 1), (1, 0), (2, 3), (3, 2)])  2.82 us
    ppermute x1, waiting for transfers between devices, body(): lax.ppermute(summed, 'row', [(0, 1), (1, 0)])  2.41 us
    pallas_call x1, Pallas kernels, pupils(): pl.pallas_call(pupil_kernel, in_specs=[VMEM] * 4 + [pl.BlockSpec(memory_s...  1.41 us
  transfers between devices with their start and end apart: 5, of which 3 were waited for; matrix products, arithmetic and copies ran while one was open for 0% of the time, Pallas kernels for 4%

profile of v5, /device:TPU:8, one launch (start us, length us, event | category | flops | bytes accessed | tf_op | source)
XLA Modules:
  0.0 31.7 jit_solution(15902657836707731726)
XLA Ops:
  0.0 0.0 copy-start.1
  0.0 0.0 copy-start.2
  0.0 0.0 copy-start
  0.0 4.3 %forward.1 = (bf16[144,256]{1,0:T(8,128)(2,1)S(1)}, bf16[144,256]{1,0:T(8,128)(2,1)S(1)}) custom-call(s32[2,4]{1,0:T(2,128)} %bitcast.15, s32[4]{0:T(128)} %weights_in.1, bf16[2048,1024]{1,0:T(8,128)(2,1)} %mask.1, bf16[272,1024]{1,0:T(8,128)(2,1)} %constant.40.clone.table_in), custom_call_target="tpu_custom_call" | custom-call | flops 1700000000 | bytes 5000000 | tf_op jit(solution)/shard_map/forward/pallas_call | solution.py:165
  4.3 2.8 %collective-permute-start.1 = (bf16[144,256]{1,0:T(8,128)(2,1)S(1)}, bf16[144,256]{1,0:T(8,128)(2,1)S(1)}, u32[]{:S(2)}, u32[]{:S(2)}) collective-permute-start(bf16[144,256]{1,0:T(8,128)(2,1)S(1)} %get-tuple-element.11), channel_id=1, source_target_pairs={{0,3},{1,0},{2,1},{3,2},{4,7},{5,4},{6,5},{7,6},{8,11},{9,8},{10,9... | collective-permute-start | bytes 221192 | tf_op jit(solution)/shard_map/ppermute | solution.py:367
  7.2 0.0 collective-permute-start
  7.2 2.3 %collective-permute-start.2 = (bf16[144,256]{1,0:T(8,128)(2,1)S(1)}, bf16[144,256]{1,0:T(8,128)(2,1)S(1)}, u32[]{:S(2)}, u32[]{:S(2)}) collective-permute-start(bf16[144,256]{1,0:T(8,128)(2,1)S(1)} %get-tuple-element.10.own.c0), channel_id=1, source_target_pairs={{0,2},{1,3},{2,0},{3,1},{4,6},{5,7},{6,4},{7,5},{8,10},{9,11},{10,... | collective-permute-start | bytes 221192 | tf_op jit(solution)/shard_map/ppermute | solution.py:367
  9.5 0.0 copy-done.1
  9.5 0.0 copy-done.2
  9.5 0.0 collective-permute-done.1.two.c2
  9.5 4.2 %collective-permute-done.one.c1 = bf16[144,256]{1,0:T(8,128)(2,1)S(1)} collective-permute-done((bf16[144,256]{1,0:T(8,128)(2,1)S(1)}, bf16[144,256]{1,0:T(8,128)(2,1)S(1)}, u32[]{:S(2)}, u32[]{:S(2)}) %collective-permute-start) | collective-permute-done | bytes 73760 | tf_op jit(solution)/shard_map/ppermute | solution.py:367
  13.7 0.0 collective-permute-done.2.three.c3
  13.8 7.3 %collective-permute-start.3 = (bf16[144,256]{1,0:T(8,128)(2,1)S(1)}, bf16[144,256]{1,0:T(8,128)(2,1)S(1)}, u32[]{:S(2)}, u32[]{:S(2)}) collective-permute-start(bf16[144,256]{1,0:T(8,128)(2,1)S(1)} %add.11.mine), channel_id=1, source_target_pairs={{0,4},{4,0},{1,5},{5,1},{2,6},{6,2},{3,7},{7,3},{8,12},{12,8},{9,1... | collective-permute-start | bytes 221192 | tf_op jit(solution)/shard_map/ppermute | solution.py:378
  21.1 2.4 %collective-permute-done.3.other = bf16[144,256]{1,0:T(8,128)(2,1)S(1)} collective-permute-done((bf16[144,256]{1,0:T(8,128)(2,1)S(1)}, bf16[144,256]{1,0:T(8,128)(2,1)S(1)}, u32[]{:S(2)}, u32[]{:S(2)}) %collective-permute-start.3) | collective-permute-done | bytes 73760 | tf_op jit(solution)/shard_map/ppermute | solution.py:378
  23.5 0.2 collective-permute-start.4
  23.7 1.4 %pupils.1 = (bf16[16,256,256]{2,1,0:T(8,128)(2,1)S(1)}, bf16[2,512,256]{2,1,0:T(8,128)(2,1)S(1)}, bf16[2,256,1024]{2,1,0:T(8,128)(2,1)S(1)}) custom-call(bf16[144,256]{1,0:T(8,128)(2,1)S(1)} %get-tuple-element.10.own.c0, bf16[144,256]{1,0:T(8,128)(2,1)S(1)} %collective-permute-done.one.c1, bf16[144,256]{1,0:T(8,128)(2,1)S(1)} %collective-permute-done.1.two.c2, ...), custom_call_target="tpu_custom_call" | custom-call | flops 10000000 | bytes 4000000 | tf_op jit(solution)/shard_map/pupils/pallas_call | solution.py:242
  25.1 2.8 %collective-permute-done.4.other = bf16[144,256]{1,0:T(8,128)(2,1)S(1)} collective-permute-done((bf16[144,256]{1,0:T(8,128)(2,1)S(1)}, bf16[144,256]{1,0:T(8,128)(2,1)S(1)}, u32[]{:S(2)}, u32[]{:S(2)}) %collective-permute-start.4) | collective-permute-done | bytes 73760 | tf_op jit(solution)/shard_map/ppermute | solution.py:379
  27.9 0.0 copy-done
  27.9 3.8 %inverse.1 = f32[128,1024]{1,0:T(8,128)} custom-call(bf16[144,256]{1,0:T(8,128)(2,1)S(1)} %finish.1.mine, bf16[144,256]{1,0:T(8,128)(2,1)S(1)} %collective-permute-done.4.other, bf16[144,256]{1,0:T(8,128)(2,1)S(1)} %get-tuple-element.10.own.c0, bf16[144,256]{1,0:T(8,128)(2,1)S(1)} %collective-permute-done.one.c1, ...), custom_call_target="tpu_custom_call" | custom-call | flops 2500000000 | bytes 3000000 | tf_op jit(solution)/shard_map/inverse/pallas_call | solution.py:340
  (7 shorter events, 0.1 us)
Async XLA Ops:
  0.0 9.5 %copy-start.1 = (bf16[2,128,256]{2,1,0:T(8,128)(2,1)S(1)}, bf16[2,128,256]{2,1,0:T(8,128)(2,1)}, u32[]{:S(2)}) copy-start(bf16[2,128,256]{2,1,0:T(8,128)(2,1)} %constant.47) | copy-start | bytes 393220
  0.0 9.5 %copy-start.2 = (bf16[2,128,256]{2,1,0:T(8,128)(2,1)S(1)}, bf16[2,128,256]{2,1,0:T(8,128)(2,1)}, u32[]{:S(2)}) copy-start(bf16[2,128,256]{2,1,0:T(8,128)(2,1)} %constant.45) | copy-start | bytes 393220
  0.0 27.9 %copy-start = (f32[8,1024]{1,0:T(8,128)S(1)}, f32[8,1024]{1,0:T(8,128)}, u32[]{:S(2)}) copy-start(f32[8,1024]{1,0:T(8,128)} %constant.43.clone.sine) | copy-start | bytes 98308
  4.3 5.2 %collective-permute-start.1 = (bf16[144,256]{1,0:T(8,128)(2,1)S(1)}, bf16[144,256]{1,0:T(8,128)(2,1)S(1)}, u32[]{:S(2)}, u32[]{:S(2)}) collective-permute-start(bf16[144,256]{1,0:T(8,128)(2,1)S(1)} %get-tuple-element.11), channel_id=1, source_target_pairs={{0,3},{1,0},{2,1},{3,2},{4,7},{5,4},{6,5},{7,6},{8,11},{9,8},{10,9... | collective-permute-start | bytes 221192 | tf_op jit(solution)/shard_map/ppermute | solution.py:367
  7.2 6.5 %collective-permute-start = (bf16[144,256]{1,0:T(8,128)(2,1)S(1)}, bf16[144,256]{1,0:T(8,128)(2,1)S(1)}, u32[]{:S(2)}, u32[]{:S(2)}) collective-permute-start(bf16[144,256]{1,0:T(8,128)(2,1)S(1)} %get-tuple-element.11), channel_id=1, source_target_pairs={{0,1},{1,2},{2,3},{3,0},{4,5},{5,6},{6,7},{7,4},{8,9},{9,10},{10,1... | collective-permute-start | bytes 221192 | tf_op jit(solution)/shard_map/ppermute | solution.py:367
  7.2 6.5 %collective-permute-start.2 = (bf16[144,256]{1,0:T(8,128)(2,1)S(1)}, bf16[144,256]{1,0:T(8,128)(2,1)S(1)}, u32[]{:S(2)}, u32[]{:S(2)}) collective-permute-start(bf16[144,256]{1,0:T(8,128)(2,1)S(1)} %get-tuple-element.10.own.c0), channel_id=1, source_target_pairs={{0,2},{1,3},{2,0},{3,1},{4,6},{5,7},{6,4},{7,5},{8,10},{9,11},{10,... | collective-permute-start | bytes 221192 | tf_op jit(solution)/shard_map/ppermute | solution.py:367
  13.8 9.7 %collective-permute-start.3 = (bf16[144,256]{1,0:T(8,128)(2,1)S(1)}, bf16[144,256]{1,0:T(8,128)(2,1)S(1)}, u32[]{:S(2)}, u32[]{:S(2)}) collective-permute-start(bf16[144,256]{1,0:T(8,128)(2,1)S(1)} %add.11.mine), channel_id=1, source_target_pairs={{0,4},{4,0},{1,5},{5,1},{2,6},{6,2},{3,7},{7,3},{8,12},{12,8},{9,1... | collective-permute-start | bytes 221192 | tf_op jit(solution)/shard_map/ppermute | solution.py:378
  23.5 4.4 %collective-permute-start.4 = (bf16[144,256]{1,0:T(8,128)(2,1)S(1)}, bf16[144,256]{1,0:T(8,128)(2,1)S(1)}, u32[]{:S(2)}, u32[]{:S(2)}) collective-permute-start(bf16[144,256]{1,0:T(8,128)(2,1)S(1)} %finish.1.mine), channel_id=1, source_target_pairs={{0,1},{1,0},{2,3},{3,2},{4,5},{5,4},{6,7},{7,6},{8,9},{9,8},{10,11... | collective-permute-start | bytes 221192 | tf_op jit(solution)/shard_map/ppermute | solution.py:379

commit v6 on v5

--- a/solution.py
+++ b/solution.py
@@ -12,7 +12,7 @@
 HALF = 128
 CHUNK = 512
 QUARTER = 64
-SENT = 144
+SENT = 136
 COARSE = 256
 NT = (((1,), (1,)), ((), ()))
 F32 = jnp.float32
@@ -65,7 +65,7 @@
     return cos_q, sin_q
 
 
-def forward_kernel(shifts_in, weights_in, mask, table_in, keep, give,
+def forward_kernel(shifts_in, weights_in, mask, table_in, far, after, before, keep,
                    shifts, weights, block, table, half_way, folded, whole, sem):
     small_copies = [
         pltpu.make_async_copy(table_in, table, sem.at[0]),
@@ -137,9 +137,9 @@
     ).astype(BF16)
     crossed = lax.dot_general(table[264:272, :HALF], edges, NT, preferred_element_type=F32)
     edges = jnp.concatenate([e_cos + crossed[:, :HALF], e_sin + crossed[:, HALF:]], 1)
-    row = lax.broadcasted_iota(jnp.int32, (16, HALF), 0)
-    first = jnp.zeros((16, HALF), F32)
-    second = jnp.zeros((16, HALF), F32)
+    row = lax.broadcasted_iota(jnp.int32, (8, HALF), 0)
+    first = jnp.zeros((8, HALF), F32)
+    second = jnp.zeros((8, HALF), F32)
     for i in range(4):
         first = jnp.where(row == 2 + i, shifts[0, i].astype(F32), first)
         second = jnp.where(row == 2 + i, shifts[1, i].astype(F32), second)
@@ -149,15 +149,17 @@
         else:
             second = jnp.where(row == 6 + i // 2, w, second)
     sources = jnp.concatenate([first, second], 1)
-    row = lax.broadcasted_iota(jnp.int32, (16, 256), 0)
-    for out, odd in ((keep, lax.rem(src_id, 2)), (give, lax.rem(src_id + 1, 2))):
+    row = lax.broadcasted_iota(jnp.int32, (8, 256), 0)
+    for outs, odd in (((far, keep), lax.rem(src_id, 2)), ((after, before), lax.rem(src_id + 1, 2))):
         at = pl.multiple_of(odd * QUARTER, QUARTER)
-        out[:QUARTER] = whole[pl.ds(at, QUARTER)].astype(BF16)
-        out[QUARTER:HALF] = whole[pl.ds(HALF + at, QUARTER)].astype(BF16)
         lines = [jnp.where(odd == 1, edges[2 + i:3 + i], edges[i:i + 1]) for i in range(2)]
-        out[HALF:SENT] = jnp.where(
-            row == 0, lines[0], jnp.where(row == 1, lines[1], sources)
-        ).astype(BF16)
+        rows = jnp.where(row == 0, lines[0], jnp.where(row == 1, lines[1], sources)).astype(BF16)
+        cos_rows = whole[pl.ds(at, QUARTER)].astype(BF16)
+        sin_rows = whole[pl.ds(HALF + at, QUARTER)].astype(BF16)
+        for out in outs:
+            out[:QUARTER] = cos_rows
+            out[QUARTER:HALF] = sin_rows
+            out[HALF:SENT] = rows
 
 
 def forward(mask_clip, shifts, weights, table):
@@ -165,8 +167,8 @@
     return pl.pallas_call(
         forward_kernel,
         in_specs=[hbm] * 4,
-        out_specs=[VMEM] * 2,
-        out_shape=[jax.ShapeDtypeStruct((SENT, 256), BF16)] * 2,
+        out_specs=[VMEM] * 4,
+        out_shape=[jax.ShapeDtypeStruct((SENT, 256), BF16)] * 4,
         scratch_shapes=[
             pltpu.SMEM((2, 4), jnp.int32),
             pltpu.SMEM((4,), jnp.int32),
@@ -256,7 +258,7 @@
 
 
 def inverse_kernel(mine, other, c0, c1, c2, c3, pupil, left, right, spread, sine, out,
-                   spec, edge, fields):
+                   spec, edge, fields, image, sem):
     src_id = lax.axis_index("src")
     for chunk, odd in ((mine, lax.rem(src_id, 2)), (other, lax.rem(src_id + 1, 2))):
         at = pl.multiple_of(odd * QUARTER, QUARTER)
@@ -328,24 +330,33 @@
     high = summed.astype(BF16)
     low = (summed - high.astype(F32)).astype(BF16)
     tail = ends[0] * sine[0:1]
-    out[...] = (
-        jnp.dot(high, spread[0], preferred_element_type=F32)
-        + jnp.dot(low, spread[0], preferred_element_type=F32)
-        + jnp.dot(high, spread[1], preferred_element_type=F32)
-        + tail
-    )
+    copies = []
+    for i in range(4):
+        span = slice(i * 256, (i + 1) * 256)
+        image[i] = (
+            jnp.dot(high, spread[0, :, span], preferred_element_type=F32)
+            + jnp.dot(low, spread[0, :, span], preferred_element_type=F32)
+            + jnp.dot(high, spread[1, :, span], preferred_element_type=F32)
+            + tail[:, span]
+        )
+        copies.append(pltpu.make_async_copy(image.at[i], out.at[:, span], sem.at[i]))
+        copies[i].start()
+    for copy in copies:
+        copy.wait()
 
 
 def inverse(*args):
     return pl.pallas_call(
         inverse_kernel,
         in_specs=[VMEM] * len(args),
-        out_specs=VMEM,
+        out_specs=pl.BlockSpec(memory_space=pltpu.HBM),
         out_shape=jax.ShapeDtypeStruct((HALF, NI), F32),
         scratch_shapes=[
             pltpu.VMEM((512, 256), BF16),
             pltpu.VMEM((8, 256), F32),
             pltpu.VMEM((2048, 512), BF16),
+            pltpu.VMEM((4, HALF, 256), F32),
+            pltpu.SemaphoreType.DMA((4,)),
         ],
         compiler_params=pltpu.CompilerParams(vmem_limit_bytes=24 * 1024 * 1024),
         cost_estimate=pl.CostEstimate(flops=2_500_000_000, bytes_accessed=3_000_000, transcendentals=0),
@@ -372,8 +383,8 @@
     left, right, spread, sine = inverse_tables()
     place = lax.axis_index("row") * 4 + lax.axis_index("src")
     left_mine = place_rows(jnp.asarray(left, BF16), place)
-    keep, give = forward(mask_clip, source_shifts.T, source_weights, jnp.asarray(table, BF16))
-    parts = [keep, ring(give, 1), ring(give, 3), ring(keep, 2)]
+    far, after, before, keep = forward(mask_clip, source_shifts.T, source_weights, jnp.asarray(table, BF16))
+    parts = [keep, ring(far, 2), ring(after, 1), ring(before, 3)]
     summed = small(add_kernel, "add", *parts)
     mine = small(finish_kernel, "finish", summed, lax.ppermute(summed, "row", [(0, 1), (1, 0)]))
     other = lax.ppermute(mine, "src", [(0, 1), (1, 0), (2, 3), (3, 2)])

time: 31.8 us -> 31.4 us (0.987); the launches traced: 31.7 us -> 30.9 us
  waiting for transfers between devices: 9.39 us -> 7.43 us
  starting transfers between devices: 12.6 us -> 13.7 us
    ppermute x3, waiting for transfers between devices: 4.16 us -> 2.21 us  [ring(): return lax.ppermute(x, 'src', [(i, (i + k) % 4) for i in range(4)])]
    ppermute x3, starting transfers between devices: 5.13 us -> 6.35 us  [ring(): return lax.ppermute(x, 'src', [(i, (i + k) % 4) for i in range(4)])]
  transfers between devices with their start and end apart: 5 -> 5, of which waited for: 3 -> 3; matrix products, arithmetic and copies ran while one was open for 0% -> 0% of each run, Pallas kernels for 4% -> 5%
where the time goes in v6:
time: 31.4 us; the launch traced here: 30.9 us
  starting transfers between devices  13.7 us (44%)
  Pallas kernels  9.54 us (30%)
  waiting for transfers between devices  7.43 us (24%)
    ppermute x1, starting transfers between devices, body(): lax.ppermute(summed, 'row', [(0, 1), (1, 0)])  7.28 us
    ppermute x3, starting transfers between devices, ring(): return lax.ppermute(x, 'src', [(i, (i + k) % 4) for i in range(4)])  6.35 us
    pallas_call x1, Pallas kernels, forward(): pl.pallas_call(forward_kernel, in_specs=[hbm] * 4, out_specs=[VMEM] * 4,...  4.33 us
    pallas_call x1, Pallas kernels, inverse(): pl.pallas_call(inverse_kernel, in_specs=[VMEM] * len(args), out_specs=pl....  3.74 us
    ppermute x1, waiting for transfers between devices, body(): other = lax.ppermute(mine, 'src', [(0, 1), (1, 0), (2, 3), (3, 2)])  2.85 us
    ppermute x1, waiting for transfers between devices, body(): lax.ppermute(summed, 'row', [(0, 1), (1, 0)])  2.36 us
    ppermute x3, waiting for transfers between devices, ring(): return lax.ppermute(x, 'src', [(i, (i + k) % 4) for i in range(4)])  2.21 us
    pallas_call x1, Pallas kernels, pupils(): pl.pallas_call(pupil_kernel, in_specs=[VMEM] * 4 + [pl.BlockSpec(memory_s...  1.41 us
  transfers between devices with their start and end apart: 5, of which 3 were waited for; matrix products, arithmetic and copies ran while one was open for 0% of the time, Pallas kernels for 5%

profile of v6, /device:TPU:8, one launch (start us, length us, event | category | flops | bytes accessed | tf_op | source)
XLA Modules:
  0.0 30.9 jit_solution(13594960043646274649)
XLA Ops:
  0.0 0.0 copy-start.1
  0.0 0.0 copy-start.2
  0.0 0.0 copy-start
  0.0 4.3 %forward.1 = (bf16[136,256]{1,0:T(8,128)(2,1)S(1)}, bf16[136,256]{1,0:T(8,128)(2,1)S(1)}, bf16[136,256]{1,0:T(8,128)(2,1)S(1)}, bf16[136,256]{1,0:T(8,128)(2,1)S(1)}) custom-call(s32[2,4]{1,0:T(2,128)} %bitcast.15, s32[4]{0:T(128)} %weights_in.1, bf16[2048,1024]{1,0:T(8,128)(2,1)} %mask.1, bf16[272,1024]{1,0:T(8,128)(2,1)} %constant.40.clone.table_in), custom_call_target="tpu_custom_call" | custom-call | flops 1700000000 | bytes 5000000 | tf_op jit(solution)/shard_map/forward/pallas_call | solution.py:167
  4.3 3.1 %collective-permute-start = (bf16[136,256]{1,0:T(8,128)(2,1)S(1)}, bf16[136,256]{1,0:T(8,128)(2,1)S(1)}, u32[]{:S(2)}, u32[]{:S(2)}) collective-permute-start(bf16[136,256]{1,0:T(8,128)(2,1)S(1)} %get-tuple-element.13), channel_id=1, source_target_pairs={{0,2},{1,3},{2,0},{3,1},{4,6},{5,7},{6,4},{7,5},{8,10},{9,11},{10,... | collective-permute-start | bytes 208904 | tf_op jit(solution)/shard_map/ppermute | solution.py:378
  7.5 0.6 %collective-permute-start.1 = (bf16[136,256]{1,0:T(8,128)(2,1)S(1)}, bf16[136,256]{1,0:T(8,128)(2,1)S(1)}, u32[]{:S(2)}, u32[]{:S(2)}) collective-permute-start(bf16[136,256]{1,0:T(8,128)(2,1)S(1)} %get-tuple-element.14), channel_id=1, source_target_pairs={{0,1},{1,2},{2,3},{3,0},{4,5},{5,6},{6,7},{7,4},{8,9},{9,10},{10,1... | collective-permute-start | bytes 208904 | tf_op jit(solution)/shard_map/ppermute | solution.py:378
  8.1 2.6 %collective-permute-start.2 = (bf16[136,256]{1,0:T(8,128)(2,1)S(1)}, bf16[136,256]{1,0:T(8,128)(2,1)S(1)}, u32[]{:S(2)}, u32[]{:S(2)}) collective-permute-start(bf16[136,256]{1,0:T(8,128)(2,1)S(1)} %get-tuple-element.15), channel_id=1, source_target_pairs={{0,3},{1,0},{2,1},{3,2},{4,7},{5,4},{6,5},{7,6},{8,11},{9,8},{10,9... | collective-permute-start | bytes 208904 | tf_op jit(solution)/shard_map/ppermute | solution.py:378
  10.7 0.0 copy-done.1
  10.7 0.0 copy-done.2
  10.8 0.0 collective-permute-done.one.c1
  10.8 2.2 %collective-permute-done.1.two.c2 = bf16[136,256]{1,0:T(8,128)(2,1)S(1)} collective-permute-done((bf16[136,256]{1,0:T(8,128)(2,1)S(1)}, bf16[136,256]{1,0:T(8,128)(2,1)S(1)}, u32[]{:S(2)}, u32[]{:S(2)}) %collective-permute-start.1) | collective-permute-done | bytes 69664 | tf_op jit(solution)/shard_map/ppermute | solution.py:378
  13.0 0.0 collective-permute-done.2.three.c3
  13.0 7.3 %collective-permute-start.3 = (bf16[136,256]{1,0:T(8,128)(2,1)S(1)}, bf16[136,256]{1,0:T(8,128)(2,1)S(1)}, u32[]{:S(2)}, u32[]{:S(2)}) collective-permute-start(bf16[136,256]{1,0:T(8,128)(2,1)S(1)} %add.11.mine), channel_id=1, source_target_pairs={{0,4},{4,0},{1,5},{5,1},{2,6},{6,2},{3,7},{7,3},{8,12},{12,8},{9,1... | collective-permute-start | bytes 208904 | tf_op jit(solution)/shard_map/ppermute | solution.py:389
  20.3 2.4 %collective-permute-done.3.other = bf16[136,256]{1,0:T(8,128)(2,1)S(1)} collective-permute-done((bf16[136,256]{1,0:T(8,128)(2,1)S(1)}, bf16[136,256]{1,0:T(8,128)(2,1)S(1)}, u32[]{:S(2)}, u32[]{:S(2)}) %collective-permute-start.3) | collective-permute-done | bytes 69664 | tf_op jit(solution)/shard_map/ppermute | solution.py:389
  22.7 0.1 collective-permute-start.4
  22.9 1.4 %pupils.1 = (bf16[16,256,256]{2,1,0:T(8,128)(2,1)S(1)}, bf16[2,512,256]{2,1,0:T(8,128)(2,1)S(1)}, bf16[2,256,1024]{2,1,0:T(8,128)(2,1)S(1)}) custom-call(bf16[136,256]{1,0:T(8,128)(2,1)S(1)} %get-tuple-element.12.own.c0, bf16[136,256]{1,0:T(8,128)(2,1)S(1)} %collective-permute-done.one.c1, bf16[136,256]{1,0:T(8,128)(2,1)S(1)} %collective-permute-done.1.two.c2, ...), custom_call_target="tpu_custom_call" | custom-call | flops 10000000 | bytes 4000000 | tf_op jit(solution)/shard_map/pupils/pallas_call | solution.py:244
  24.3 2.9 %collective-permute-done.4.other = bf16[136,256]{1,0:T(8,128)(2,1)S(1)} collective-permute-done((bf16[136,256]{1,0:T(8,128)(2,1)S(1)}, bf16[136,256]{1,0:T(8,128)(2,1)S(1)}, u32[]{:S(2)}, u32[]{:S(2)}) %collective-permute-start.4) | collective-permute-done | bytes 69664 | tf_op jit(solution)/shard_map/ppermute | solution.py:390
  27.1 0.0 copy-done
  27.1 3.7 %inverse.1 = f32[128,1024]{1,0:T(8,128)} custom-call(bf16[136,256]{1,0:T(8,128)(2,1)S(1)} %finish.1.mine, bf16[136,256]{1,0:T(8,128)(2,1)S(1)} %collective-permute-done.4.other, bf16[136,256]{1,0:T(8,128)(2,1)S(1)} %get-tuple-element.12.own.c0, bf16[136,256]{1,0:T(8,128)(2,1)S(1)} %collective-permute-done.one.c1, ...), custom_call_target="tpu_custom_call" | custom-call | flops 2500000000 | bytes 3000000 | tf_op jit(solution)/shard_map/inverse/pallas_call | solution.py:349
  (7 shorter events, 0.1 us)
Async XLA Ops:
  0.0 10.7 %copy-start.1 = (bf16[2,128,256]{2,1,0:T(8,128)(2,1)S(1)}, bf16[2,128,256]{2,1,0:T(8,128)(2,1)}, u32[]{:S(2)}) copy-start(bf16[2,128,256]{2,1,0:T(8,128)(2,1)} %constant.47) | copy-start | bytes 393220
  0.0 10.7 %copy-start.2 = (bf16[2,128,256]{2,1,0:T(8,128)(2,1)S(1)}, bf16[2,128,256]{2,1,0:T(8,128)(2,1)}, u32[]{:S(2)}) copy-start(bf16[2,128,256]{2,1,0:T(8,128)(2,1)} %constant.45) | copy-start | bytes 393220
  0.0 27.1 %copy-start = (f32[8,1024]{1,0:T(8,128)S(1)}, f32[8,1024]{1,0:T(8,128)}, u32[]{:S(2)}) copy-start(f32[8,1024]{1,0:T(8,128)} %constant.43.clone.sine) | copy-start | bytes 98308
  4.3 6.4 %collective-permute-start = (bf16[136,256]{1,0:T(8,128)(2,1)S(1)}, bf16[136,256]{1,0:T(8,128)(2,1)S(1)}, u32[]{:S(2)}, u32[]{:S(2)}) collective-permute-start(bf16[136,256]{1,0:T(8,128)(2,1)S(1)} %get-tuple-element.13), channel_id=1, source_target_pairs={{0,2},{1,3},{2,0},{3,1},{4,6},{5,7},{6,4},{7,5},{8,10},{9,11},{10,... | collective-permute-start | bytes 208904 | tf_op jit(solution)/shard_map/ppermute | solution.py:378
  7.5 5.5 %collective-permute-start.1 = (bf16[136,256]{1,0:T(8,128)(2,1)S(1)}, bf16[136,256]{1,0:T(8,128)(2,1)S(1)}, u32[]{:S(2)}, u32[]{:S(2)}) collective-permute-start(bf16[136,256]{1,0:T(8,128)(2,1)S(1)} %get-tuple-element.14), channel_id=1, source_target_pairs={{0,1},{1,2},{2,3},{3,0},{4,5},{5,6},{6,7},{7,4},{8,9},{9,10},{10,1... | collective-permute-start | bytes 208904 | tf_op jit(solution)/shard_map/ppermute | solution.py:378
  8.1 4.9 %collective-permute-start.2 = (bf16[136,256]{1,0:T(8,128)(2,1)S(1)}, bf16[136,256]{1,0:T(8,128)(2,1)S(1)}, u32[]{:S(2)}, u32[]{:S(2)}) collective-permute-start(bf16[136,256]{1,0:T(8,128)(2,1)S(1)} %get-tuple-element.15), channel_id=1, source_target_pairs={{0,3},{1,0},{2,1},{3,2},{4,7},{5,4},{6,5},{7,6},{8,11},{9,8},{10,9... | collective-permute-start | bytes 208904 | tf_op jit(solution)/shard_map/ppermute | solution.py:378
  13.0 9.7 %collective-permute-start.3 = (bf16[136,256]{1,0:T(8,128)(2,1)S(1)}, bf16[136,256]{1,0:T(8,128)(2,1)S(1)}, u32[]{:S(2)}, u32[]{:S(2)}) collective-permute-start(bf16[136,256]{1,0:T(8,128)(2,1)S(1)} %add.11.mine), channel_id=1, source_target_pairs={{0,4},{4,0},{1,5},{5,1},{2,6},{6,2},{3,7},{7,3},{8,12},{12,8},{9,1... | collective-permute-start | bytes 208904 | tf_op jit(solution)/shard_map/ppermute | solution.py:389
  22.7 4.4 %collective-permute-start.4 = (bf16[136,256]{1,0:T(8,128)(2,1)S(1)}, bf16[136,256]{1,0:T(8,128)(2,1)S(1)}, u32[]{:S(2)}, u32[]{:S(2)}) collective-permute-start(bf16[136,256]{1,0:T(8,128)(2,1)S(1)} %finish.1.mine), channel_id=1, source_target_pairs={{0,1},{1,0},{2,3},{3,2},{4,5},{5,4},{6,7},{7,6},{8,9},{9,8},{10,11... | collective-permute-start | bytes 208904 | tf_op jit(solution)/shard_map/ppermute | solution.py:390

commit v7 on v6

--- a/solution.py
+++ b/solution.py
@@ -65,12 +65,13 @@
     return cos_q, sin_q
 
 
-def forward_kernel(shifts_in, weights_in, mask, table_in, far, after, before, keep,
-                   shifts, weights, block, table, half_way, folded, whole, sem):
-    small_copies = [
-        pltpu.make_async_copy(table_in, table, sem.at[0]),
-        pltpu.make_async_copy(shifts_in, shifts, sem.at[1]),
-        pltpu.make_async_copy(weights_in, weights, sem.at[2]),
+def forward_kernel(shifts_in, weights_in, mask, upright_in, table_in, far, after, before, keep,
+                   shifts, weights, block, upright, table, half_way, folded, whole, sem):
+    upright_copy = pltpu.make_async_copy(upright_in, upright, sem.at[0])
+    late_copies = [
+        pltpu.make_async_copy(table_in, table, sem.at[1]),
+        pltpu.make_async_copy(shifts_in, shifts, sem.at[2]),
+        pltpu.make_async_copy(weights_in, weights, sem.at[7]),
     ]
     copies = [
         pltpu.make_async_copy(
@@ -78,7 +79,7 @@
         )
         for i in range(4)
     ]
-    for copy in (small_copies[0], *copies, *small_copies[1:]):
+    for copy in (upright_copy, *copies, *late_copies):
         copy.start()
     row_id = lax.axis_index("row")
     src_id = lax.axis_index("src")
@@ -96,14 +97,14 @@
         c, s = cos_g[:x.shape[0]], sin_g[:x.shape[0]]
         return c * x[:, :HALF] - s * x[:, HALF:], c * x[:, HALF:] + s * x[:, :HALF]
 
-    small_copies[0].wait()
+    upright_copy.wait()
 
     @pl.loop(0, 4)
     def _(i):
         rows = pl.ds(pl.multiple_of(i * CHUNK, CHUNK), CHUNK)
         pltpu.make_async_copy(mask.at[rows], block.at[rows], sem.at[3 + i]).wait()
-        half_way[rows] = lax.dot_general(
-            block[rows], table[:256, :], NT, preferred_element_type=F32
+        half_way[rows] = jnp.dot(
+            block[rows], upright[...], preferred_element_type=F32
         ).astype(BF16)
         lanes = pl.ds(pl.multiple_of((i // 2) * HALF, HALF), HALF)
         for low in range(0, CHUNK, 64):
@@ -113,13 +114,13 @@
                 tiles = [tiles[t] + tiles[t + 1] for t in range(0, len(tiles), 2)]
             folded[pl.ds(pl.multiple_of(lax.rem(i, 2) * CHUNK + low, 64), 64), lanes] = tiles[0]
 
+    for copy in late_copies:
+        copy.wait()
     sums = [
         jnp.dot(table[:264], half_way[h * TILE:(h + 1) * TILE], preferred_element_type=F32)
         for h in range(2)
     ]
     sides = jnp.dot(table[:256, :], folded[...], preferred_element_type=F32)
-    for copy in small_copies[1:]:
-        copy.wait()
     a, b = sums
     for start, x in zip((0, HALF), join_rows(a, b)):
         x_cos, x_sin = turn_columns(x)
@@ -162,27 +163,28 @@
             out[HALF:SENT] = rows
 
 
-def forward(mask_clip, shifts, weights, table):
+def forward(mask_clip, shifts, weights, upright, table):
     hbm = pl.BlockSpec(memory_space=pltpu.HBM)
     return pl.pallas_call(
         forward_kernel,
-        in_specs=[hbm] * 4,
+        in_specs=[hbm] * 5,
         out_specs=[VMEM] * 4,
         out_shape=[jax.ShapeDtypeStruct((SENT, 256), BF16)] * 4,
         scratch_shapes=[
             pltpu.SMEM((2, 4), jnp.int32),
             pltpu.SMEM((4,), jnp.int32),
             pltpu.VMEM((2 * TILE, TILE), BF16),
+            pltpu.VMEM((TILE, 256), BF16),
             pltpu.VMEM((272, TILE), BF16),
             pltpu.VMEM((2 * TILE, 256), BF16),
             pltpu.VMEM((TILE, 256), BF16),
             pltpu.VMEM((256, 256), F32),
-            pltpu.SemaphoreType.DMA((7,)),
+            pltpu.SemaphoreType.DMA((8,)),
         ],
         compiler_params=pltpu.CompilerParams(vmem_limit_bytes=16 * 1024 * 1024),
         cost_estimate=pl.CostEstimate(flops=1_700_000_000, bytes_accessed=5_000_000, transcendentals=0),
         name="forward",
-    )(*[pltpu.with_memory_space_constraint(x, pltpu.HBM) for x in (shifts, weights, mask_clip, table)])
+    )(*[pltpu.with_memory_space_constraint(x, pltpu.HBM) for x in (shifts, weights, mask_clip, upright, table)])
 
 
 def add_kernel(own, one, two, three, out):
@@ -383,7 +385,13 @@
     left, right, spread, sine = inverse_tables()
     place = lax.axis_index("row") * 4 + lax.axis_index("src")
     left_mine = place_rows(jnp.asarray(left, BF16), place)
-    far, after, before, keep = forward(mask_clip, source_shifts.T, source_weights, jnp.asarray(table, BF16))
+    far, after, before, keep = forward(
+        mask_clip,
+        source_shifts.T,
+        source_weights,
+        jnp.asarray(table[:256].T, BF16),
+        jnp.asarray(table, BF16),
+    )
     parts = [keep, ring(far, 2), ring(after, 1), ring(before, 3)]
     summed = small(add_kernel, "add", *parts)
     mine = small(finish_kernel, "finish", summed, lax.ppermute(summed, "row", [(0, 1), (1, 0)]))

time: 31.4 us -> 31.5 us (level)
  no operation moved by 1% of the time
where the time goes in v7:
time: 31.5 us; the launch traced here: 30.9 us
  starting transfers between devices  13.7 us (43%)
  Pallas kernels  9.63 us (31%)
  waiting for transfers between devices  7.43 us (24%)
    ppermute x1, starting transfers between devices, body(): lax.ppermute(summed, 'row', [(0, 1), (1, 0)])  7.27 us
    ppermute x3, starting transfers between devices, ring(): return lax.ppermute(x, 'src', [(i, (i + k) % 4) for i in range(4)])  6.35 us
    pallas_call x1, Pallas kernels, forward(): pl.pallas_call(forward_kernel, in_specs=[hbm] * 5, out_specs=[VMEM] * 4,...  4.41 us
    pallas_call x1, Pallas kernels, inverse(): pl.pallas_call(inverse_kernel, in_specs=[VMEM] * len(args), out_specs=pl....  3.74 us
    ppermute x1, waiting for transfers between devices, body(): other = lax.ppermute(mine, 'src', [(0, 1), (1, 0), (2, 3), (3, 2)])  2.85 us
    ppermute x1, waiting for transfers between devices, body(): lax.ppermute(summed, 'row', [(0, 1), (1, 0)])  2.37 us
    ppermute x3, waiting for transfers between devices, ring(): return lax.ppermute(x, 'src', [(i, (i + k) % 4) for i in range(4)])  2.21 us
    pallas_call x1, Pallas kernels, pupils(): pl.pallas_call(pupil_kernel, in_specs=[VMEM] * 4 + [pl.BlockSpec(memory_s...  1.41 us
  transfers between devices with their start and end apart: 5, of which 3 were waited for; matrix products, arithmetic and copies ran while one was open for 0% of the time, Pallas kernels for 5%

profile of v7, /device:TPU:8, one launch (start us, length us, event | category | flops | bytes accessed | tf_op | source)
XLA Modules:
  0.0 30.9 jit_solution(11564638439565515113)
XLA Ops:
  0.0 0.0 copy-start.1
  0.0 0.0 copy-start.2
  0.0 0.0 copy-start
  0.0 4.4 %forward.1 = (bf16[136,256]{1,0:T(8,128)(2,1)S(1)}, bf16[136,256]{1,0:T(8,128)(2,1)S(1)}, bf16[136,256]{1,0:T(8,128)(2,1)S(1)}, bf16[136,256]{1,0:T(8,128)(2,1)S(1)}) custom-call(s32[2,4]{1,0:T(2,128)} %bitcast.15, s32[4]{0:T(128)} %weights_in.1, bf16[2048,1024]{1,0:T(8,128)(2,1)} %mask.1, bf16[1024,256]{1,0:T(8,128)(2,1)} %constant.42.clone.upright_in, ...), custom_call_target="tpu_custom_call" | custom-call | flops 1700000000 | bytes 5000000 | tf_op jit(solution)/shard_map/forward/pallas_call | solution.py:168
  4.4 3.1 %collective-permute-start = (bf16[136,256]{1,0:T(8,128)(2,1)S(1)}, bf16[136,256]{1,0:T(8,128)(2,1)S(1)}, u32[]{:S(2)}, u32[]{:S(2)}) collective-permute-start(bf16[136,256]{1,0:T(8,128)(2,1)S(1)} %get-tuple-element.13), channel_id=1, source_target_pairs={{0,2},{1,3},{2,0},{3,1},{4,6},{5,7},{6,4},{7,5},{8,10},{9,11},{10,... | collective-permute-start | bytes 208904 | tf_op jit(solution)/shard_map/ppermute | solution.py:380
  7.5 0.6 %collective-permute-start.1 = (bf16[136,256]{1,0:T(8,128)(2,1)S(1)}, bf16[136,256]{1,0:T(8,128)(2,1)S(1)}, u32[]{:S(2)}, u32[]{:S(2)}) collective-permute-start(bf16[136,256]{1,0:T(8,128)(2,1)S(1)} %get-tuple-element.14), channel_id=1, source_target_pairs={{0,1},{1,2},{2,3},{3,0},{4,5},{5,6},{6,7},{7,4},{8,9},{9,10},{10,1... | collective-permute-start | bytes 208904 | tf_op jit(solution)/shard_map/ppermute | solution.py:380
  8.1 2.6 %collective-permute-start.2 = (bf16[136,256]{1,0:T(8,128)(2,1)S(1)}, bf16[136,256]{1,0:T(8,128)(2,1)S(1)}, u32[]{:S(2)}, u32[]{:S(2)}) collective-permute-start(bf16[136,256]{1,0:T(8,128)(2,1)S(1)} %get-tuple-element.15), channel_id=1, source_target_pairs={{0,3},{1,0},{2,1},{3,2},{4,7},{5,4},{6,5},{7,6},{8,11},{9,8},{10,9... | collective-permute-start | bytes 208904 | tf_op jit(solution)/shard_map/ppermute | solution.py:380
  10.8 0.0 copy-done.1
  10.8 0.0 copy-done.2
  10.8 0.0 collective-permute-done.one.c1
  10.9 2.2 %collective-permute-done.1.two.c2 = bf16[136,256]{1,0:T(8,128)(2,1)S(1)} collective-permute-done((bf16[136,256]{1,0:T(8,128)(2,1)S(1)}, bf16[136,256]{1,0:T(8,128)(2,1)S(1)}, u32[]{:S(2)}, u32[]{:S(2)}) %collective-permute-start.1) | collective-permute-done | bytes 69664 | tf_op jit(solution)/shard_map/ppermute | solution.py:380
  13.1 0.0 collective-permute-done.2.three.c3
  13.1 7.3 %collective-permute-start.3 = (bf16[136,256]{1,0:T(8,128)(2,1)S(1)}, bf16[136,256]{1,0:T(8,128)(2,1)S(1)}, u32[]{:S(2)}, u32[]{:S(2)}) collective-permute-start(bf16[136,256]{1,0:T(8,128)(2,1)S(1)} %add.11.mine), channel_id=1, source_target_pairs={{0,4},{4,0},{1,5},{5,1},{2,6},{6,2},{3,7},{7,3},{8,12},{12,8},{9,1... | collective-permute-start | bytes 208904 | tf_op jit(solution)/shard_map/ppermute | solution.py:397
  20.4 2.4 %collective-permute-done.3.other = bf16[136,256]{1,0:T(8,128)(2,1)S(1)} collective-permute-done((bf16[136,256]{1,0:T(8,128)(2,1)S(1)}, bf16[136,256]{1,0:T(8,128)(2,1)S(1)}, u32[]{:S(2)}, u32[]{:S(2)}) %collective-permute-start.3) | collective-permute-done | bytes 69664 | tf_op jit(solution)/shard_map/ppermute | solution.py:397
  22.8 0.1 collective-permute-start.4
  22.9 1.4 %pupils.1 = (bf16[16,256,256]{2,1,0:T(8,128)(2,1)S(1)}, bf16[2,512,256]{2,1,0:T(8,128)(2,1)S(1)}, bf16[2,256,1024]{2,1,0:T(8,128)(2,1)S(1)}) custom-call(bf16[136,256]{1,0:T(8,128)(2,1)S(1)} %get-tuple-element.12.own.c0, bf16[136,256]{1,0:T(8,128)(2,1)S(1)} %collective-permute-done.one.c1, bf16[136,256]{1,0:T(8,128)(2,1)S(1)} %collective-permute-done.1.two.c2, ...), custom_call_target="tpu_custom_call" | custom-call | flops 10000000 | bytes 4000000 | tf_op jit(solution)/shard_map/pupils/pallas_call | solution.py:246
  24.4 2.9 %collective-permute-done.4.other = bf16[136,256]{1,0:T(8,128)(2,1)S(1)} collective-permute-done((bf16[136,256]{1,0:T(8,128)(2,1)S(1)}, bf16[136,256]{1,0:T(8,128)(2,1)S(1)}, u32[]{:S(2)}, u32[]{:S(2)}) %collective-permute-start.4) | collective-permute-done | bytes 69664 | tf_op jit(solution)/shard_map/ppermute | solution.py:398
  27.2 0.0 copy-done
  27.2 3.7 %inverse.1 = f32[128,1024]{1,0:T(8,128)} custom-call(bf16[136,256]{1,0:T(8,128)(2,1)S(1)} %finish.1.mine, bf16[136,256]{1,0:T(8,128)(2,1)S(1)} %collective-permute-done.4.other, bf16[136,256]{1,0:T(8,128)(2,1)S(1)} %get-tuple-element.12.own.c0, bf16[136,256]{1,0:T(8,128)(2,1)S(1)} %collective-permute-done.one.c1, ...), custom_call_target="tpu_custom_call" | custom-call | flops 2500000000 | bytes 3000000 | tf_op jit(solution)/shard_map/inverse/pallas_call | solution.py:351
  (7 shorter events, 0.1 us)
Async XLA Ops:
  0.0 10.8 %copy-start.1 = (bf16[2,128,256]{2,1,0:T(8,128)(2,1)S(1)}, bf16[2,128,256]{2,1,0:T(8,128)(2,1)}, u32[]{:S(2)}) copy-start(bf16[2,128,256]{2,1,0:T(8,128)(2,1)} %constant.50) | copy-start | bytes 393220
  0.0 10.8 %copy-start.2 = (bf16[2,128,256]{2,1,0:T(8,128)(2,1)S(1)}, bf16[2,128,256]{2,1,0:T(8,128)(2,1)}, u32[]{:S(2)}) copy-start(bf16[2,128,256]{2,1,0:T(8,128)(2,1)} %constant.48) | copy-start | bytes 393220
  0.0 27.2 %copy-start = (f32[8,1024]{1,0:T(8,128)S(1)}, f32[8,1024]{1,0:T(8,128)}, u32[]{:S(2)}) copy-start(f32[8,1024]{1,0:T(8,128)} %constant.46.clone.sine) | copy-start | bytes 98308
  4.4 6.4 %collective-permute-start = (bf16[136,256]{1,0:T(8,128)(2,1)S(1)}, bf16[136,256]{1,0:T(8,128)(2,1)S(1)}, u32[]{:S(2)}, u32[]{:S(2)}) collective-permute-start(bf16[136,256]{1,0:T(8,128)(2,1)S(1)} %get-tuple-element.13), channel_id=1, source_target_pairs={{0,2},{1,3},{2,0},{3,1},{4,6},{5,7},{6,4},{7,5},{8,10},{9,11},{10,... | collective-permute-start | bytes 208904 | tf_op jit(solution)/shard_map/ppermute | solution.py:380
  7.5 5.5 %collective-permute-start.1 = (bf16[136,256]{1,0:T(8,128)(2,1)S(1)}, bf16[136,256]{1,0:T(8,128)(2,1)S(1)}, u32[]{:S(2)}, u32[]{:S(2)}) collective-permute-start(bf16[136,256]{1,0:T(8,128)(2,1)S(1)} %get-tuple-element.14), channel_id=1, source_target_pairs={{0,1},{1,2},{2,3},{3,0},{4,5},{5,6},{6,7},{7,4},{8,9},{9,10},{10,1... | collective-permute-start | bytes 208904 | tf_op jit(solution)/shard_map/ppermute | solution.py:380
  8.1 4.9 %collective-permute-start.2 = (bf16[136,256]{1,0:T(8,128)(2,1)S(1)}, bf16[136,256]{1,0:T(8,128)(2,1)S(1)}, u32[]{:S(2)}, u32[]{:S(2)}) collective-permute-start(bf16[136,256]{1,0:T(8,128)(2,1)S(1)} %get-tuple-element.15), channel_id=1, source_target_pairs={{0,3},{1,0},{2,1},{3,2},{4,7},{5,4},{6,5},{7,6},{8,11},{9,8},{10,9... | collective-permute-start | bytes 208904 | tf_op jit(solution)/shard_map/ppermute | solution.py:380
  13.1 9.7 %collective-permute-start.3 = (bf16[136,256]{1,0:T(8,128)(2,1)S(1)}, bf16[136,256]{1,0:T(8,128)(2,1)S(1)}, u32[]{:S(2)}, u32[]{:S(2)}) collective-permute-start(bf16[136,256]{1,0:T(8,128)(2,1)S(1)} %add.11.mine), channel_id=1, source_target_pairs={{0,4},{4,0},{1,5},{5,1},{2,6},{6,2},{3,7},{7,3},{8,12},{12,8},{9,1... | collective-permute-start | bytes 208904 | tf_op jit(solution)/shard_map/ppermute | solution.py:397
  22.8 4.4 %collective-permute-start.4 = (bf16[136,256]{1,0:T(8,128)(2,1)S(1)}, bf16[136,256]{1,0:T(8,128)(2,1)S(1)}, u32[]{:S(2)}, u32[]{:S(2)}) collective-permute-start(bf16[136,256]{1,0:T(8,128)(2,1)S(1)} %finish.1.mine), channel_id=1, source_target_pairs={{0,1},{1,0},{2,3},{3,2},{4,5},{5,4},{6,7},{7,6},{8,9},{9,8},{10,11... | collective-permute-start | bytes 208904 | tf_op jit(solution)/shard_map/ppermute | solution.py:398

commit v8 on v7

--- a/solution.py
+++ b/solution.py
@@ -392,7 +392,7 @@
         jnp.asarray(table[:256].T, BF16),
         jnp.asarray(table, BF16),
     )
-    parts = [keep, ring(far, 2), ring(after, 1), ring(before, 3)]
+    parts = [keep, ring(far, 2), ring(before, 3), ring(after, 1)]
     summed = small(add_kernel, "add", *parts)
     mine = small(finish_kernel, "finish", summed, lax.ppermute(summed, "row", [(0, 1), (1, 0)]))
     other = lax.ppermute(mine, "src", [(0, 1), (1, 0), (2, 3), (3, 2)])

time: 31.5 us -> 32.2 us (1.022); the launches traced: 30.9 us -> 32.1 us
  waiting for transfers between devices: 7.43 us -> 9.79 us
  starting transfers between devices: 13.7 us -> 12.5 us
    ppermute x3, waiting for transfers between devices: 2.21 us -> 4.57 us  [ring(): return lax.ppermute(x, 'src', [(i, (i + k) % 4) for i in range(4)])]
    ppermute x3, starting transfers between devices: 6.35 us -> 5.14 us  [ring(): return lax.ppermute(x, 'src', [(i, (i + k) % 4) for i in range(4)])]
  transfers between devices with their start and end apart: 5 -> 5, of which waited for: 3 -> 5; matrix products, arithmetic and copies ran while one was open for 0% -> 0% of each run, Pallas kernels for 5% -> 4%
where the time goes in v8:
time: 32.2 us; the launch traced here: 32.1 us
  starting transfers between devices  12.5 us (39%)
  waiting for transfers between devices  9.79 us (30%)
  Pallas kernels  9.63 us (30%)
    ppermute x1, starting transfers between devices, body(): lax.ppermute(summed, 'row', [(0, 1), (1, 0)])  7.27 us
    ppermute x3, starting transfers between devices, ring(): return lax.ppermute(x, 'src', [(i, (i + k) % 4) for i in range(4)])  5.14 us
    ppermute x3, waiting for transfers between devices, ring(): return lax.ppermute(x, 'src', [(i, (i + k) % 4) for i in range(4)])  4.57 us
    pallas_call x1, Pallas kernels, forward(): pl.pallas_call(forward_kernel, in_specs=[hbm] * 5, out_specs=[VMEM] * 4,...  4.41 us
    pallas_call x1, Pallas kernels, inverse(): pl.pallas_call(inverse_kernel, in_specs=[VMEM] * len(args), out_specs=pl....  3.74 us
    ppermute x1, waiting for transfers between devices, body(): other = lax.ppermute(mine, 'src', [(0, 1), (1, 0), (2, 3), (3, 2)])  2.85 us
    ppermute x1, waiting for transfers between devices, body(): lax.ppermute(summed, 'row', [(0, 1), (1, 0)])  2.36 us
    pallas_call x1, Pallas kernels, pupils(): pl.pallas_call(pupil_kernel, in_specs=[VMEM] * 4 + [pl.BlockSpec(memory_s...  1.41 us
  transfers between devices with their start and end apart: 5, of which 5 were waited for; matrix products, arithmetic and copies ran while one was open for 0% of the time, Pallas kernels for 4%

profile of v8, /device:TPU:8, one launch (start us, length us, event | category | flops | bytes accessed | tf_op | source)
XLA Modules:
  0.0 32.1 jit_solution(11548442497327010635)
XLA Ops:
  0.0 0.0 copy-start.1
  0.0 0.0 copy-start.2
  0.0 0.0 copy-start
  0.0 4.4 %forward.1 = (bf16[136,256]{1,0:T(8,128)(2,1)S(1)}, bf16[136,256]{1,0:T(8,128)(2,1)S(1)}, bf16[136,256]{1,0:T(8,128)(2,1)S(1)}, bf16[136,256]{1,0:T(8,128)(2,1)S(1)}) custom-call(s32[2,4]{1,0:T(2,128)} %bitcast.15, s32[4]{0:T(128)} %weights_in.1, bf16[2048,1024]{1,0:T(8,128)(2,1)} %mask.1, bf16[1024,256]{1,0:T(8,128)(2,1)} %constant.42.clone.upright_in, ...), custom_call_target="tpu_custom_call" | custom-call | flops 1700000000 | bytes 5000000 | tf_op jit(solution)/shard_map/forward/pallas_call | solution.py:168
  4.4 3.1 %collective-permute-start = (bf16[136,256]{1,0:T(8,128)(2,1)S(1)}, bf16[136,256]{1,0:T(8,128)(2,1)S(1)}, u32[]{:S(2)}, u32[]{:S(2)}) collective-permute-start(bf16[136,256]{1,0:T(8,128)(2,1)S(1)} %get-tuple-element.13), channel_id=1, source_target_pairs={{0,2},{1,3},{2,0},{3,1},{4,6},{5,7},{6,4},{7,5},{8,10},{9,11},{10,... | collective-permute-start | bytes 208904 | tf_op jit(solution)/shard_map/ppermute | solution.py:380
  7.5 1.1 %collective-permute-start.1 = (bf16[136,256]{1,0:T(8,128)(2,1)S(1)}, bf16[136,256]{1,0:T(8,128)(2,1)S(1)}, u32[]{:S(2)}, u32[]{:S(2)}) collective-permute-start(bf16[136,256]{1,0:T(8,128)(2,1)S(1)} %get-tuple-element.14), channel_id=1, source_target_pairs={{0,3},{1,0},{2,1},{3,2},{4,7},{5,4},{6,5},{7,6},{8,11},{9,8},{10,9... | collective-permute-start | bytes 208904 | tf_op jit(solution)/shard_map/ppermute | solution.py:380
  8.7 0.9 %collective-permute-start.2 = (bf16[136,256]{1,0:T(8,128)(2,1)S(1)}, bf16[136,256]{1,0:T(8,128)(2,1)S(1)}, u32[]{:S(2)}, u32[]{:S(2)}) collective-permute-start(bf16[136,256]{1,0:T(8,128)(2,1)S(1)} %get-tuple-element.15), channel_id=1, source_target_pairs={{0,1},{1,2},{2,3},{3,0},{4,5},{5,6},{6,7},{7,4},{8,9},{9,10},{10,1... | collective-permute-start | bytes 208904 | tf_op jit(solution)/shard_map/ppermute | solution.py:380
  9.6 0.0 copy-done.1
  9.6 0.0 copy-done.2
  9.6 0.7 %collective-permute-done.one.c1 = bf16[136,256]{1,0:T(8,128)(2,1)S(1)} collective-permute-done((bf16[136,256]{1,0:T(8,128)(2,1)S(1)}, bf16[136,256]{1,0:T(8,128)(2,1)S(1)}, u32[]{:S(2)}, u32[]{:S(2)}) %collective-permute-start) | collective-permute-done | bytes 69664 | tf_op jit(solution)/shard_map/ppermute | solution.py:380
  10.3 1.6 %collective-permute-done.1.two.c2 = bf16[136,256]{1,0:T(8,128)(2,1)S(1)} collective-permute-done((bf16[136,256]{1,0:T(8,128)(2,1)S(1)}, bf16[136,256]{1,0:T(8,128)(2,1)S(1)}, u32[]{:S(2)}, u32[]{:S(2)}) %collective-permute-start.1) | collective-permute-done | bytes 69664 | tf_op jit(solution)/shard_map/ppermute | solution.py:380
  11.9 2.3 %collective-permute-done.2.three.c3 = bf16[136,256]{1,0:T(8,128)(2,1)S(1)} collective-permute-done((bf16[136,256]{1,0:T(8,128)(2,1)S(1)}, bf16[136,256]{1,0:T(8,128)(2,1)S(1)}, u32[]{:S(2)}, u32[]{:S(2)}) %collective-permute-start.2) | collective-permute-done | bytes 69664 | tf_op jit(solution)/shard_map/ppermute | solution.py:380
  14.2 7.3 %collective-permute-start.3 = (bf16[136,256]{1,0:T(8,128)(2,1)S(1)}, bf16[136,256]{1,0:T(8,128)(2,1)S(1)}, u32[]{:S(2)}, u32[]{:S(2)}) collective-permute-start(bf16[136,256]{1,0:T(8,128)(2,1)S(1)} %add.11.mine), channel_id=1, source_target_pairs={{0,4},{4,0},{1,5},{5,1},{2,6},{6,2},{3,7},{7,3},{8,12},{12,8},{9,1... | collective-permute-start | bytes 208904 | tf_op jit(solution)/shard_map/ppermute | solution.py:397
  21.5 2.4 %collective-permute-done.3.other = bf16[136,256]{1,0:T(8,128)(2,1)S(1)} collective-permute-done((bf16[136,256]{1,0:T(8,128)(2,1)S(1)}, bf16[136,256]{1,0:T(8,128)(2,1)S(1)}, u32[]{:S(2)}, u32[]{:S(2)}) %collective-permute-start.3) | collective-permute-done | bytes 69664 | tf_op jit(solution)/shard_map/ppermute | solution.py:397
  23.9 0.1 collective-permute-start.4
  24.1 1.4 %pupils.1 = (bf16[16,256,256]{2,1,0:T(8,128)(2,1)S(1)}, bf16[2,512,256]{2,1,0:T(8,128)(2,1)S(1)}, bf16[2,256,1024]{2,1,0:T(8,128)(2,1)S(1)}) custom-call(bf16[136,256]{1,0:T(8,128)(2,1)S(1)} %get-tuple-element.12.own.c0, bf16[136,256]{1,0:T(8,128)(2,1)S(1)} %collective-permute-done.one.c1, bf16[136,256]{1,0:T(8,128)(2,1)S(1)} %collective-permute-done.1.two.c2, ...), custom_call_target="tpu_custom_call" | custom-call | flops 10000000 | bytes 4000000 | tf_op jit(solution)/shard_map/pupils/pallas_call | solution.py:246
  25.5 2.9 %collective-permute-done.4.other = bf16[136,256]{1,0:T(8,128)(2,1)S(1)} collective-permute-done((bf16[136,256]{1,0:T(8,128)(2,1)S(1)}, bf16[136,256]{1,0:T(8,128)(2,1)S(1)}, u32[]{:S(2)}, u32[]{:S(2)}) %collective-permute-start.4) | collective-permute-done | bytes 69664 | tf_op jit(solution)/shard_map/ppermute | solution.py:398
  28.3 0.0 copy-done
  28.3 3.7 %inverse.1 = f32[128,1024]{1,0:T(8,128)} custom-call(bf16[136,256]{1,0:T(8,128)(2,1)S(1)} %finish.1.mine, bf16[136,256]{1,0:T(8,128)(2,1)S(1)} %collective-permute-done.4.other, bf16[136,256]{1,0:T(8,128)(2,1)S(1)} %get-tuple-element.12.own.c0, bf16[136,256]{1,0:T(8,128)(2,1)S(1)} %collective-permute-done.one.c1, ...), custom_call_target="tpu_custom_call" | custom-call | flops 2500000000 | bytes 3000000 | tf_op jit(solution)/shard_map/inverse/pallas_call | solution.py:351
  (7 shorter events, 0.1 us)
Async XLA Ops:
  0.0 9.6 %copy-start.1 = (bf16[2,128,256]{2,1,0:T(8,128)(2,1)S(1)}, bf16[2,128,256]{2,1,0:T(8,128)(2,1)}, u32[]{:S(2)}) copy-start(bf16[2,128,256]{2,1,0:T(8,128)(2,1)} %constant.50) | copy-start | bytes 393220
  0.0 9.6 %copy-start.2 = (bf16[2,128,256]{2,1,0:T(8,128)(2,1)S(1)}, bf16[2,128,256]{2,1,0:T(8,128)(2,1)}, u32[]{:S(2)}) copy-start(bf16[2,128,256]{2,1,0:T(8,128)(2,1)} %constant.48) | copy-start | bytes 393220
  0.0 28.3 %copy-start = (f32[8,1024]{1,0:T(8,128)S(1)}, f32[8,1024]{1,0:T(8,128)}, u32[]{:S(2)}) copy-start(f32[8,1024]{1,0:T(8,128)} %constant.46.clone.sine) | copy-start | bytes 98308
  4.4 5.9 %collective-permute-start = (bf16[136,256]{1,0:T(8,128)(2,1)S(1)}, bf16[136,256]{1,0:T(8,128)(2,1)S(1)}, u32[]{:S(2)}, u32[]{:S(2)}) collective-permute-start(bf16[136,256]{1,0:T(8,128)(2,1)S(1)} %get-tuple-element.13), channel_id=1, source_target_pairs={{0,2},{1,3},{2,0},{3,1},{4,6},{5,7},{6,4},{7,5},{8,10},{9,11},{10,... | collective-permute-start | bytes 208904 | tf_op jit(solution)/shard_map/ppermute | solution.py:380
  7.5 4.4 %collective-permute-start.1 = (bf16[136,256]{1,0:T(8,128)(2,1)S(1)}, bf16[136,256]{1,0:T(8,128)(2,1)S(1)}, u32[]{:S(2)}, u32[]{:S(2)}) collective-permute-start(bf16[136,256]{1,0:T(8,128)(2,1)S(1)} %get-tuple-element.14), channel_id=1, source_target_pairs={{0,3},{1,0},{2,1},{3,2},{4,7},{5,4},{6,5},{7,6},{8,11},{9,8},{10,9... | collective-permute-start | bytes 208904 | tf_op jit(solution)/shard_map/ppermute | solution.py:380
  8.7 5.5 %collective-permute-start.2 = (bf16[136,256]{1,0:T(8,128)(2,1)S(1)}, bf16[136,256]{1,0:T(8,128)(2,1)S(1)}, u32[]{:S(2)}, u32[]{:S(2)}) collective-permute-start(bf16[136,256]{1,0:T(8,128)(2,1)S(1)} %get-tuple-element.15), channel_id=1, source_target_pairs={{0,1},{1,2},{2,3},{3,0},{4,5},{5,6},{6,7},{7,4},{8,9},{9,10},{10,1... | collective-permute-start | bytes 208904 | tf_op jit(solution)/shard_map/ppermute | solution.py:380
  14.2 9.7 %collective-permute-start.3 = (bf16[136,256]{1,0:T(8,128)(2,1)S(1)}, bf16[136,256]{1,0:T(8,128)(2,1)S(1)}, u32[]{:S(2)}, u32[]{:S(2)}) collective-permute-start(bf16[136,256]{1,0:T(8,128)(2,1)S(1)} %add.11.mine), channel_id=1, source_target_pairs={{0,4},{4,0},{1,5},{5,1},{2,6},{6,2},{3,7},{7,3},{8,12},{12,8},{9,1... | collective-permute-start | bytes 208904 | tf_op jit(solution)/shard_map/ppermute | solution.py:397
  23.9 4.4 %collective-permute-start.4 = (bf16[136,256]{1,0:T(8,128)(2,1)S(1)}, bf16[136,256]{1,0:T(8,128)(2,1)S(1)}, u32[]{:S(2)}, u32[]{:S(2)}) collective-permute-start(bf16[136,256]{1,0:T(8,128)(2,1)S(1)} %finish.1.mine), channel_id=1, source_target_pairs={{0,1},{1,0},{2,3},{3,2},{4,5},{5,4},{6,7},{7,6},{8,9},{9,8},{10,11... | collective-permute-start | bytes 208904 | tf_op jit(solution)/shard_map/ppermute | solution.py:398
